TPU v7x, 32 devices: a whole 2x2x4 slice. The times are simulated.
32 devices in a mesh: dp: 4 (over y, x), expert: 8 (over z, core).
Axes of the slice: x: 2, y: 2, z: 4, core: 2. Of those that a mesh axis runs over, the one named last changes fastest.
Arguments:
- out_grad: bfloat16 [384, 3072], P(('dp', 'expert')), may hold values from -6 to 6
- layer_input: bfloat16 [384, 3072], P(('dp', 'expert')), may hold values from -6 to 6
- expert_ids: int32 [384, 2], P(('dp', 'expert')), may hold values from 0 to 7, as said below
- gate_prob: float32 [384, 2], P(('dp', 'expert')), may hold values from 0.05 to 1
- w_stack: bfloat16 [3, 3072, 8192], P(None, 'dp', 'expert'), may hold values from -0.109375 to 0.109375
- scale_exps: int32 [3, 24, 64], P(None, 'dp', 'expert'), may hold values from -1 to 1
Outputs:
- input_grad: bfloat16 [384, 3072], P(('dp', 'expert'))
- weight_grads: float32 [3, 3072, 8192], P(None, 'dp', 'expert')
Inputs may be any that keep to these rules, and one draw needn't show every extreme that they name: `expert_ids`: each row names two different experts. In each aligned block of 12 rows (the tokens of one device) between 1 and 3 rows name expert 0, and some blocks have exactly 3 in every draw.
All inputs are finite; a program needn't handle non-finite values.
Results may differ from a plain program's by a relative error of at most 0.015.
Values may be sent and summed in bfloat16 or wider, within the bound.
No kernel may reach another device: no remote copies, remote signals or barrier semaphores. Data moves between devices by JAX's collectives and lax.ppermute only.
A program may use at most 128 MiB of HBM per device.

v0:
```python
import jax
import jax.numpy as jnp
from jax import lax
from jax.sharding import PartitionSpec as P

TILE = 128
CAP = 3


def back_project(grad_rows, matrix):
    return lax.dot_general(
        grad_rows, matrix, (((1,), (1,)), ((), ())), preferred_element_type=jnp.float32
    )


def per_device(out_grad, layer_input, expert_ids, gate_prob, w_stack, scale_exps):
    tok_count = out_grad.shape[0]
    routed = expert_ids == 0
    routed_mask = jnp.any(routed, axis=1)
    expert_prob = jnp.sum(jnp.where(routed, gate_prob, 0.0), axis=1)
    slot_index = jnp.cumsum(routed_mask.astype(jnp.int32)) - 1
    places = jnp.arange(CAP, dtype=jnp.int32)
    slot_hit = (slot_index[None, :] == places[:, None]) & routed_mask[None, :]
    source = jnp.sum(
        jnp.where(slot_hit, jnp.arange(tok_count, dtype=jnp.int32)[None, :], 0), axis=1
    )
    slot_valid = jnp.any(slot_hit, axis=1)
    sent_input = jnp.where(slot_valid[:, None], layer_input[source], jnp.zeros((), jnp.bfloat16))
    sent_grad = jnp.where(
        slot_valid[:, None],
        expert_prob[source][:, None] * out_grad[source].astype(jnp.float32),
        0.0,
    ).astype(jnp.bfloat16)
    routed_input, routed_grad = (
        lax.all_gather(sent_input, "expert", axis=0, tiled=True),
        lax.all_gather(sent_grad, "expert", axis=0, tiled=True),
    )
    local_shape = w_stack.shape
    factor = jnp.exp2(scale_exps.astype(jnp.float32))
    scaled = (
        w_stack.astype(jnp.float32).reshape(
            3, local_shape[1] // TILE, TILE, local_shape[2] // TILE, TILE
        )
        * factor[:, :, None, :, None]
    )
    weights = lax.all_gather(
        scaled.reshape(local_shape).astype(jnp.bfloat16), "dp", axis=1, tiled=True
    )
    gate_value = jnp.dot(routed_input, weights[0], preferred_element_type=jnp.float32)
    up_value = jnp.dot(routed_input, weights[1], preferred_element_type=jnp.float32)
    down_back = jnp.dot(routed_grad, weights[2], preferred_element_type=jnp.float32)
    gate_sigmoid = jax.nn.sigmoid(gate_value)
    gate_act = gate_value * gate_sigmoid
    gate_grad = (
        down_back * up_value * gate_sigmoid * (1.0 + gate_value * (1.0 - gate_sigmoid))
    ).astype(jnp.bfloat16)
    up_grad = (down_back * gate_act).astype(jnp.bfloat16)
    hidden = (gate_act * up_value).astype(jnp.bfloat16)
    returned = lax.psum_scatter(
        back_project(gate_grad, weights[0]) + back_project(up_grad, weights[1]),
        "expert",
        scatter_dimension=0,
        tiled=True,
    )
    picked = returned[jnp.clip(slot_index, 0, CAP - 1)]
    input_grad = jnp.where(routed_mask[:, None], picked, 0.0).astype(jnp.bfloat16)
    dp_count = lax.axis_size("dp")
    slot_rows = routed_input.shape[0]
    column_input, column_grad = (
        lax.all_to_all(routed_input, "dp", split_axis=1, concat_axis=0, tiled=True),
        lax.all_to_all(routed_grad, "dp", split_axis=1, concat_axis=0, tiled=True),
    )
    gate_all, up_all, hidden_all = (
        lax.all_gather(gate_grad, "dp", axis=0, tiled=True),
        lax.all_gather(up_grad, "dp", axis=0, tiled=True),
        lax.all_gather(hidden, "dp", axis=0, tiled=True),
    )
    column_input = column_input.reshape(dp_count, slot_rows, -1)
    column_grad = column_grad.reshape(dp_count, slot_rows, -1)
    gate_all = gate_all.reshape(dp_count, slot_rows, -1)
    up_all = up_all.reshape(dp_count, slot_rows, -1)
    hidden_all = hidden_all.reshape(dp_count, slot_rows, -1)
    each_group = jnp.stack(
        [
            jnp.einsum("rkd,rkh->rdh", column_input, gate_all, preferred_element_type=jnp.float32),
            jnp.einsum("rkd,rkh->rdh", column_input, up_all, preferred_element_type=jnp.float32),
            jnp.einsum("rkd,rkh->rdh", column_grad, hidden_all, preferred_element_type=jnp.float32),
        ],
        axis=1,
    )
    rounded = lax.optimization_barrier(each_group.astype(jnp.bfloat16))
    weight_grads = jnp.sum(rounded.astype(jnp.float32), axis=0)
    return (input_grad, weight_grads)


def solution(mesh):
    in_specs = (
        P(("dp", "expert"), None),
        P(("dp", "expert"), None),
        P(("dp", "expert"), None),
        P(("dp", "expert"), None),
        P(None, "dp", "expert"),
        P(None, "dp", "expert"),
    )
    out_specs = (P(("dp", "expert"), None), P(None, "dp", "expert"))
    return jax.shard_map(
        per_device, mesh=mesh, in_specs=in_specs, out_specs=out_specs, check_vma=False
    )
```

profile of v0, /device:TPU:0, one launch (start us, length us, event | category | flops | bytes accessed | tf_op | source)
XLA Modules:
  0.0 335.4 jit_solution(13567222837073245276)
XLA Ops:
  7.2 0.0 copy-start
  7.2 0.0 all-gather.4.cloned.1.call-start
  7.2 0.7 multiply_exponential_fusion
  7.9 4.4 %mul.42 = f32[3,6,128,8,128]{4,3,2,1,0:T(8,128)} broadcast(f32[3,6,8]{2,1,0:T(8,128)S(1)} %multiply_exponential_fusion), dimensions={0,1,3} | broadcast | bytes 9437760 | tf_op jit(solution)/shard_map/mul | solution.py:41
  12.4 11.2 %mul.43 = f32[3,768,1024]{2,1,0:T(8,128)} reshape(f32[3,6,128,8,128]{4,3,2,1,0:T(8,128)} %mul.42) | data formatting | bytes 18874368 | tf_op jit(solution)/shard_map/mul | solution.py:41
  23.6 9.1 %multiply_convert_fusion = bf16[3,768,1024]{2,1,0:T(8,128)(2,1)} fusion(f32[3,768,1024]{2,1,0:T(8,128)} %mul.43, bf16[3,768,1024]{2,1,0:T(8,128)(2,1)} %param.10), kind=kLoop, calls=%fused_computation.6 | loop fusion | flops 7077888 | bytes 18874368 | tf_op jit(solution)/shard_map/convert_element_type | solution.py:47
  32.7 0.0 all-gather.4.cloned.1.call-update
  32.7 0.2 reduce-window.4
  32.9 0.1 select_reduce_fusion
  33.1 0.6 gather_fusion.2
  33.7 0.1 fusion.12
  33.8 0.1 select_bitcast_fusion
  33.9 15.9 %all-gather.1 = bf16[8,3,3072]{2,1,0:T(4,128)(2,1)S(1)} all-gather(bf16[1,3,3072]{2,1,0:T(4,128)(2,1)S(1)} %select_bitcast_fusion), channel_id=1, replica_groups=mesh['dp'=4,'expert'=8] {'expert'}, dimensions={0}, use_global_device_ids=true | all-gather | bytes 165888 | tf_op jit(solution)/shard_map/all_gather | solution.py:35
  49.7 0.1 all_to_all.24
  49.9 0.7 copy.12
  50.6 3.7 %all-to-all-start = ((bf16[24,4,768]{2,0,1:T(8,128)(2,1)}), bf16[24,4,768]{2,0,1:T(8,128)(2,1)S(1)}, u32[]{:S(2)}, u32[]{:S(2)}) async-start(bf16[24,4,768]{2,0,1:T(8,128)(2,1)} %copy.12), calls=%async_computation | async-start | bytes 294912 | tf_op jit(solution)/shard_map/all_to_all | solution.py:70
  54.3 0.6 gather_fusion
  54.9 0.6 gather_fusion.1
  55.5 0.1 fusion.10
  55.6 14.1 %all-gather = bf16[8,3,3072]{2,1,0:T(4,128)(2,1)S(1)} all-gather(bf16[1,3,3072]{2,1,0:T(4,128)(2,1)S(1)} %fusion.10), channel_id=1, replica_groups=mesh['dp'=4,'expert'=8] {'expert'}, dimensions={0}, use_global_device_ids=true | all-gather | bytes 165888 | tf_op jit(solution)/shard_map/all_gather | solution.py:36
  69.7 0.1 all_to_all.27
  69.8 0.1 reshape.117
  69.9 0.1 reshape.119
  70.1 0.7 copy.13
  70.7 0.6 dynamic-slice
  72.0 140.3 %all-gather.4.cloned.1.call-done = bf16[3,3072,1024]{2,1,0:T(8,128)(2,1)} async-done(((bf16[3,768,1024]{2,1,0:T(8,128)(2,1)}), bf16[3,3072,1024]{2,1,0:T(8,128)(2,1)}) %all-gather.4.cloned.1.call-update) | async-done | bytes 18874384 | tf_op jit(solution)/shard_map/all_gather | solution.py:46
  212.3 3.9 %fusion = f32[24,1024]{1,0:T(8,128)S(1)} fusion(bf16[24,3072]{1,0:T(8,128)(2,1)S(1)} %reshape.117, bf16[3,3072,1024]{2,1,0:T(8,128)(2,1)} %all-gather.4.cloned.1.call-done), kind=kOutput, calls=%fused_computation.10 | convolution fusion | flops 150994944 | bytes 6537216 | tf_op jit(solution)/shard_map/dot_general | solution.py:51
  216.1 4.3 %fusion.4 = f32[24,1024]{1,0:T(8,128)S(1)} fusion(bf16[24,3072]{1,0:T(8,128)(2,1)S(1)} %reshape.119, bf16[3,3072,1024]{2,1,0:T(8,128)(2,1)} %all-gather.4.cloned.1.call-done), kind=kOutput, calls=%fused_computation.17 | convolution fusion | flops 150994944 | bytes 6537216 | tf_op jit(solution)/shard_map/dot_general | solution.py:49
  220.5 4.5 %multiply_convert_fusion.1 = (bf16[24,1024]{1,0:T(8,128)(2,1)S(1)}, bf16[24,1024]{1,0:T(8,128)(2,1)S(1)}, bf16[24,1024]{1,0:T(8,128)(2,1)S(1)}) fusion(f32[24,1024]{1,0:T(8,128)S(1)} %fusion.4, f32[24,1024]{1,0:T(8,128)S(1)} %fusion, bf16[24,3072]{1,0:T(8,128)(2,1)S(1)} %reshape.119, bf16[3,3072,1024]{2,1,0:T(8,128)(2,1)} %all-gather.4.cloned.1.call-done), kind=kOutput, calls=%fused_computation.23 | convolution fusion | flops 151363584 | bytes 6782976 | tf_op jit(solution)/shard_map/dot_general | solution.py:50
  225.0 0.0 copy-done.3
  225.0 1.7 fusion.1
  226.7 1.8 fusion.5
  228.5 31.7 %all-reduce.2 = bf16[24,3072]{1,0:T(8,128)(2,1)S(1)} all-reduce(f32[24,3072]{1,0:T(8,128)S(1)} %fusion.5), channel_id=2, replica_groups=mesh['dp'=4,'expert'=8] {'expert'}, use_global_device_ids=true, to_apply=%region_5.6.clone | all-reduce | flops 73728 | bytes 442368
  260.2 0.6 gather_fusion.3
  260.8 0.7 select_convert_fusion
  261.5 9.0 %all_gather.21 = bf16[96,1024]{1,0:T(8,128)(2,1)S(1)} all-gather(bf16[24,1024]{1,0:T(8,128)(2,1)S(1)} %get-tuple-element.3), channel_id=1, replica_groups=mesh['dp'=4,'expert'=8] {'dp'}, dimensions={0}, use_global_device_ids=true | all-gather | bytes 245760 | tf_op jit(solution)/shard_map/all_gather | solution.py:74
  270.5 7.9 %all_gather.22 = bf16[96,1024]{1,0:T(8,128)(2,1)S(1)} all-gather(bf16[24,1024]{1,0:T(8,128)(2,1)S(1)} %get-tuple-element.4), channel_id=1, replica_groups=mesh['dp'=4,'expert'=8] {'dp'}, dimensions={0}, use_global_device_ids=true | all-gather | bytes 245760 | tf_op jit(solution)/shard_map/all_gather | solution.py:75
  278.3 0.0 all-to-all-done
  278.3 3.5 %all-to-all-start.1 = ((bf16[24,4,768]{2,0,1:T(8,128)(2,1)}), bf16[24,4,768]{2,0,1:T(8,128)(2,1)S(1)}, u32[]{:S(2)}, u32[]{:S(2)}) async-start(bf16[24,4,768]{2,0,1:T(8,128)(2,1)} %copy.13), calls=%async_computation.1 | async-start | bytes 294912 | tf_op jit(solution)/shard_map/all_to_all | solution.py:71
  281.9 4.5 %convert_bitcast_fusion.1 = bf16[4,1,768,1024]{3,2,0,1:T(8,128)(2,1)} fusion(bf16[4,24,1024]{2,1,0:T(8,128)(2,1)S(1)} %bitcast.58, bf16[24,4,768]{2,0,1:T(8,128)(2,1)S(1)} %all-to-all-done), kind=kOutput, calls=%fused_computation.12 | convolution fusion | flops 154140672 | bytes 6635520 | tf_op jit(solution)/shard_map/rkd,rkh->rdh/dot_general | solution.py:86
  286.4 4.4 %convert_bitcast_fusion.2 = bf16[4,1,768,1024]{3,2,0,1:T(8,128)(2,1)} fusion(bf16[4,24,1024]{2,1,0:T(8,128)(2,1)S(1)} %bitcast.57, bf16[24,4,768]{2,0,1:T(8,128)(2,1)S(1)} %all-to-all-done), kind=kOutput, calls=%fused_computation.13 | convolution fusion | flops 154140672 | bytes 6635520 | tf_op jit(solution)/shard_map/rkd,rkh->rdh/dot_general | solution.py:85
  290.9 9.0 %all_gather.23 = bf16[96,1024]{1,0:T(8,128)(2,1)S(1)} all-gather(bf16[24,1024]{1,0:T(8,128)(2,1)S(1)} %get-tuple-element.2), channel_id=1, replica_groups=mesh['dp'=4,'expert'=8] {'dp'}, dimensions={0}, use_global_device_ids=true | all-gather | bytes 245760 | tf_op jit(solution)/shard_map/all_gather | solution.py:76
  299.9 0.0 all-to-all-done.1
  299.9 0.0 copy-start.2
  299.9 1.8 convert_bitcast_fusion
  301.7 0.9 copy-done.2
  302.7 11.1 %pad_maximum_fusion = bf16[4,3,768,1024]{3,2,0,1:T(8,128)(2,1)} fusion(bf16[4,1,768,1024]{3,2,0,1:T(8,128)(2,1)S(1)} %convert_bitcast_fusion, bf16[4,1,768,1024]{3,2,0,1:T(8,128)(2,1)S(1)} %copy-done.2, bf16[4,1,768,1024]{3,2,0,1:T(8,128)(2,1)} %convert_bitcast_fusion.2), kind=kLoop, calls=%fused_computation.5 | loop fusion | flops 18874368 | bytes 37748736 | tf_op jit(solution)/shard_map/stack | solution.py:83
  313.7 14.8 %convert_reduce_fusion = f32[3,768,1024]{2,1,0:T(8,128)} fusion(bf16[4,3,768,1024]{3,2,0,1:T(8,128)(2,1)} %pad_maximum_fusion), kind=kLoop, calls=%fused_computation.4 | loop fusion | flops 16515072 | bytes 28311552 | tf_op jit(solution)/shard_map/reduce_sum | solution.py:92
  (20 shorter events, 0.1 us)
Async XLA Ops:
  7.2 25.9 %copy-start = (bf16[12,3072]{1,0:T(8,128)(2,1)S(1)}, bf16[12,3072]{1,0:T(8,128)(2,1)}, u32[]{:S(2)}) copy-start(bf16[12,3072]{1,0:T(8,128)(2,1)} %param.7) | copy-start | bytes 221188
  7.2 205.1 %all-gather.4.cloned.1.call-start = ((), (), s32[]{:S(2)}) async-start(), calls=%async_computation.2 | async-start | bytes 23592960 | tf_op jit(solution)/shard_map/all_gather | solution.py:46
  23.6 9.1 %copy-start.5 = (s32[12,2]{0,1:T(2,128)S(1)}, s32[12,2]{0,1:T(2,128)}, u32[]{:S(2)}) copy-start(s32[12,2]{0,1:T(2,128)} %param.8) | copy-start | bytes 292
  23.6 30.7 %copy-start.6 = (f32[12,2]{0,1:T(2,128)S(1)}, f32[12,2]{0,1:T(2,128)}, u32[]{:S(2)}) copy-start(f32[12,2]{0,1:T(2,128)} %param.9) | copy-start | bytes 292
  23.6 31.4 %copy-start.4 = (bf16[12,3072]{1,0:T(8,128)(2,1)S(1)}, bf16[12,3072]{1,0:T(8,128)(2,1)}, u32[]{:S(2)}) copy-start(bf16[12,3072]{1,0:T(8,128)(2,1)} %param.6) | copy-start | bytes 221188
  23.6 47.2 %copy-start.7 = (u32[32]{0:T(128)S(1)}, u32[32]{0:T(128)}, u32[]{:S(2)}) copy-start(u32[32]{0:T(128)} %constant.34) | copy-start | bytes 388
  50.6 227.8 %all-to-all-start = ((bf16[24,4,768]{2,0,1:T(8,128)(2,1)}), bf16[24,4,768]{2,0,1:T(8,128)(2,1)S(1)}, u32[]{:S(2)}, u32[]{:S(2)}) async-start(bf16[24,4,768]{2,0,1:T(8,128)(2,1)} %copy.12), calls=%async_computation | async-start | bytes 294912 | tf_op jit(solution)/shard_map/all_to_all | solution.py:70
  212.3 12.7 %copy-start.3 = (bf16[3,3072,1024]{2,1,0:T(8,128)(2,1)S(1)}, bf16[3,3072,1024]{2,1,0:T(8,128)(2,1)}, u32[]{:S(2)}) copy-start(bf16[3,3072,1024]{2,1,0:T(8,128)(2,1)} %all-gather.4.cloned.1.call-done) | copy-start | bytes 56623108
  278.3 21.5 %all-to-all-start.1 = ((bf16[24,4,768]{2,0,1:T(8,128)(2,1)}), bf16[24,4,768]{2,0,1:T(8,128)(2,1)S(1)}, u32[]{:S(2)}, u32[]{:S(2)}) async-start(bf16[24,4,768]{2,0,1:T(8,128)(2,1)} %copy.13), calls=%async_computation.1 | async-start | bytes 294912 | tf_op jit(solution)/shard_map/all_to_all | solution.py:71
  299.9 2.8 copy-start.2
  302.7 25.9 %copy-start.1 = (bf16[12,3072]{1,0:T(8,128)(2,1)S(1)}, bf16[12,3072]{1,0:T(8,128)(2,1)}, u32[]{:S(2)}) copy-start(bf16[12,3072]{1,0:T(8,128)(2,1)} %param.7) | copy-start | bytes 221188
Sparse Core Ops, SparseCore 0:
  32.8 179.3 all-gather.3
where the time goes:
time: 336 us; the launch traced here: 335 us
  waiting for transfers between devices  140 us (42%)
  blocking collectives  87.5 us (26%)
  other arithmetic  37.1 us (11%)
  matrix products  27 us (8%)
  local copies, waits for them, and re-layouts  21.4 us (6%)
  between operations  14.8 us (4%)
  starting transfers between devices  7.28 us (2%)
    all_gather x1, waiting for transfers between devices, per_device(): lax.all_gather(scaled.reshape(local_shape).astype(jnp.bfloat16), 'dp', ax...  140 us
    unnamed x1, blocking collectives  31.7 us
    all_gather x1, blocking collectives, per_device(): lax.all_gather(sent_input, 'expert', axis=0, tiled=True)  15.9 us
    mul x2, local copies, waits for them, and re-layouts, per_device(): w_stack.astype(jnp.float32)  15.6 us
    reduce_sum x1, other arithmetic, per_device(): weight_grads = jnp.sum(rounded.astype(jnp.float32), axis=0)  14.8 us
    all_gather x1, blocking collectives, per_device(): lax.all_gather(sent_grad, 'expert', axis=0, tiled=True)  14.1 us
    another operation x1, other arithmetic, per_device(): jnp.stack([jnp.einsum('rkd,rkh->rdh', column_input, gate_all, preferred_e...  11.1 us
    convert_element_type x1, other arithmetic, per_device(): scaled.reshape(local_shape).astype(jnp.bfloat16)  9.1 us
  transfers between devices with their start and end apart: 3, of which 1 were waited for; matrix products, arithmetic and copies ran while one was open for 9% of the time, Pallas kernels for 0%

commit v1 on v0

v1 whole, which is shorter than its diff:
```python
import jax
import jax.numpy as jnp
from jax import lax
from jax.experimental import pallas as pl
from jax.experimental.pallas import tpu as pltpu
from jax.sharding import PartitionSpec as P

CAP = 3
BF16 = jnp.bfloat16
F32 = jnp.float32
I32 = jnp.int32
ROWS = 8
CORES = 2
VMEM = pltpu.VMEM
SMEM = pltpu.SMEM


def log2(n):
    return n.bit_length() - 1


def is_pow2(n):
    return n & (n - 1) == 0


def xor_pairs(n, k):
    return [(i, i ^ k) for i in range(n)]


def nn(a, b):
    return lax.dot_general(a, b, (((1,), (0,)), ((), ())), preferred_element_type=F32)


def nt(a, b):
    return lax.dot_general(a, b, (((1,), (1,)), ((), ())), preferred_element_type=F32)


def tn(a, b):
    return lax.dot_general(a, b, (((0,), (0,)), ((), ())), preferred_element_type=F32)


def slots_kernel(p_ref, ids_ref, prob_ref, grad_ref, inp_ref, hit_ref, *refs):
    outs, scratch = refs[:-1], refs[-1]
    n_dp = len(outs)
    width = outs[0].shape[1]
    tok = ids_ref.shape[1]
    named = ids_ref[...] == 0
    prob = jnp.sum(jnp.where(named, prob_ref[...], 0.0), axis=0, keepdims=True)
    routed = jnp.sum(named.astype(F32), axis=0, keepdims=True)
    earlier = lax.broadcasted_iota(I32, (tok, tok), 0) <= lax.broadcasted_iota(I32, (tok, tok), 1)
    rank = nn(jnp.broadcast_to(routed, (ROWS, tok)).astype(BF16), earlier.astype(BF16)) - 1.0
    row = lax.broadcasted_iota(I32, (ROWS, tok), 0)
    is_routed = jnp.broadcast_to(routed, (ROWS, tok)) > 0.5
    hit_in = is_routed & (rank == row.astype(F32))
    hit_gr = is_routed & (rank == (row - CAP).astype(F32))
    hit_in = jnp.where(hit_in & (row < CAP), 1.0, 0.0)
    hit_gr = jnp.where(hit_gr & (row >= CAP) & (row < 2 * CAP), 1.0, 0.0)
    slot_prob = jnp.sum(hit_gr * prob, axis=1, keepdims=True)
    hit_ref[...] = hit_in
    rows = nn(hit_in.astype(BF16), inp_ref[...]) + slot_prob * nn(hit_gr.astype(BF16), grad_ref[...])
    for d in range(n_dp):
        scratch[d] = rows[:, d * width : (d + 1) * width].astype(BF16)
    p = p_ref[0]
    for k in range(n_dp):
        outs[k][...] = scratch[p ^ k]


def slots(p, ids, prob, grad, inp, n_dp):
    tok, d_model = inp.shape
    width = d_model // n_dp
    return pl.pallas_call(
        slots_kernel,
        out_shape=[jax.ShapeDtypeStruct((ROWS, tok), F32)]
        + [jax.ShapeDtypeStruct((ROWS, width), BF16)] * n_dp,
        in_specs=[pl.BlockSpec(memory_space=SMEM)] + [pl.BlockSpec(memory_space=VMEM)] * 4,
        out_specs=[pl.BlockSpec(memory_space=VMEM)] * (n_dp + 1),
        scratch_shapes=[pltpu.VMEM((n_dp, ROWS, width), BF16)],
        name="slots",
    )(p, ids, prob, grad, inp)


def scale_kernel(factor_ref, w_ref, out_ref, *, tile):
    a = pl.program_id(0)
    r = pl.program_id(1)
    _, rows, cols = w_ref.shape
    for i in range(rows // tile):
        for j in range(cols // tile):
            at = (0, slice(i * tile, (i + 1) * tile), slice(j * tile, (j + 1) * tile))
            factor = factor_ref[a, r * (rows // tile) + i, j]
            out_ref[at] = (w_ref[at].astype(F32) * factor).astype(BF16)


def scale_weights(factor, w):
    import functools

    n, rows, cols = w.shape
    tile = rows // factor.shape[1]
    steps = 2 if factor.shape[1] % 2 == 0 else 1
    block = (1, rows // steps, cols)
    return pl.pallas_call(
        functools.partial(scale_kernel, tile=tile),
        grid=(n, steps),
        out_shape=jax.ShapeDtypeStruct(w.shape, BF16),
        in_specs=[
            pl.BlockSpec(memory_space=SMEM),
            pl.BlockSpec(block, lambda a, r: (a, r, 0)),
        ],
        out_specs=pl.BlockSpec(block, lambda a, r: (a, r, 0)),
        name="scale",
    )(factor, w)


def forward_kernel(p_ref, m0_ref, m1_ref, w_ref, x_ref, a_ref, b_ref, *, n_dp, n_z):
    slot_count = x_ref.shape[1]
    group = slot_count // n_dp
    span = m0_ref.shape[0]
    p = p_ref[0]
    col = lax.broadcasted_iota(I32, (1, span), 1)
    r = col & (ROWS - 1)
    pk = (col >> log2(ROWS)) & (n_dp - 1)
    zk = col >> (log2(ROWS) + log2(n_dp))
    line = lax.broadcasted_iota(I32, (slot_count, span), 0)

    def pick(low):
        total = None
        for ck, m_ref in enumerate((m0_ref, m1_ref)):
            slot = (p ^ pk) * group + (ck * n_z + zk) * CAP + (r - low)
            slot = jnp.where((r >= low) & (r < low + CAP), slot, -1)
            sel = jnp.where(line == slot, 1.0, 0.0).astype(BF16)
            part = nn(sel, m_ref[...])
            total = part if total is None else total + part
        return total.astype(BF16)

    x = pick(0)
    g = pick(CAP)
    x_ref[0] = x
    x_ref[1] = g
    half = a_ref.shape[2]
    for i, left in enumerate((x, x, g)):
        a_ref[i] = nn(left, w_ref[i, :, :half]).astype(BF16)
        b_ref[i] = nn(left, w_ref[i, :, half:]).astype(BF16)


def forward(p, m0, m1, w, n_dp, n_z):
    import functools

    slot_count = n_dp * CORES * n_z * CAP
    n, width, cols = w.shape
    part = jax.ShapeDtypeStruct((n, slot_count, cols // 2), BF16)
    return pl.pallas_call(
        functools.partial(forward_kernel, n_dp=n_dp, n_z=n_z),
        out_shape=[jax.ShapeDtypeStruct((2, slot_count, width), BF16), part, part],
        in_specs=[pl.BlockSpec(memory_space=SMEM)] + [pl.BlockSpec(memory_space=VMEM)] * 3,
        out_specs=[pl.BlockSpec(memory_space=VMEM)] * 3,
        name="forward",
    )(p, m0, m1, w)


def backward_kernel(p_ref, a_ref, ra_ref, b_ref, rb_ref, w_ref, g_ref, keep_ref, send_ref, *, n_dp, n_z):
    slot_count = g_ref.shape[1]
    group = slot_count // n_dp
    half = a_ref.shape[2]
    back = None
    for h, (u_ref, v_ref) in enumerate(((a_ref, ra_ref), (b_ref, rb_ref))):
        at = slice(h * half, (h + 1) * half)
        gate = u_ref[0].astype(F32) + v_ref[0].astype(F32)
        up = u_ref[1].astype(F32) + v_ref[1].astype(F32)
        down = u_ref[2].astype(F32) + v_ref[2].astype(F32)
        sig = jax.nn.sigmoid(gate)
        act = gate * sig
        gate_grad = (down * up * sig * (1.0 + gate * (1.0 - sig))).astype(BF16)
        up_grad = (down * act).astype(BF16)
        g_ref[0, :, at] = gate_grad
        g_ref[1, :, at] = up_grad
        g_ref[2, :, at] = (act * up).astype(BF16)
        part = nt(gate_grad, w_ref[0, :, at]) + nt(up_grad, w_ref[1, :, at])
        back = part if back is None else back + part
    back = back.astype(BF16)
    p = p_ref[0]
    rows = keep_ref.shape[0]
    capp = rows // (n_z * n_dp)
    for ck, out_ref in enumerate((keep_ref, send_ref)):
        o = lax.broadcasted_iota(I32, (rows, slot_count), 0)
        c = o & (capp - 1)
        pk = (o >> log2(capp)) & (n_dp - 1)
        zk = o >> (log2(capp) + log2(n_dp))
        slot = (p ^ pk) * group + (ck * n_z + zk) * CAP + c
        hit = (lax.broadcasted_iota(I32, (rows, slot_count), 1) == slot) & (c < CAP)
        out_ref[...] = nn(jnp.where(hit, 1.0, 0.0).astype(BF16), back).astype(BF16)


def backward(p, a, ra, b, rb, w, n_dp, n_z):
    import functools

    n, slot_count, half = a.shape
    width = w.shape[1]
    capp = 4
    out = jax.ShapeDtypeStruct((n_z * n_dp * capp, width), BF16)
    return pl.pallas_call(
        functools.partial(backward_kernel, n_dp=n_dp, n_z=n_z),
        out_shape=[jax.ShapeDtypeStruct((n, slot_count, 2 * half), BF16), out, out],
        in_specs=[pl.BlockSpec(memory_space=SMEM)] + [pl.BlockSpec(memory_space=VMEM)] * 5,
        out_specs=[pl.BlockSpec(memory_space=VMEM)] * 3,
        name="backward",
    )(p, a, ra, b, rb, w)


def weight_grad_kernel(x_ref, g_ref, out_ref):
    out_ref[0] = tn(x_ref[0], g_ref[0])


def weight_grad(x, g):
    n, slot_count, cols = g.shape
    width = x.shape[2]
    steps = 3 if width % (3 * 128) == 0 else 1
    tile = width // steps
    return pl.pallas_call(
        weight_grad_kernel,
        grid=(n, steps),
        out_shape=jax.ShapeDtypeStruct((n, width, cols), F32),
        in_specs=[
            pl.BlockSpec((1, slot_count, tile), lambda a, r: (a // 2, 0, r)),
            pl.BlockSpec((1, slot_count, cols), lambda a, r: (a, 0, 0)),
        ],
        out_specs=pl.BlockSpec((1, tile, cols), lambda a, r: (a, r, 0)),
        name="weight_grad",
    )(x, g)


def place_kernel(p_ref, hit_ref, *refs):
    parts, out_ref = refs[:-1], refs[-1]
    width = parts[0].shape[1]
    capp = parts[0].shape[0]
    p = p_ref[0]
    hit = hit_ref[:capp, :].astype(BF16)
    for k, part in enumerate(parts):
        at = pl.multiple_of((p ^ k) * width, 128)
        out_ref[:, pl.ds(at, width)] = tn(hit, part[...]).astype(BF16)


def place(p, hit, parts, tok):
    capp, width = parts[0].shape
    return pl.pallas_call(
        place_kernel,
        out_shape=jax.ShapeDtypeStruct((tok, width * len(parts)), BF16),
        in_specs=[pl.BlockSpec(memory_space=SMEM)]
        + [pl.BlockSpec(memory_space=VMEM)] * (1 + len(parts)),
        out_specs=pl.BlockSpec(memory_space=VMEM),
        name="place",
    )(p, hit, *parts)


def add_bf16(u, v):
    return (u.astype(F32) + v.astype(F32)).astype(BF16)


def per_device_fast(out_grad, layer_input, expert_ids, gate_prob, w_stack, scale_exps):
    n_dp = lax.axis_size("dp")
    n_ex = lax.axis_size("expert")
    n_z = n_ex // CORES
    tok = out_grad.shape[0]
    p = lax.axis_index("dp").astype(I32).reshape(1)
    hit, *blocks = slots(p, expert_ids.T, gate_prob.T, out_grad, layer_input, n_dp)
    factor = jnp.exp2(scale_exps.astype(F32))
    w = scale_weights(factor, w_stack)
    got = [blocks[0]] + [
        lax.ppermute(blocks[k], "dp", xor_pairs(n_dp, k)) for k in range(1, n_dp)
    ]
    mine = jnp.concatenate(got, axis=0)
    column = [mine] + [
        lax.ppermute(mine, "expert", xor_pairs(n_ex, k * CORES)) for k in range(1, n_z)
    ]
    m0 = jnp.concatenate(column, axis=0)
    m1 = lax.ppermute(m0, "expert", xor_pairs(n_ex, 1))
    x, a, b = forward(p, m0, m1, w, n_dp, n_z)
    ra = lax.ppermute(a, "dp", xor_pairs(n_dp, 1))
    rb = lax.ppermute(b, "dp", xor_pairs(n_dp, 2))
    a = add_bf16(a, ra)
    b = add_bf16(b, rb)
    ra = lax.ppermute(a, "dp", xor_pairs(n_dp, 2))
    rb = lax.ppermute(b, "dp", xor_pairs(n_dp, 1))
    g, keep, send = backward(p, a, ra, b, rb, w, n_dp, n_z)
    weight_grads = weight_grad(x, g)
    summed = add_bf16(keep, lax.ppermute(send, "expert", xor_pairs(n_ex, 1)))
    summed = summed.reshape(n_z, -1, summed.shape[1])
    total = summed[0].astype(F32)
    for k in range(1, n_z):
        total = total + lax.ppermute(summed[k], "expert", xor_pairs(n_ex, k * CORES)).astype(F32)
    total = total.astype(BF16).reshape(n_dp, -1, summed.shape[2])
    parts = [total[0]] + [
        lax.ppermute(total[k], "dp", xor_pairs(n_dp, k)) for k in range(1, n_dp)
    ]
    input_grad = place(p, hit, parts, tok)
    return input_grad, weight_grads


def per_device_any(out_grad, layer_input, expert_ids, gate_prob, w_stack, scale_exps):
    n_dp = lax.axis_size("dp")
    tok, d_model = out_grad.shape
    routed = expert_ids == 0
    mask = jnp.any(routed, axis=1)
    prob = jnp.sum(jnp.where(routed, gate_prob, 0.0), axis=1)
    rank = jnp.cumsum(mask.astype(I32)) - 1
    hit = ((rank[None, :] == jnp.arange(CAP)[:, None]) & mask[None, :]).astype(BF16)
    slot_input = jnp.dot(hit, layer_input, preferred_element_type=F32)
    slot_prob = jnp.sum(hit.astype(F32) * prob[None, :], axis=1)
    slot_grad = slot_prob[:, None] * jnp.dot(hit, out_grad, preferred_element_type=F32)
    both = jnp.stack([slot_input, slot_grad]).astype(BF16)
    both = both.reshape(2, CAP, n_dp, d_model // n_dp).transpose(2, 0, 1, 3)
    both = lax.all_to_all(both, "dp", split_axis=0, concat_axis=0, tiled=True)
    both = lax.all_gather(both, "expert", axis=0)
    both = both.transpose(2, 0, 1, 3, 4)
    lead = both.shape[1:4]
    both = both.reshape(2, -1, both.shape[-1])
    n, rows, cols = w_stack.shape
    factor = jnp.exp2(scale_exps.astype(F32))
    tiles = factor.shape[1:]
    w = w_stack.astype(F32).reshape(n, tiles[0], rows // tiles[0], tiles[1], cols // tiles[1])
    w = (w * factor[:, :, None, :, None]).reshape(n, rows, cols).astype(BF16)
    sides = jnp.stack([both[0], both[0], both[1]])
    partial = jnp.einsum("nrk,nkh->nrh", sides, w, preferred_element_type=F32)
    gate, up, down = lax.psum(partial, "dp")
    sig = jax.nn.sigmoid(gate)
    act = gate * sig
    gate_grad = (down * up * sig * (1.0 + gate * (1.0 - sig))).astype(BF16)
    up_grad = (down * act).astype(BF16)
    hidden = (act * up).astype(BF16)
    back = nt(gate_grad, w[0]) + nt(up_grad, w[1])
    back = lax.psum_scatter(back.reshape(lead + (rows,)), "expert", scatter_dimension=0, tiled=False)
    back = lax.all_to_all(back, "dp", split_axis=0, concat_axis=0, tiled=True)
    back = back.transpose(1, 0, 2).reshape(CAP, d_model)
    input_grad = tn(hit, back.astype(BF16)).astype(BF16)
    weight_grads = jnp.einsum(
        "nrd,nrh->ndh", sides, jnp.stack([gate_grad, up_grad, hidden]), preferred_element_type=F32
    )
    return input_grad, weight_grads


def solution(mesh):
    n_dp, n_ex = mesh.shape["dp"], mesh.shape["expert"]
    n_z = n_ex // CORES
    fast = n_dp == 4 and n_ex % CORES == 0 and is_pow2(n_z) and n_z <= 4
    in_specs = (
        P(("dp", "expert"), None),
        P(("dp", "expert"), None),
        P(("dp", "expert"), None),
        P(("dp", "expert"), None),
        P(None, "dp", "expert"),
        P(None, "dp", "expert"),
    )
    out_specs = (P(("dp", "expert"), None), P(None, "dp", "expert"))
    return jax.shard_map(
        per_device_fast if fast else per_device_any,
        mesh=mesh,
        in_specs=in_specs,
        out_specs=out_specs,
        check_vma=False,
    )
```

time: 336 us -> 84.2 us (0.25)
  waiting for transfers between devices: 140 us -> 30.1 us
  blocking collectives: 87.5 us -> 0 us
  other arithmetic: 37.1 us -> 4.33 us
  matrix products: 27 us -> 0 us
  Pallas kernels: 0 us -> 27 us
  local copies, waits for them, and re-layouts: 21.4 us -> 3.34 us
  between operations: 14.8 us -> 0.77 us
  starting transfers between devices: 7.28 us -> 18 us
    all_gather x1 -> x0, waiting for transfers between devices: 140 us -> none  [per_device(): lax.all_gather(scaled.reshape(local_shape).astype(jnp.bfloat16), 'dp', ax...]
    all_gather x5 -> x0, blocking collectives: 55.8 us -> none  [the longest x1 15.9 us: per_device(): lax.all_gather(sent_input, 'expert', axis=0, tiled=True)]
    unnamed x1 -> x0, blocking collectives: 31.7 us -> none
    ppermute x0 -> x18, waiting for transfers between devices: none -> 30.1 us  [the longest x1 8.59 us: per_device_fast(): ra = lax.ppermute(a, 'dp', xor_pairs(n_dp, 1))]
    pallas_call x0 -> x6, Pallas kernels: none -> 27 us  [the longest x1 8.02 us: weight_grad(): pl.pallas_call(weight_grad_kernel, grid=(n, steps), out_shape=jax.ShapeDt...]
    dot_general x8 -> x0, matrix products: 27 us -> none  [the longest x1 4.55 us: per_device(): jnp.einsum('rkd,rkh->rdh', column_input, up_all, preferred_element_type=j...]
    ppermute x0 -> x18, starting transfers between devices: none -> 18 us  [the longest x3 4.5 us: per_device_fast(): lax.ppermute(blocks[k], 'dp', xor_pairs(n_dp, k))]
    mul x2 -> x0, local copies, waits for them, and re-layouts: 15.6 us -> none  [per_device(): w_stack.astype(jnp.float32)]
  transfers between devices with their start and end apart: 3 -> 18, of which waited for: 1 -> 11; matrix products, arithmetic and copies ran while one was open for 9% -> 5% of each run, Pallas kernels for 0% -> 17%
where the time goes in v1:
time: 84.2 us; the launch traced here: 83.5 us
  waiting for transfers between devices  30.1 us (36%)
  Pallas kernels  27 us (32%)
  starting transfers between devices  18 us (21%)
  other arithmetic  4.33 us (5%)
  local copies, waits for them, and re-layouts  3.34 us (4%)
    ppermute x1, waiting for transfers between devices, per_device_fast(): ra = lax.ppermute(a, 'dp', xor_pairs(n_dp, 1))  8.59 us
    pallas_call x1, Pallas kernels, weight_grad(): pl.pallas_call(weight_grad_kernel, grid=(n, steps), out_shape=jax.ShapeDt...  8.02 us
    pallas_call x1, Pallas kernels, scale_weights(): pl.pallas_call(functools.partial(scale_kernel, tile=tile), grid=(n, steps...  6.45 us
    ppermute x1, waiting for transfers between devices, per_device_fast(): ra = lax.ppermute(a, 'dp', xor_pairs(n_dp, 2))  6.4 us
    ppermute x3, waiting for transfers between devices, per_device_fast(): lax.ppermute(mine, 'expert', xor_pairs(n_ex, k * CORES))  5.4 us
    pallas_call x1, Pallas kernels, backward(): pl.pallas_call(functools.partial(backward_kernel, n_dp=n_dp, n_z=n_z), ou...  4.73 us
    ppermute x3, starting transfers between devices, per_device_fast(): lax.ppermute(blocks[k], 'dp', xor_pairs(n_dp, k))  4.5 us
    pallas_call x1, Pallas kernels, forward(): pl.pallas_call(functools.partial(forward_kernel, n_dp=n_dp, n_z=n_z), out...  4.34 us
  transfers between devices with their start and end apart: 18, of which 11 were waited for; matrix products, arithmetic and copies ran while one was open for 5% of the time, Pallas kernels for 17%

profile of v1, /device:TPU:0, one launch (start us, length us, event | category | flops | bytes accessed | tf_op | source)
XLA Modules:
  0.0 83.5 jit_solution(3550580753404439275)
XLA Ops:
  0.6 1.9 %slots.1 = (f32[8,12]{1,0:T(8,128)}, bf16[8,768]{1,0:T(8,128)(2,1)}, bf16[8,768]{1,0:T(8,128)(2,1)}, bf16[8,768]{1,0:T(8,128)(2,1)}, bf16[8,768]{1,0:T(8,128)(2,1)}) custom-call(s32[1]{0:T(128)} %bitcast.p_ref, s32[2,12]{1,0:T(2,128)} %bitcast.3, f32[2,12]{1,0:T(2,128)} %bitcast.4, bf16[12,3072]{1,0:T(8,128)(2,1)} %grad_ref.1, bf16[12,3072]{1,0:T(8,128)(2,1)} %inp_ref.1), custom_call_target="tpu_custom_call" | custom-call | tf_op jit(solution)/shard_map/slots/pallas_call | solution.py:71
  2.5 3.0 %collective-permute-start = (bf16[8,768]{1,0:T(8,128)(2,1)}, bf16[8,768]{1,0:T(8,128)(2,1)S(1)}, u32[]{:S(2)}, u32[]{:S(2)}) collective-permute-start(bf16[8,768]{1,0:T(8,128)(2,1)} %get-tuple-element.15), channel_id=1, source_target_pairs={{0,8},{8,0},{16,24},{24,16},{1,9},{9,1},{17,25},{25,17},{2,10},{10... | collective-permute-start | bytes 36872 | tf_op jit(solution)/shard_map/ppermute | solution.py:267
  5.5 1.5 %collective-permute-start.1 = (bf16[8,768]{1,0:T(8,128)(2,1)}, bf16[8,768]{1,0:T(8,128)(2,1)S(1)}, u32[]{:S(2)}, u32[]{:S(2)}) collective-permute-start(bf16[8,768]{1,0:T(8,128)(2,1)} %get-tuple-element.16), channel_id=1, source_target_pairs={{0,16},{8,24},{16,0},{24,8},{1,17},{9,25},{17,1},{25,9},{2,18},{10... | collective-permute-start | bytes 36872 | tf_op jit(solution)/shard_map/ppermute | solution.py:267
  7.0 0.0 collective-permute-start.2
  7.0 0.7 constant_dynamic-update-slice_fusion.3
  7.7 0.0 collective-permute-done
  7.7 1.7 %collective-permute-done.1 = bf16[8,768]{1,0:T(8,128)(2,1)S(1)} collective-permute-done((bf16[8,768]{1,0:T(8,128)(2,1)}, bf16[8,768]{1,0:T(8,128)(2,1)S(1)}, u32[]{:S(2)}, u32[]{:S(2)}) %collective-permute-start.1) | collective-permute-done | bytes 12320 | tf_op jit(solution)/shard_map/ppermute | solution.py:267
  9.4 2.4 %collective-permute-done.2 = bf16[8,768]{1,0:T(8,128)(2,1)S(1)} collective-permute-done((bf16[8,768]{1,0:T(8,128)(2,1)}, bf16[8,768]{1,0:T(8,128)(2,1)S(1)}, u32[]{:S(2)}, u32[]{:S(2)}) %collective-permute-start.2) | collective-permute-done | bytes 12320 | tf_op jit(solution)/shard_map/ppermute | solution.py:267
  11.8 1.6 %collective-permute-start.3 = (bf16[32,768]{1,0:T(8,128)(2,1)S(1)}, bf16[32,768]{1,0:T(8,128)(2,1)S(1)}, u32[]{:S(2)}, u32[]{:S(2)}) collective-permute-start(bf16[32,768]{1,0:T(8,128)(2,1)S(1)} %get-tuple-element.31), channel_id=1, source_target_pairs={{0,2},{1,3},{2,0},{3,1},{4,6},{5,7},{6,4},{7,5},{8,10},{9,11},{10,... | collective-permute-start | bytes 147464 | tf_op jit(solution)/shard_map/ppermute | solution.py:271
  13.4 2.5 %collective-permute-start.5 = (bf16[32,768]{1,0:T(8,128)(2,1)S(1)}, bf16[32,768]{1,0:T(8,128)(2,1)S(1)}, u32[]{:S(2)}, u32[]{:S(2)}) collective-permute-start(bf16[32,768]{1,0:T(8,128)(2,1)S(1)} %get-tuple-element.31), channel_id=1, source_target_pairs={{0,6},{1,7},{2,4},{3,5},{4,2},{5,3},{6,0},{7,1},{8,14},{9,15},{10,... | collective-permute-start | bytes 147464 | tf_op jit(solution)/shard_map/ppermute | solution.py:271
  15.9 0.1 collective-permute-start.4
  16.0 0.5 collective-permute-done.3
  16.5 4.9 %collective-permute-done.4 = bf16[32,768]{1,0:T(8,128)(2,1)S(1)} collective-permute-done((bf16[32,768]{1,0:T(8,128)(2,1)S(1)}, bf16[32,768]{1,0:T(8,128)(2,1)S(1)}, u32[]{:S(2)}, u32[]{:S(2)}) %collective-permute-start.4) | collective-permute-done | bytes 49184 | tf_op jit(solution)/shard_map/ppermute | solution.py:271
  21.4 0.0 collective-permute-done.5
  21.4 0.1 collective-permute-start.6
  21.5 1.3 %multiply_exponential_fusion.factor_ref = f32[3,6,8]{2,1,0:T(8,128)} fusion(s32[3,6,8]{2,1,0:T(8,128)} %param.11), kind=kLoop, calls=%fused_computation.15 | loop fusion | flops 288 | bytes 1152 | tf_op jit(solution)/shard_map/exp2 | solution.py:264
  22.8 6.5 %scale.1.w_ref = bf16[3,768,1024]{2,1,0:T(8,128)(2,1)} custom-call(f32[3,6,8]{2,1,0:T(8,128)} %multiply_exponential_fusion.factor_ref, bf16[3,768,1024]{2,1,0:T(8,128)(2,1)} %w_ref.1), custom_call_target="tpu_custom_call" | custom-call | tf_op jit(solution)/shard_map/scale/pallas_call | solution.py:100
  29.3 0.7 copy-done.5
  30.0 4.3 %forward.1 = (bf16[2,96,768]{2,1,0:T(8,128)(2,1)}, bf16[3,96,512]{2,1,0:T(8,128)(2,1)}, bf16[3,96,512]{2,1,0:T(8,128)(2,1)}) custom-call(s32[1]{0:T(128)} %bitcast.p_ref, bf16[128,768]{1,0:T(8,128)(2,1)} %copy-done.4, bf16[128,768]{1,0:T(8,128)(2,1)} %copy-done.5, bf16[3,768,1024]{2,1,0:T(8,128)(2,1)} %scale.1.w_ref), custom_call_target="tpu_custom_call" | custom-call | tf_op jit(solution)/shard_map/forward/pallas_call | solution.py:150
  34.3 0.5 collective-permute-start.7
  34.8 0.5 collective-permute-start.9
  35.3 8.6 %collective-permute-done.7 = bf16[3,96,512]{2,1,0:T(8,128)(2,1)S(1)} collective-permute-done((bf16[3,96,512]{2,1,0:T(8,128)(2,1)}, bf16[3,96,512]{2,1,0:T(8,128)(2,1)S(1)}, u32[]{:S(2)}, u32[]{:S(2)}) %collective-permute-start.7) | collective-permute-done | bytes 294944 | tf_op jit(solution)/shard_map/ppermute | solution.py:276
  43.9 1.0 %add_convert_fusion.1.a_ref = bf16[3,96,512]{2,1,0:T(8,128)(2,1)S(1)} fusion(bf16[3,96,512]{2,1,0:T(8,128)(2,1)S(1)} %collective-permute-done.7, bf16[3,96,512]{2,1,0:T(8,128)(2,1)} %get-tuple-element.18), kind=kLoop, calls=%fused_computation.1 | loop fusion | flops 589824 | bytes 884736 | tf_op jit(solution)/shard_map/convert_element_type | solution.py:254
  45.0 0.6 collective-permute-start.8
  45.5 1.0 %add_convert_fusion.b_ref = bf16[3,96,512]{2,1,0:T(8,128)(2,1)S(1)} fusion(bf16[3,96,512]{2,1,0:T(8,128)(2,1)S(1)} %collective-permute-done.9, bf16[3,96,512]{2,1,0:T(8,128)(2,1)} %get-tuple-element.19), kind=kLoop, calls=%fused_computation | loop fusion | flops 589824 | bytes 884736 | tf_op jit(solution)/shard_map/convert_element_type | solution.py:254
  46.6 0.6 collective-permute-start.10
  47.2 6.4 %collective-permute-done.8.ra_ref = bf16[3,96,512]{2,1,0:T(8,128)(2,1)S(1)} collective-permute-done((bf16[3,96,512]{2,1,0:T(8,128)(2,1)S(1)}, bf16[3,96,512]{2,1,0:T(8,128)(2,1)S(1)}, u32[]{:S(2)}, u32[]{:S(2)}) %collective-permute-start.8) | collective-permute-done | bytes 294944 | tf_op jit(solution)/shard_map/ppermute | solution.py:280
  53.6 1.3 %collective-permute-done.10.rb_ref = bf16[3,96,512]{2,1,0:T(8,128)(2,1)S(1)} collective-permute-done((bf16[3,96,512]{2,1,0:T(8,128)(2,1)S(1)}, bf16[3,96,512]{2,1,0:T(8,128)(2,1)S(1)}, u32[]{:S(2)}, u32[]{:S(2)}) %collective-permute-start.10) | collective-permute-done | bytes 294944 | tf_op jit(solution)/shard_map/ppermute | solution.py:281
  54.9 0.7 copy-done.3
  55.7 4.7 %backward.1 = (bf16[3,96,1024]{2,1,0:T(8,128)(2,1)}, bf16[64,768]{1,0:T(8,128)(2,1)}, bf16[64,768]{1,0:T(8,128)(2,1)}) custom-call(s32[1]{0:T(128)} %bitcast.p_ref, bf16[3,96,512]{2,1,0:T(8,128)(2,1)} %copy-done, bf16[3,96,512]{2,1,0:T(8,128)(2,1)} %copy-done.2, bf16[3,96,512]{2,1,0:T(8,128)(2,1)} %copy-done.1, bf16[3,96,512]{2,1,0:T(8,128)(2,1)} %copy-done.3, ...), custom_call_target="tpu_custom_call" | custom-call | tf_op jit(solution)/shard_map/backward/pallas_call | solution.py:199
  60.4 0.0 collective-permute-start.11
  60.4 1.5 %collective-permute-done.11 = bf16[64,768]{1,0:T(8,128)(2,1)S(1)} collective-permute-done((bf16[64,768]{1,0:T(8,128)(2,1)}, bf16[64,768]{1,0:T(8,128)(2,1)S(1)}, u32[]{:S(2)}, u32[]{:S(2)}) %collective-permute-start.11) | collective-permute-done | bytes 98336 | tf_op jit(solution)/shard_map/ppermute | solution.py:284
  61.9 0.9 %add_convert_fusion.2 = bf16[64,768]{1,0:T(8,128)(2,1)S(1)} fusion(bf16[64,768]{1,0:T(8,128)(2,1)S(1)} %collective-permute-done.11, bf16[64,768]{1,0:T(8,128)(2,1)} %get-tuple-element.20), kind=kLoop, calls=%fused_computation.2 | loop fusion | flops 196608 | bytes 294912 | tf_op jit(solution)/shard_map/convert_element_type | solution.py:254
  62.8 0.3 collective-permute-start.12
  63.2 1.3 %collective-permute-start.14 = (bf16[16,768]{1,0:T(8,128)(2,1)S(1)}, bf16[16,768]{1,0:T(8,128)(2,1)S(1)}, u32[]{:S(2)}, u32[]{:S(2)}) collective-permute-start(bf16[16,768]{1,0:T(8,128)(2,1)S(1)} %get-tuple-element.25), channel_id=1, source_target_pairs={{0,6},{1,7},{2,4},{3,5},{4,2},{5,3},{6,0},{7,1},{8,14},{9,15},{10,... | collective-permute-start | bytes 73736 | tf_op jit(solution)/shard_map/ppermute | solution.py:288
  64.4 2.0 %collective-permute-start.13 = (bf16[16,768]{1,0:T(8,128)(2,1)S(1)}, bf16[16,768]{1,0:T(8,128)(2,1)S(1)}, u32[]{:S(2)}, u32[]{:S(2)}) collective-permute-start(bf16[16,768]{1,0:T(8,128)(2,1)S(1)} %get-tuple-element.26), channel_id=1, source_target_pairs={{0,4},{1,5},{2,6},{3,7},{4,0},{5,1},{6,2},{7,3},{8,12},{9,13},{10,... | collective-permute-start | bytes 73736 | tf_op jit(solution)/shard_map/ppermute | solution.py:288
  66.4 0.3 collective-permute-done.12
  66.7 2.1 %collective-permute-done.14 = bf16[16,768]{1,0:T(8,128)(2,1)S(1)} collective-permute-done((bf16[16,768]{1,0:T(8,128)(2,1)S(1)}, bf16[16,768]{1,0:T(8,128)(2,1)S(1)}, u32[]{:S(2)}, u32[]{:S(2)}) %collective-permute-start.14) | collective-permute-done | bytes 24608 | tf_op jit(solution)/shard_map/ppermute | solution.py:288
  68.8 0.4 collective-permute-done.13
  69.2 0.6 fusion.1
  69.8 1.5 %collective-permute-start.17 = (bf16[4,768]{1,0:T(4,128)(2,1)S(1)}, bf16[4,768]{1,0:T(4,128)(2,1)S(1)}, u32[]{:S(2)}, u32[]{:S(2)}) collective-permute-start(bf16[4,768]{1,0:T(4,128)(2,1)S(1)} %get-tuple-element.27), channel_id=1, source_target_pairs={{0,24},{8,16},{16,8},{24,0},{1,25},{9,17},{17,9},{25,1},{2,26},{10... | collective-permute-start | bytes 18440 | tf_op jit(solution)/shard_map/ppermute | solution.py:291
  71.3 0.5 collective-permute-start.16
  71.8 1.5 %collective-permute-start.15 = (bf16[4,768]{1,0:T(4,128)(2,1)S(1)}, bf16[4,768]{1,0:T(4,128)(2,1)S(1)}, u32[]{:S(2)}, u32[]{:S(2)}) collective-permute-start(bf16[4,768]{1,0:T(4,128)(2,1)S(1)} %get-tuple-element.29), channel_id=1, source_target_pairs={{0,8},{8,0},{16,24},{24,16},{1,9},{9,1},{17,25},{25,17},{2,10},{10... | collective-permute-start | bytes 18440 | tf_op jit(solution)/shard_map/ppermute | solution.py:291
  73.3 8.0 %weight_grad.1 = f32[3,768,1024]{2,1,0:T(8,128)} custom-call(bf16[2,96,768]{2,1,0:T(8,128)(2,1)} %get-tuple-element.22.x_ref, bf16[3,96,1024]{2,1,0:T(8,128)(2,1)} %get-tuple-element.23.g_ref), custom_call_target="tpu_custom_call" | custom-call | tf_op jit(solution)/shard_map/weight_grad/pallas_call | solution.py:217
  81.3 0.6 copy-done.6
  81.9 0.0 copy-done.7
  81.9 0.0 copy-done.8
  81.9 1.6 %place.1 = bf16[12,3072]{1,0:T(8,128)(2,1)} custom-call(s32[1]{0:T(128)} %bitcast.p_ref, f32[8,12]{1,0:T(8,128)} %get-tuple-element.13.hit_ref, bf16[4,768]{1,0:T(4,128)(2,1)} %get-tuple-element.30.refs_0_, bf16[4,768]{1,0:T(4,128)(2,1)} %copy-done.8, bf16[4,768]{1,0:T(4,128)(2,1)} %copy-done.7, bf16[4,768]{1,0:T(4,128)(2,1)} %copy-done.6), custom_call_target="tpu_custom_call" | custom-call | tf_op jit(solution)/shard_map/place/pallas_call | solution.py:243
  (26 shorter events, 0.1 us)
Async XLA Ops:
  2.5 5.2 %collective-permute-start = (bf16[8,768]{1,0:T(8,128)(2,1)}, bf16[8,768]{1,0:T(8,128)(2,1)S(1)}, u32[]{:S(2)}, u32[]{:S(2)}) collective-permute-start(bf16[8,768]{1,0:T(8,128)(2,1)} %get-tuple-element.15), channel_id=1, source_target_pairs={{0,8},{8,0},{16,24},{24,16},{1,9},{9,1},{17,25},{25,17},{2,10},{10... | collective-permute-start | bytes 36872 | tf_op jit(solution)/shard_map/ppermute | solution.py:267
  5.5 3.9 %collective-permute-start.1 = (bf16[8,768]{1,0:T(8,128)(2,1)}, bf16[8,768]{1,0:T(8,128)(2,1)S(1)}, u32[]{:S(2)}, u32[]{:S(2)}) collective-permute-start(bf16[8,768]{1,0:T(8,128)(2,1)} %get-tuple-element.16), channel_id=1, source_target_pairs={{0,16},{8,24},{16,0},{24,8},{1,17},{9,25},{17,1},{25,9},{2,18},{10... | collective-permute-start | bytes 36872 | tf_op jit(solution)/shard_map/ppermute | solution.py:267
  7.0 4.8 %collective-permute-start.2 = (bf16[8,768]{1,0:T(8,128)(2,1)}, bf16[8,768]{1,0:T(8,128)(2,1)S(1)}, u32[]{:S(2)}, u32[]{:S(2)}) collective-permute-start(bf16[8,768]{1,0:T(8,128)(2,1)} %get-tuple-element.17), channel_id=1, source_target_pairs={{0,24},{8,16},{16,8},{24,0},{1,25},{9,17},{17,9},{25,1},{2,26},{10... | collective-permute-start | bytes 36872 | tf_op jit(solution)/shard_map/ppermute | solution.py:267
  11.8 4.6 %collective-permute-start.3 = (bf16[32,768]{1,0:T(8,128)(2,1)S(1)}, bf16[32,768]{1,0:T(8,128)(2,1)S(1)}, u32[]{:S(2)}, u32[]{:S(2)}) collective-permute-start(bf16[32,768]{1,0:T(8,128)(2,1)S(1)} %get-tuple-element.31), channel_id=1, source_target_pairs={{0,2},{1,3},{2,0},{3,1},{4,6},{5,7},{6,4},{7,5},{8,10},{9,11},{10,... | collective-permute-start | bytes 147464 | tf_op jit(solution)/shard_map/ppermute | solution.py:271
  13.4 8.0 %collective-permute-start.5 = (bf16[32,768]{1,0:T(8,128)(2,1)S(1)}, bf16[32,768]{1,0:T(8,128)(2,1)S(1)}, u32[]{:S(2)}, u32[]{:S(2)}) collective-permute-start(bf16[32,768]{1,0:T(8,128)(2,1)S(1)} %get-tuple-element.31), channel_id=1, source_target_pairs={{0,6},{1,7},{2,4},{3,5},{4,2},{5,3},{6,0},{7,1},{8,14},{9,15},{10,... | collective-permute-start | bytes 147464 | tf_op jit(solution)/shard_map/ppermute | solution.py:271
  15.9 5.5 %collective-permute-start.4 = (bf16[32,768]{1,0:T(8,128)(2,1)S(1)}, bf16[32,768]{1,0:T(8,128)(2,1)S(1)}, u32[]{:S(2)}, u32[]{:S(2)}) collective-permute-start(bf16[32,768]{1,0:T(8,128)(2,1)S(1)} %get-tuple-element.31), channel_id=1, source_target_pairs={{0,4},{1,5},{2,6},{3,7},{4,0},{5,1},{6,2},{7,3},{8,12},{9,13},{10,... | collective-permute-start | bytes 147464 | tf_op jit(solution)/shard_map/ppermute | solution.py:271
  21.4 7.9 %copy-start.4 = (bf16[128,768]{1,0:T(8,128)(2,1)}, bf16[128,768]{1,0:T(8,128)(2,1)S(1)}, u32[]{:S(2)}) copy-start(bf16[128,768]{1,0:T(8,128)(2,1)S(1)} %constant_dynamic-update-slice_fusion.4.m0_ref) | copy-start | bytes 589828
  21.4 7.9 %collective-permute-start.6 = (bf16[128,768]{1,0:T(8,128)(2,1)S(1)}, bf16[128,768]{1,0:T(8,128)(2,1)S(1)}, u32[]{:S(2)}, u32[]{:S(2)}) collective-permute-start(bf16[128,768]{1,0:T(8,128)(2,1)S(1)} %constant_dynamic-update-slice_fusion.4.m0_ref), channel_id=1, source_target_pairs={{0,1},{1,0},{2,3},{3,2},{4,5},{5,4},{6,7},{7,6},{8,9},{9,8},{10,11... | collective-permute-start | bytes 589832 | tf_op jit(solution)/shard_map/ppermute | solution.py:274
  29.3 0.7 copy-start.5
  34.3 9.6 %collective-permute-start.7 = (bf16[3,96,512]{2,1,0:T(8,128)(2,1)}, bf16[3,96,512]{2,1,0:T(8,128)(2,1)S(1)}, u32[]{:S(2)}, u32[]{:S(2)}) collective-permute-start(bf16[3,96,512]{2,1,0:T(8,128)(2,1)} %get-tuple-element.18), channel_id=1, source_target_pairs={{0,8},{8,0},{16,24},{24,16},{1,9},{9,1},{17,25},{25,17},{2,10},{10... | collective-permute-start | bytes 884744 | tf_op jit(solution)/shard_map/ppermute | solution.py:276
  34.8 10.7 %collective-permute-start.9 = (bf16[3,96,512]{2,1,0:T(8,128)(2,1)}, bf16[3,96,512]{2,1,0:T(8,128)(2,1)S(1)}, u32[]{:S(2)}, u32[]{:S(2)}) collective-permute-start(bf16[3,96,512]{2,1,0:T(8,128)(2,1)} %get-tuple-element.19), channel_id=1, source_target_pairs={{0,16},{8,24},{16,0},{24,8},{1,17},{9,25},{17,1},{25,9},{2,18},{10... | collective-permute-start | bytes 884744 | tf_op jit(solution)/shard_map/ppermute | solution.py:277
  45.0 10.0 %copy-start = (bf16[3,96,512]{2,1,0:T(8,128)(2,1)}, bf16[3,96,512]{2,1,0:T(8,128)(2,1)S(1)}, u32[]{:S(2)}) copy-start(bf16[3,96,512]{2,1,0:T(8,128)(2,1)S(1)} %add_convert_fusion.1.a_ref) | copy-start | bytes 884740
  45.0 8.6 %collective-permute-start.8 = (bf16[3,96,512]{2,1,0:T(8,128)(2,1)S(1)}, bf16[3,96,512]{2,1,0:T(8,128)(2,1)S(1)}, u32[]{:S(2)}, u32[]{:S(2)}) collective-permute-start(bf16[3,96,512]{2,1,0:T(8,128)(2,1)S(1)} %add_convert_fusion.1.a_ref), channel_id=1, source_target_pairs={{0,16},{8,24},{16,0},{24,8},{1,17},{9,25},{17,1},{25,9},{2,18},{10... | collective-permute-start | bytes 884744 | tf_op jit(solution)/shard_map/ppermute | solution.py:280
  46.6 8.3 %copy-start.1 = (bf16[3,96,512]{2,1,0:T(8,128)(2,1)}, bf16[3,96,512]{2,1,0:T(8,128)(2,1)S(1)}, u32[]{:S(2)}) copy-start(bf16[3,96,512]{2,1,0:T(8,128)(2,1)S(1)} %add_convert_fusion.b_ref) | copy-start | bytes 884740
  46.6 8.3 %collective-permute-start.10 = (bf16[3,96,512]{2,1,0:T(8,128)(2,1)S(1)}, bf16[3,96,512]{2,1,0:T(8,128)(2,1)S(1)}, u32[]{:S(2)}, u32[]{:S(2)}) collective-permute-start(bf16[3,96,512]{2,1,0:T(8,128)(2,1)S(1)} %add_convert_fusion.b_ref), channel_id=1, source_target_pairs={{0,8},{8,0},{16,24},{24,16},{1,9},{9,1},{17,25},{25,17},{2,10},{10... | collective-permute-start | bytes 884744 | tf_op jit(solution)/shard_map/ppermute | solution.py:281
  53.6 1.3 %copy-start.2 = (bf16[3,96,512]{2,1,0:T(8,128)(2,1)}, bf16[3,96,512]{2,1,0:T(8,128)(2,1)S(1)}, u32[]{:S(2)}) copy-start(bf16[3,96,512]{2,1,0:T(8,128)(2,1)S(1)} %collective-permute-done.8.ra_ref) | copy-start | bytes 884740
  54.9 0.7 copy-start.3
  60.4 1.5 %collective-permute-start.11 = (bf16[64,768]{1,0:T(8,128)(2,1)}, bf16[64,768]{1,0:T(8,128)(2,1)S(1)}, u32[]{:S(2)}, u32[]{:S(2)}) collective-permute-start(bf16[64,768]{1,0:T(8,128)(2,1)} %get-tuple-element.21), channel_id=1, source_target_pairs={{0,1},{1,0},{2,3},{3,2},{4,5},{5,4},{6,7},{7,6},{8,9},{9,8},{10,11... | collective-permute-start | bytes 294920 | tf_op jit(solution)/shard_map/ppermute | solution.py:284
  62.8 3.9 %collective-permute-start.12 = (bf16[16,768]{1,0:T(8,128)(2,1)S(1)}, bf16[16,768]{1,0:T(8,128)(2,1)S(1)}, u32[]{:S(2)}, u32[]{:S(2)}) collective-permute-start(bf16[16,768]{1,0:T(8,128)(2,1)S(1)} %get-tuple-element.24), channel_id=1, source_target_pairs={{0,2},{1,3},{2,0},{3,1},{4,6},{5,7},{6,4},{7,5},{8,10},{9,11},{10,... | collective-permute-start | bytes 73736 | tf_op jit(solution)/shard_map/ppermute | solution.py:288
  63.2 5.6 %collective-permute-start.14 = (bf16[16,768]{1,0:T(8,128)(2,1)S(1)}, bf16[16,768]{1,0:T(8,128)(2,1)S(1)}, u32[]{:S(2)}, u32[]{:S(2)}) collective-permute-start(bf16[16,768]{1,0:T(8,128)(2,1)S(1)} %get-tuple-element.25), channel_id=1, source_target_pairs={{0,6},{1,7},{2,4},{3,5},{4,2},{5,3},{6,0},{7,1},{8,14},{9,15},{10,... | collective-permute-start | bytes 73736 | tf_op jit(solution)/shard_map/ppermute | solution.py:288
  64.4 4.7 %collective-permute-start.13 = (bf16[16,768]{1,0:T(8,128)(2,1)S(1)}, bf16[16,768]{1,0:T(8,128)(2,1)S(1)}, u32[]{:S(2)}, u32[]{:S(2)}) collective-permute-start(bf16[16,768]{1,0:T(8,128)(2,1)S(1)} %get-tuple-element.26), channel_id=1, source_target_pairs={{0,4},{1,5},{2,6},{3,7},{4,0},{5,1},{6,2},{7,3},{8,12},{9,13},{10,... | collective-permute-start | bytes 73736 | tf_op jit(solution)/shard_map/ppermute | solution.py:288
  69.8 11.5 %collective-permute-start.17 = (bf16[4,768]{1,0:T(4,128)(2,1)S(1)}, bf16[4,768]{1,0:T(4,128)(2,1)S(1)}, u32[]{:S(2)}, u32[]{:S(2)}) collective-permute-start(bf16[4,768]{1,0:T(4,128)(2,1)S(1)} %get-tuple-element.27), channel_id=1, source_target_pairs={{0,24},{8,16},{16,8},{24,0},{1,25},{9,17},{17,9},{25,1},{2,26},{10... | collective-permute-start | bytes 18440 | tf_op jit(solution)/shard_map/ppermute | solution.py:291
  71.3 10.0 %collective-permute-start.16 = (bf16[4,768]{1,0:T(4,128)(2,1)S(1)}, bf16[4,768]{1,0:T(4,128)(2,1)S(1)}, u32[]{:S(2)}, u32[]{:S(2)}) collective-permute-start(bf16[4,768]{1,0:T(4,128)(2,1)S(1)} %get-tuple-element.28), channel_id=1, source_target_pairs={{0,16},{8,24},{16,0},{24,8},{1,17},{9,25},{17,1},{25,9},{2,18},{10... | collective-permute-start | bytes 18440 | tf_op jit(solution)/shard_map/ppermute | solution.py:291
  71.8 9.5 %collective-permute-start.15 = (bf16[4,768]{1,0:T(4,128)(2,1)S(1)}, bf16[4,768]{1,0:T(4,128)(2,1)S(1)}, u32[]{:S(2)}, u32[]{:S(2)}) collective-permute-start(bf16[4,768]{1,0:T(4,128)(2,1)S(1)} %get-tuple-element.29), channel_id=1, source_target_pairs={{0,8},{8,0},{16,24},{24,16},{1,9},{9,1},{17,25},{25,17},{2,10},{10... | collective-permute-start | bytes 18440 | tf_op jit(solution)/shard_map/ppermute | solution.py:291
  81.3 0.6 copy-start.6
  81.3 0.6 copy-start.7
  81.3 0.6 copy-start.8

commit v2 on v1

--- a/solution.py
+++ b/solution.py
@@ -10,11 +10,17 @@
 F32 = jnp.float32
 I32 = jnp.int32
 ROWS = 8
+CHUNKS = 3
 CORES = 2
+LIMIT = 20 * 1024 * 1024
 VMEM = pltpu.VMEM
 SMEM = pltpu.SMEM
 
 
+def in_hbm(x):
+    return pltpu.with_memory_space_constraint(x, pltpu.HBM)
+
+
 def log2(n):
     return n.bit_length() - 1
 
@@ -39,8 +45,15 @@
     return lax.dot_general(a, b, (((0,), (0,)), ((), ())), preferred_element_type=F32)
 
 
-def slots_kernel(p_ref, ids_ref, prob_ref, grad_ref, inp_ref, hit_ref, *refs):
-    outs, scratch = refs[:-1], refs[-1]
+def slots_kernel(p_ref, ids_hbm, prob_hbm, grad_hbm, inp_hbm, hit_ref, *refs):
+    outs = refs[:-6]
+    scratch, ids_ref, prob_ref, grad_ref, inp_ref, sem = refs[-6:]
+    pairs = ((ids_hbm, ids_ref), (prob_hbm, prob_ref), (inp_hbm, inp_ref), (grad_hbm, grad_ref))
+    copies = [pltpu.make_async_copy(u, v, sem.at[i]) for i, (u, v) in enumerate(pairs)]
+    for copy in copies:
+        copy.start()
+    for copy in copies:
+        copy.wait()
     n_dp = len(outs)
     width = outs[0].shape[1]
     tok = ids_ref.shape[1]
@@ -70,44 +83,56 @@
     width = d_model // n_dp
     return pl.pallas_call(
         slots_kernel,
-        out_shape=[jax.ShapeDtypeStruct((ROWS, tok), F32)]
-        + [jax.ShapeDtypeStruct((ROWS, width), BF16)] * n_dp,
-        in_specs=[pl.BlockSpec(memory_space=SMEM)] + [pl.BlockSpec(memory_space=VMEM)] * 4,
+        out_shape=[pltpu.VMEM((ROWS, tok), F32)] + [pltpu.VMEM((ROWS, width), BF16)] * n_dp,
+        in_specs=[pl.BlockSpec(memory_space=SMEM)] + [pl.BlockSpec(memory_space=pltpu.HBM)] * 4,
         out_specs=[pl.BlockSpec(memory_space=VMEM)] * (n_dp + 1),
-        scratch_shapes=[pltpu.VMEM((n_dp, ROWS, width), BF16)],
+        scratch_shapes=[
+            pltpu.VMEM((n_dp, ROWS, width), BF16),
+            pltpu.VMEM(ids.shape, I32),
+            pltpu.VMEM(prob.shape, F32),
+            pltpu.VMEM(grad.shape, BF16),
+            pltpu.VMEM(inp.shape, BF16),
+            pltpu.SemaphoreType.DMA((4,)),
+        ],
+        compiler_params=pltpu.CompilerParams(vmem_limit_bytes=LIMIT),
         name="slots",
-    )(p, ids, prob, grad, inp)
-
-
-def scale_kernel(factor_ref, w_ref, out_ref, *, tile):
-    a = pl.program_id(0)
-    r = pl.program_id(1)
-    _, rows, cols = w_ref.shape
-    for i in range(rows // tile):
-        for j in range(cols // tile):
-            at = (0, slice(i * tile, (i + 1) * tile), slice(j * tile, (j + 1) * tile))
-            factor = factor_ref[a, r * (rows // tile) + i, j]
-            out_ref[at] = (w_ref[at].astype(F32) * factor).astype(BF16)
+    )(p, *(in_hbm(v) for v in (ids, prob, grad, inp)))
+
+
+def scale_kernel(factor_ref, w_ref, out_ref, sem):
+    n, rows, cols = w_ref.shape
+    tile = rows // factor_ref.shape[1]
+    chunk = rows // CHUNKS if factor_ref.shape[1] % CHUNKS == 0 else rows
+    copies = []
+    for a in range(n):
+        for c in range(rows // chunk):
+            at = (a, pl.ds(c * chunk, chunk))
+            copies.append(
+                pltpu.make_async_copy(w_ref.at[at], out_ref.at[at], sem.at[len(copies)])
+            )
+    for copy in copies:
+        copy.start()
+    for step, copy in enumerate(copies):
+        a, c = divmod(step, rows // chunk)
+        copy.wait()
+        for i in range(chunk // tile):
+            for j in range(cols // tile):
+                row = c * (chunk // tile) + i
+                at = (a, slice(row * tile, (row + 1) * tile), slice(j * tile, (j + 1) * tile))
+                out_ref[at] = out_ref[at] * factor_ref[a, row, j].astype(BF16)
 
 
 def scale_weights(factor, w):
-    import functools
-
     n, rows, cols = w.shape
-    tile = rows // factor.shape[1]
-    steps = 2 if factor.shape[1] % 2 == 0 else 1
-    block = (1, rows // steps, cols)
-    return pl.pallas_call(
-        functools.partial(scale_kernel, tile=tile),
-        grid=(n, steps),
-        out_shape=jax.ShapeDtypeStruct(w.shape, BF16),
-        in_specs=[
-            pl.BlockSpec(memory_space=SMEM),
-            pl.BlockSpec(block, lambda a, r: (a, r, 0)),
-        ],
-        out_specs=pl.BlockSpec(block, lambda a, r: (a, r, 0)),
+    return pl.pallas_call(
+        scale_kernel,
+        out_shape=pltpu.VMEM(w.shape, BF16),
+        in_specs=[pl.BlockSpec(memory_space=SMEM), pl.BlockSpec(memory_space=pltpu.HBM)],
+        out_specs=pl.BlockSpec(memory_space=VMEM),
+        scratch_shapes=[pltpu.SemaphoreType.DMA((n * CHUNKS,))],
+        compiler_params=pltpu.CompilerParams(vmem_limit_bytes=LIMIT),
         name="scale",
-    )(factor, w)
+    )(factor, in_hbm(w))
 
 
 def forward_kernel(p_ref, m0_ref, m1_ref, w_ref, x_ref, a_ref, b_ref, *, n_dp, n_z):
@@ -152,6 +177,7 @@
         out_shape=[jax.ShapeDtypeStruct((2, slot_count, width), BF16), part, part],
         in_specs=[pl.BlockSpec(memory_space=SMEM)] + [pl.BlockSpec(memory_space=VMEM)] * 3,
         out_specs=[pl.BlockSpec(memory_space=VMEM)] * 3,
+        compiler_params=pltpu.CompilerParams(vmem_limit_bytes=LIMIT),
         name="forward",
     )(p, m0, m1, w)
 
@@ -201,12 +227,16 @@
         out_shape=[jax.ShapeDtypeStruct((n, slot_count, 2 * half), BF16), out, out],
         in_specs=[pl.BlockSpec(memory_space=SMEM)] + [pl.BlockSpec(memory_space=VMEM)] * 5,
         out_specs=[pl.BlockSpec(memory_space=VMEM)] * 3,
+        compiler_params=pltpu.CompilerParams(vmem_limit_bytes=LIMIT),
         name="backward",
     )(p, a, ra, b, rb, w)
 
 
 def weight_grad_kernel(x_ref, g_ref, out_ref):
-    out_ref[0] = tn(x_ref[0], g_ref[0])
+    a = pl.program_id(0)
+    tile = out_ref.shape[1]
+    at = pl.multiple_of(pl.program_id(1) * tile, 128)
+    out_ref[0] = tn(x_ref[a // 2, :, pl.ds(at, tile)], g_ref[a])
 
 
 def weight_grad(x, g):
@@ -218,11 +248,9 @@
         weight_grad_kernel,
         grid=(n, steps),
         out_shape=jax.ShapeDtypeStruct((n, width, cols), F32),
-        in_specs=[
-            pl.BlockSpec((1, slot_count, tile), lambda a, r: (a // 2, 0, r)),
-            pl.BlockSpec((1, slot_count, cols), lambda a, r: (a, 0, 0)),
-        ],
+        in_specs=[pl.BlockSpec(memory_space=VMEM)] * 2,
         out_specs=pl.BlockSpec((1, tile, cols), lambda a, r: (a, r, 0)),
+        compiler_params=pltpu.CompilerParams(vmem_limit_bytes=LIMIT),
         name="weight_grad",
     )(x, g)
 
@@ -246,6 +274,7 @@
         in_specs=[pl.BlockSpec(memory_space=SMEM)]
         + [pl.BlockSpec(memory_space=VMEM)] * (1 + len(parts)),
         out_specs=pl.BlockSpec(memory_space=VMEM),
+        compiler_params=pltpu.CompilerParams(vmem_limit_bytes=LIMIT),
         name="place",
     )(p, hit, *parts)
 

time: 84.2 us -> 64.7 us (0.77)
  Pallas kernels: 27 us -> 14.3 us
  other arithmetic: 4.33 us -> 0.92 us
  local copies, waits for them, and re-layouts: 3.34 us -> 0.05 us
    pallas_call x2, Pallas kernels: 8.34 us -> 4.58 us  [the longest x1 3.26 us: scale_weights(): pl.pallas_call(scale_kernel, out_shape=pltpu.VMEM(w.shape, BF16), in_spec...]
    pallas_call x1, Pallas kernels: 4.73 us -> 1.39 us  [backward(): pl.pallas_call(functools.partial(backward_kernel, n_dp=n_dp, n_z=n_z), ou...]
    pallas_call x1, Pallas kernels: 4.34 us -> 1.07 us  [forward(): pl.pallas_call(functools.partial(forward_kernel, n_dp=n_dp, n_z=n_z), out...]
    convert_element_type x3, other arithmetic: 3 us -> 0.18 us  [add_bf16(): return (u.astype(F32) + v.astype(F32)).astype(BF16)]
    unnamed x23 -> x5, local copies, waits for them, and re-layouts: 2.72 us -> 0.02 us
    pallas_call x1, Pallas kernels: 8.02 us -> 6.45 us  [weight_grad(): pl.pallas_call(weight_grad_kernel, grid=(n, steps), out_shape=jax.ShapeDt...]
    ppermute x1, waiting for transfers between devices: 1.34 us -> 0.38 us  [per_device_fast(): rb = lax.ppermute(b, 'dp', xor_pairs(n_dp, 1))]
  transfers between devices with their start and end apart: 18 -> 18, of which waited for: 11 -> 12; matrix products, arithmetic and copies ran while one was open for 5% -> 1% of each run, Pallas kernels for 17% -> 15%
where the time goes in v2:
time: 64.7 us; the launch traced here: 64.4 us
  waiting for transfers between devices  29.6 us (46%)
  starting transfers between devices  18.8 us (29%)
  Pallas kernels  14.3 us (22%)
  other arithmetic  0.92 us (1%)
  between operations  0.75 us (1%)
    ppermute x1, waiting for transfers between devices, per_device_fast(): ra = lax.ppermute(a, 'dp', xor_pairs(n_dp, 1))  8.36 us
    ppermute x1, waiting for transfers between devices, per_device_fast(): ra = lax.ppermute(a, 'dp', xor_pairs(n_dp, 2))  6.8 us
    pallas_call x1, Pallas kernels, weight_grad(): pl.pallas_call(weight_grad_kernel, grid=(n, steps), out_shape=jax.ShapeDt...  6.45 us
    ppermute x3, waiting for transfers between devices, per_device_fast(): lax.ppermute(mine, 'expert', xor_pairs(n_ex, k * CORES))  5.4 us
    ppermute x3, starting transfers between devices, per_device_fast(): lax.ppermute(blocks[k], 'dp', xor_pairs(n_dp, k))  4.57 us
    ppermute x3, waiting for transfers between devices, per_device_fast(): lax.ppermute(blocks[k], 'dp', xor_pairs(n_dp, k))  4.57 us
    ppermute x3, starting transfers between devices, per_device_fast(): lax.ppermute(mine, 'expert', xor_pairs(n_ex, k * CORES))  4.16 us
    ppermute x3, starting transfers between devices, per_device_fast(): lax.ppermute(total[k], 'dp', xor_pairs(n_dp, k))  3.55 us
  transfers between devices with their start and end apart: 18, of which 12 were waited for; matrix products, arithmetic and copies ran while one was open for 1% of the time, Pallas kernels for 15%

profile of v2, /device:TPU:0, one launch (start us, length us, event | category | flops | bytes accessed | tf_op | source)
XLA Modules:
  0.0 64.4 jit_solution(625792815782405663)
XLA Ops:
  0.6 1.3 %slots.1 = (f32[8,12]{1,0:T(8,128)S(1)}, bf16[8,768]{1,0:T(8,128)(2,1)S(1)}, bf16[8,768]{1,0:T(8,128)(2,1)S(1)}, bf16[8,768]{1,0:T(8,128)(2,1)S(1)}, bf16[8,768]{1,0:T(8,128)(2,1)S(1)}) custom-call(s32[1]{0:T(128)} %bitcast.p_ref, s32[2,12]{1,0:T(2,128)} %bitcast.3, f32[2,12]{1,0:T(2,128)} %bitcast.4, bf16[12,3072]{1,0:T(8,128)(2,1)} %grad_hbm.1, ...), custom_call_target="tpu_custom_call" | custom-call | tf_op jit(solution)/shard_map/slots/pallas_call | solution.py:84
  2.0 3.0 %collective-permute-start = (bf16[8,768]{1,0:T(8,128)(2,1)S(1)}, bf16[8,768]{1,0:T(8,128)(2,1)S(1)}, u32[]{:S(2)}, u32[]{:S(2)}) collective-permute-start(bf16[8,768]{1,0:T(8,128)(2,1)S(1)} %get-tuple-element.15), channel_id=1, source_target_pairs={{0,8},{8,0},{16,24},{24,16},{1,9},{9,1},{17,25},{25,17},{2,10},{10... | collective-permute-start | bytes 36872 | tf_op jit(solution)/shard_map/ppermute | solution.py:296
  5.0 1.5 %collective-permute-start.1 = (bf16[8,768]{1,0:T(8,128)(2,1)S(1)}, bf16[8,768]{1,0:T(8,128)(2,1)S(1)}, u32[]{:S(2)}, u32[]{:S(2)}) collective-permute-start(bf16[8,768]{1,0:T(8,128)(2,1)S(1)} %get-tuple-element.16), channel_id=1, source_target_pairs={{0,16},{8,24},{16,0},{24,8},{1,17},{9,25},{17,1},{25,9},{2,18},{10... | collective-permute-start | bytes 36872 | tf_op jit(solution)/shard_map/ppermute | solution.py:296
  6.5 0.0 collective-permute-start.2
  6.5 0.1 collective-permute-done
  6.7 2.0 %collective-permute-done.1 = bf16[8,768]{1,0:T(8,128)(2,1)S(1)} collective-permute-done((bf16[8,768]{1,0:T(8,128)(2,1)S(1)}, bf16[8,768]{1,0:T(8,128)(2,1)S(1)}, u32[]{:S(2)}, u32[]{:S(2)}) %collective-permute-start.1) | collective-permute-done | bytes 12320 | tf_op jit(solution)/shard_map/ppermute | solution.py:296
  8.7 2.4 %collective-permute-done.2 = bf16[8,768]{1,0:T(8,128)(2,1)S(1)} collective-permute-done((bf16[8,768]{1,0:T(8,128)(2,1)S(1)}, bf16[8,768]{1,0:T(8,128)(2,1)S(1)}, u32[]{:S(2)}, u32[]{:S(2)}) %collective-permute-start.2) | collective-permute-done | bytes 12320 | tf_op jit(solution)/shard_map/ppermute | solution.py:296
  11.1 1.6 %collective-permute-start.3 = (bf16[32,768]{1,0:T(8,128)(2,1)S(1)}, bf16[32,768]{1,0:T(8,128)(2,1)S(1)}, u32[]{:S(2)}, u32[]{:S(2)}) collective-permute-start(bf16[32,768]{1,0:T(8,128)(2,1)S(1)} %get-tuple-element.31), channel_id=1, source_target_pairs={{0,2},{1,3},{2,0},{3,1},{4,6},{5,7},{6,4},{7,5},{8,10},{9,11},{10,... | collective-permute-start | bytes 147464 | tf_op jit(solution)/shard_map/ppermute | solution.py:300
  12.7 2.5 %collective-permute-start.5 = (bf16[32,768]{1,0:T(8,128)(2,1)S(1)}, bf16[32,768]{1,0:T(8,128)(2,1)S(1)}, u32[]{:S(2)}, u32[]{:S(2)}) collective-permute-start(bf16[32,768]{1,0:T(8,128)(2,1)S(1)} %get-tuple-element.31), channel_id=1, source_target_pairs={{0,6},{1,7},{2,4},{3,5},{4,2},{5,3},{6,0},{7,1},{8,14},{9,15},{10,... | collective-permute-start | bytes 147464 | tf_op jit(solution)/shard_map/ppermute | solution.py:300
  15.2 0.1 collective-permute-start.4
  15.3 0.5 collective-permute-done.3
  15.7 4.9 %collective-permute-done.4 = bf16[32,768]{1,0:T(8,128)(2,1)S(1)} collective-permute-done((bf16[32,768]{1,0:T(8,128)(2,1)S(1)}, bf16[32,768]{1,0:T(8,128)(2,1)S(1)}, u32[]{:S(2)}, u32[]{:S(2)}) %collective-permute-start.4) | collective-permute-done | bytes 49184 | tf_op jit(solution)/shard_map/ppermute | solution.py:300
  20.7 0.0 collective-permute-done.5
  20.7 0.1 collective-permute-start.6
  20.8 0.7 %multiply_exponential_fusion.factor_ref = f32[3,6,8]{2,1,0:T(8,128)S(1)} fusion(s32[3,6,8]{2,1,0:T(8,128)} %param.11), kind=kLoop, calls=%fused_computation.15 | loop fusion | flops 288 | bytes 1152 | tf_op jit(solution)/shard_map/exp2 | solution.py:293
  21.5 3.3 %scale.1.w_ref = bf16[3,768,1024]{2,1,0:T(8,128)(2,1)S(1)} custom-call(f32[3,6,8]{2,1,0:T(8,128)S(1)} %multiply_exponential_fusion.factor_ref, bf16[3,768,1024]{2,1,0:T(8,128)(2,1)} %w_ref.1), custom_call_target="tpu_custom_call" | custom-call | tf_op jit(solution)/shard_map/scale/pallas_call | solution.py:127
  24.8 0.0 collective-permute-done.6.m1_ref
  24.8 1.1 %forward.1 = (bf16[2,96,768]{2,1,0:T(8,128)(2,1)S(1)}, bf16[3,96,512]{2,1,0:T(8,128)(2,1)S(1)}, bf16[3,96,512]{2,1,0:T(8,128)(2,1)S(1)}) custom-call(s32[1]{0:T(128)} %bitcast.p_ref, bf16[128,768]{1,0:T(8,128)(2,1)S(1)} %constant_dynamic-update-slice_fusion.4.m0_ref, bf16[128,768]{1,0:T(8,128)(2,1)S(1)} %collective-permute-done.6.m1_ref, ...), custom_call_target="tpu_custom_call" | custom-call | tf_op jit(solution)/shard_map/forward/pallas_call | solution.py:175
  25.9 0.6 collective-permute-start.7
  26.5 0.5 collective-permute-start.9
  27.0 8.4 %collective-permute-done.7 = bf16[3,96,512]{2,1,0:T(8,128)(2,1)S(1)} collective-permute-done((bf16[3,96,512]{2,1,0:T(8,128)(2,1)S(1)}, bf16[3,96,512]{2,1,0:T(8,128)(2,1)S(1)}, u32[]{:S(2)}, u32[]{:S(2)}) %collective-permute-start.7) | collective-permute-done | bytes 294944 | tf_op jit(solution)/shard_map/ppermute | solution.py:305
  35.3 0.1 add_convert_fusion.1.a_ref
  35.4 0.6 collective-permute-start.8
  36.0 0.0 collective-permute-done.9
  36.0 0.1 add_convert_fusion.b_ref
  36.1 1.2 %collective-permute-start.10 = (bf16[3,96,512]{2,1,0:T(8,128)(2,1)S(1)}, bf16[3,96,512]{2,1,0:T(8,128)(2,1)S(1)}, u32[]{:S(2)}, u32[]{:S(2)}) collective-permute-start(bf16[3,96,512]{2,1,0:T(8,128)(2,1)S(1)} %add_convert_fusion.b_ref), channel_id=1, source_target_pairs={{0,8},{8,0},{16,24},{24,16},{1,9},{9,1},{17,25},{25,17},{2,10},{10... | collective-permute-start | bytes 884744 | tf_op jit(solution)/shard_map/ppermute | solution.py:310
  37.2 6.8 %collective-permute-done.8.ra_ref = bf16[3,96,512]{2,1,0:T(8,128)(2,1)S(1)} collective-permute-done((bf16[3,96,512]{2,1,0:T(8,128)(2,1)S(1)}, bf16[3,96,512]{2,1,0:T(8,128)(2,1)S(1)}, u32[]{:S(2)}, u32[]{:S(2)}) %collective-permute-start.8) | collective-permute-done | bytes 294944 | tf_op jit(solution)/shard_map/ppermute | solution.py:309
  44.0 0.4 collective-permute-done.10.rb_ref
  44.4 1.4 %backward.1 = (bf16[3,96,1024]{2,1,0:T(8,128)(2,1)S(1)}, bf16[64,768]{1,0:T(8,128)(2,1)S(1)}, bf16[64,768]{1,0:T(8,128)(2,1)S(1)}) custom-call(s32[1]{0:T(128)} %bitcast.p_ref, bf16[3,96,512]{2,1,0:T(8,128)(2,1)S(1)} %add_convert_fusion.1.a_ref, bf16[3,96,512]{2,1,0:T(8,128)(2,1)S(1)} %collective-permute-done.8.ra_ref, ...), custom_call_target="tpu_custom_call" | custom-call | tf_op jit(solution)/shard_map/backward/pallas_call | solution.py:225
  45.8 0.1 collective-permute-start.11
  45.9 1.3 %collective-permute-done.11 = bf16[64,768]{1,0:T(8,128)(2,1)S(1)} collective-permute-done((bf16[64,768]{1,0:T(8,128)(2,1)S(1)}, bf16[64,768]{1,0:T(8,128)(2,1)S(1)}, u32[]{:S(2)}, u32[]{:S(2)}) %collective-permute-start.11) | collective-permute-done | bytes 98336 | tf_op jit(solution)/shard_map/ppermute | solution.py:313
  47.2 0.3 collective-permute-start.12
  47.5 1.3 %collective-permute-start.14 = (bf16[16,768]{1,0:T(8,128)(2,1)S(1)}, bf16[16,768]{1,0:T(8,128)(2,1)S(1)}, u32[]{:S(2)}, u32[]{:S(2)}) collective-permute-start(bf16[16,768]{1,0:T(8,128)(2,1)S(1)} %get-tuple-element.25), channel_id=1, source_target_pairs={{0,6},{1,7},{2,4},{3,5},{4,2},{5,3},{6,0},{7,1},{8,14},{9,15},{10,... | collective-permute-start | bytes 73736 | tf_op jit(solution)/shard_map/ppermute | solution.py:317
  48.8 2.0 %collective-permute-start.13 = (bf16[16,768]{1,0:T(8,128)(2,1)S(1)}, bf16[16,768]{1,0:T(8,128)(2,1)S(1)}, u32[]{:S(2)}, u32[]{:S(2)}) collective-permute-start(bf16[16,768]{1,0:T(8,128)(2,1)S(1)} %get-tuple-element.26), channel_id=1, source_target_pairs={{0,4},{1,5},{2,6},{3,7},{4,0},{5,1},{6,2},{7,3},{8,12},{9,13},{10,... | collective-permute-start | bytes 73736 | tf_op jit(solution)/shard_map/ppermute | solution.py:317
  50.8 0.3 collective-permute-done.12
  51.1 2.0 %collective-permute-done.14 = bf16[16,768]{1,0:T(8,128)(2,1)S(1)} collective-permute-done((bf16[16,768]{1,0:T(8,128)(2,1)S(1)}, bf16[16,768]{1,0:T(8,128)(2,1)S(1)}, u32[]{:S(2)}, u32[]{:S(2)}) %collective-permute-start.14) | collective-permute-done | bytes 24608 | tf_op jit(solution)/shard_map/ppermute | solution.py:317
  53.2 0.4 collective-permute-done.13
  53.6 1.6 %collective-permute-start.17 = (bf16[4,768]{1,0:T(4,128)(2,1)S(1)}, bf16[4,768]{1,0:T(4,128)(2,1)S(1)}, u32[]{:S(2)}, u32[]{:S(2)}) collective-permute-start(bf16[4,768]{1,0:T(4,128)(2,1)S(1)} %get-tuple-element.27), channel_id=1, source_target_pairs={{0,24},{8,16},{16,8},{24,0},{1,25},{9,17},{17,9},{25,1},{2,26},{10... | collective-permute-start | bytes 18440 | tf_op jit(solution)/shard_map/ppermute | solution.py:320
  55.1 1.1 %collective-permute-start.16 = (bf16[4,768]{1,0:T(4,128)(2,1)S(1)}, bf16[4,768]{1,0:T(4,128)(2,1)S(1)}, u32[]{:S(2)}, u32[]{:S(2)}) collective-permute-start(bf16[4,768]{1,0:T(4,128)(2,1)S(1)} %get-tuple-element.28), channel_id=1, source_target_pairs={{0,16},{8,24},{16,0},{24,8},{1,17},{9,25},{17,1},{25,9},{2,18},{10... | collective-permute-start | bytes 18440 | tf_op jit(solution)/shard_map/ppermute | solution.py:320
  56.2 0.9 %collective-permute-start.15 = (bf16[4,768]{1,0:T(4,128)(2,1)S(1)}, bf16[4,768]{1,0:T(4,128)(2,1)S(1)}, u32[]{:S(2)}, u32[]{:S(2)}) collective-permute-start(bf16[4,768]{1,0:T(4,128)(2,1)S(1)} %get-tuple-element.29), channel_id=1, source_target_pairs={{0,8},{8,0},{16,24},{24,16},{1,9},{9,1},{17,25},{25,17},{2,10},{10... | collective-permute-start | bytes 18440 | tf_op jit(solution)/shard_map/ppermute | solution.py:320
  57.1 6.4 %weight_grad.1 = f32[3,768,1024]{2,1,0:T(8,128)} custom-call(bf16[2,96,768]{2,1,0:T(8,128)(2,1)S(1)} %get-tuple-element.22.x_ref, bf16[3,96,1024]{2,1,0:T(8,128)(2,1)S(1)} %get-tuple-element.23.g_ref), custom_call_target="tpu_custom_call" | custom-call | tf_op jit(solution)/shard_map/weight_grad/pallas_call | solution.py:247
  63.6 0.0 collective-permute-done.17.refs_3_
  63.6 0.0 collective-permute-done.16.refs_2_
  63.6 0.0 collective-permute-done.15.refs_1_
  63.6 0.8 %place.1 = bf16[12,3072]{1,0:T(8,128)(2,1)} custom-call(s32[1]{0:T(128)} %bitcast.p_ref, f32[8,12]{1,0:T(8,128)S(1)} %get-tuple-element.13.hit_ref, bf16[4,768]{1,0:T(4,128)(2,1)S(1)} %get-tuple-element.30.refs_0_, bf16[4,768]{1,0:T(4,128)(2,1)S(1)} %collective-permute-done.15.refs_1_, bf16[4,768]{1,0:T(4,128)(2,1)S(1)} %collective-permute-done.16.refs_2_, ...), custom_call_target="tpu_custom_call" | custom-call | tf_op jit(solution)/shard_map/place/pallas_call | solution.py:271
  (11 shorter events, 0.1 us)
Async XLA Ops:
  2.0 4.7 %collective-permute-start = (bf16[8,768]{1,0:T(8,128)(2,1)S(1)}, bf16[8,768]{1,0:T(8,128)(2,1)S(1)}, u32[]{:S(2)}, u32[]{:S(2)}) collective-permute-start(bf16[8,768]{1,0:T(8,128)(2,1)S(1)} %get-tuple-element.15), channel_id=1, source_target_pairs={{0,8},{8,0},{16,24},{24,16},{1,9},{9,1},{17,25},{25,17},{2,10},{10... | collective-permute-start | bytes 36872 | tf_op jit(solution)/shard_map/ppermute | solution.py:296
  5.0 3.7 %collective-permute-start.1 = (bf16[8,768]{1,0:T(8,128)(2,1)S(1)}, bf16[8,768]{1,0:T(8,128)(2,1)S(1)}, u32[]{:S(2)}, u32[]{:S(2)}) collective-permute-start(bf16[8,768]{1,0:T(8,128)(2,1)S(1)} %get-tuple-element.16), channel_id=1, source_target_pairs={{0,16},{8,24},{16,0},{24,8},{1,17},{9,25},{17,1},{25,9},{2,18},{10... | collective-permute-start | bytes 36872 | tf_op jit(solution)/shard_map/ppermute | solution.py:296
  6.5 4.6 %collective-permute-start.2 = (bf16[8,768]{1,0:T(8,128)(2,1)S(1)}, bf16[8,768]{1,0:T(8,128)(2,1)S(1)}, u32[]{:S(2)}, u32[]{:S(2)}) collective-permute-start(bf16[8,768]{1,0:T(8,128)(2,1)S(1)} %get-tuple-element.17), channel_id=1, source_target_pairs={{0,24},{8,16},{16,8},{24,0},{1,25},{9,17},{17,9},{25,1},{2,26},{10... | collective-permute-start | bytes 36872 | tf_op jit(solution)/shard_map/ppermute | solution.py:296
  11.1 4.6 %collective-permute-start.3 = (bf16[32,768]{1,0:T(8,128)(2,1)S(1)}, bf16[32,768]{1,0:T(8,128)(2,1)S(1)}, u32[]{:S(2)}, u32[]{:S(2)}) collective-permute-start(bf16[32,768]{1,0:T(8,128)(2,1)S(1)} %get-tuple-element.31), channel_id=1, source_target_pairs={{0,2},{1,3},{2,0},{3,1},{4,6},{5,7},{6,4},{7,5},{8,10},{9,11},{10,... | collective-permute-start | bytes 147464 | tf_op jit(solution)/shard_map/ppermute | solution.py:300
  12.7 8.0 %collective-permute-start.5 = (bf16[32,768]{1,0:T(8,128)(2,1)S(1)}, bf16[32,768]{1,0:T(8,128)(2,1)S(1)}, u32[]{:S(2)}, u32[]{:S(2)}) collective-permute-start(bf16[32,768]{1,0:T(8,128)(2,1)S(1)} %get-tuple-element.31), channel_id=1, source_target_pairs={{0,6},{1,7},{2,4},{3,5},{4,2},{5,3},{6,0},{7,1},{8,14},{9,15},{10,... | collective-permute-start | bytes 147464 | tf_op jit(solution)/shard_map/ppermute | solution.py:300
  15.2 5.5 %collective-permute-start.4 = (bf16[32,768]{1,0:T(8,128)(2,1)S(1)}, bf16[32,768]{1,0:T(8,128)(2,1)S(1)}, u32[]{:S(2)}, u32[]{:S(2)}) collective-permute-start(bf16[32,768]{1,0:T(8,128)(2,1)S(1)} %get-tuple-element.31), channel_id=1, source_target_pairs={{0,4},{1,5},{2,6},{3,7},{4,0},{5,1},{6,2},{7,3},{8,12},{9,13},{10,... | collective-permute-start | bytes 147464 | tf_op jit(solution)/shard_map/ppermute | solution.py:300
  20.7 4.1 %collective-permute-start.6 = (bf16[128,768]{1,0:T(8,128)(2,1)S(1)}, bf16[128,768]{1,0:T(8,128)(2,1)S(1)}, u32[]{:S(2)}, u32[]{:S(2)}) collective-permute-start(bf16[128,768]{1,0:T(8,128)(2,1)S(1)} %constant_dynamic-update-slice_fusion.4.m0_ref), channel_id=1, source_target_pairs={{0,1},{1,0},{2,3},{3,2},{4,5},{5,4},{6,7},{7,6},{8,9},{9,8},{10,11... | collective-permute-start | bytes 589832 | tf_op jit(solution)/shard_map/ppermute | solution.py:303
  25.9 9.5 %collective-permute-start.7 = (bf16[3,96,512]{2,1,0:T(8,128)(2,1)S(1)}, bf16[3,96,512]{2,1,0:T(8,128)(2,1)S(1)}, u32[]{:S(2)}, u32[]{:S(2)}) collective-permute-start(bf16[3,96,512]{2,1,0:T(8,128)(2,1)S(1)} %get-tuple-element.18), channel_id=1, source_target_pairs={{0,8},{8,0},{16,24},{24,16},{1,9},{9,1},{17,25},{25,17},{2,10},{10... | collective-permute-start | bytes 884744 | tf_op jit(solution)/shard_map/ppermute | solution.py:305
  26.5 9.5 %collective-permute-start.9 = (bf16[3,96,512]{2,1,0:T(8,128)(2,1)S(1)}, bf16[3,96,512]{2,1,0:T(8,128)(2,1)S(1)}, u32[]{:S(2)}, u32[]{:S(2)}) collective-permute-start(bf16[3,96,512]{2,1,0:T(8,128)(2,1)S(1)} %get-tuple-element.19), channel_id=1, source_target_pairs={{0,16},{8,24},{16,0},{24,8},{1,17},{9,25},{17,1},{25,9},{2,18},{10... | collective-permute-start | bytes 884744 | tf_op jit(solution)/shard_map/ppermute | solution.py:306
  35.4 8.6 %collective-permute-start.8 = (bf16[3,96,512]{2,1,0:T(8,128)(2,1)S(1)}, bf16[3,96,512]{2,1,0:T(8,128)(2,1)S(1)}, u32[]{:S(2)}, u32[]{:S(2)}) collective-permute-start(bf16[3,96,512]{2,1,0:T(8,128)(2,1)S(1)} %add_convert_fusion.1.a_ref), channel_id=1, source_target_pairs={{0,16},{8,24},{16,0},{24,8},{1,17},{9,25},{17,1},{25,9},{2,18},{10... | collective-permute-start | bytes 884744 | tf_op jit(solution)/shard_map/ppermute | solution.py:309
  36.1 8.3 %collective-permute-start.10 = (bf16[3,96,512]{2,1,0:T(8,128)(2,1)S(1)}, bf16[3,96,512]{2,1,0:T(8,128)(2,1)S(1)}, u32[]{:S(2)}, u32[]{:S(2)}) collective-permute-start(bf16[3,96,512]{2,1,0:T(8,128)(2,1)S(1)} %add_convert_fusion.b_ref), channel_id=1, source_target_pairs={{0,8},{8,0},{16,24},{24,16},{1,9},{9,1},{17,25},{25,17},{2,10},{10... | collective-permute-start | bytes 884744 | tf_op jit(solution)/shard_map/ppermute | solution.py:310
  45.8 1.4 %collective-permute-start.11 = (bf16[64,768]{1,0:T(8,128)(2,1)S(1)}, bf16[64,768]{1,0:T(8,128)(2,1)S(1)}, u32[]{:S(2)}, u32[]{:S(2)}) collective-permute-start(bf16[64,768]{1,0:T(8,128)(2,1)S(1)} %get-tuple-element.21), channel_id=1, source_target_pairs={{0,1},{1,0},{2,3},{3,2},{4,5},{5,4},{6,7},{7,6},{8,9},{9,8},{10,11... | collective-permute-start | bytes 294920 | tf_op jit(solution)/shard_map/ppermute | solution.py:313
  47.2 3.9 %collective-permute-start.12 = (bf16[16,768]{1,0:T(8,128)(2,1)S(1)}, bf16[16,768]{1,0:T(8,128)(2,1)S(1)}, u32[]{:S(2)}, u32[]{:S(2)}) collective-permute-start(bf16[16,768]{1,0:T(8,128)(2,1)S(1)} %get-tuple-element.24), channel_id=1, source_target_pairs={{0,2},{1,3},{2,0},{3,1},{4,6},{5,7},{6,4},{7,5},{8,10},{9,11},{10,... | collective-permute-start | bytes 73736 | tf_op jit(solution)/shard_map/ppermute | solution.py:317
  47.5 5.6 %collective-permute-start.14 = (bf16[16,768]{1,0:T(8,128)(2,1)S(1)}, bf16[16,768]{1,0:T(8,128)(2,1)S(1)}, u32[]{:S(2)}, u32[]{:S(2)}) collective-permute-start(bf16[16,768]{1,0:T(8,128)(2,1)S(1)} %get-tuple-element.25), channel_id=1, source_target_pairs={{0,6},{1,7},{2,4},{3,5},{4,2},{5,3},{6,0},{7,1},{8,14},{9,15},{10,... | collective-permute-start | bytes 73736 | tf_op jit(solution)/shard_map/ppermute | solution.py:317
  48.8 4.7 %collective-permute-start.13 = (bf16[16,768]{1,0:T(8,128)(2,1)S(1)}, bf16[16,768]{1,0:T(8,128)(2,1)S(1)}, u32[]{:S(2)}, u32[]{:S(2)}) collective-permute-start(bf16[16,768]{1,0:T(8,128)(2,1)S(1)} %get-tuple-element.26), channel_id=1, source_target_pairs={{0,4},{1,5},{2,6},{3,7},{4,0},{5,1},{6,2},{7,3},{8,12},{9,13},{10,... | collective-permute-start | bytes 73736 | tf_op jit(solution)/shard_map/ppermute | solution.py:317
  53.6 10.0 %collective-permute-start.17 = (bf16[4,768]{1,0:T(4,128)(2,1)S(1)}, bf16[4,768]{1,0:T(4,128)(2,1)S(1)}, u32[]{:S(2)}, u32[]{:S(2)}) collective-permute-start(bf16[4,768]{1,0:T(4,128)(2,1)S(1)} %get-tuple-element.27), channel_id=1, source_target_pairs={{0,24},{8,16},{16,8},{24,0},{1,25},{9,17},{17,9},{25,1},{2,26},{10... | collective-permute-start | bytes 18440 | tf_op jit(solution)/shard_map/ppermute | solution.py:320
  55.1 8.4 %collective-permute-start.16 = (bf16[4,768]{1,0:T(4,128)(2,1)S(1)}, bf16[4,768]{1,0:T(4,128)(2,1)S(1)}, u32[]{:S(2)}, u32[]{:S(2)}) collective-permute-start(bf16[4,768]{1,0:T(4,128)(2,1)S(1)} %get-tuple-element.28), channel_id=1, source_target_pairs={{0,16},{8,24},{16,0},{24,8},{1,17},{9,25},{17,1},{25,9},{2,18},{10... | collective-permute-start | bytes 18440 | tf_op jit(solution)/shard_map/ppermute | solution.py:320
  56.2 7.4 %collective-permute-start.15 = (bf16[4,768]{1,0:T(4,128)(2,1)S(1)}, bf16[4,768]{1,0:T(4,128)(2,1)S(1)}, u32[]{:S(2)}, u32[]{:S(2)}) collective-permute-start(bf16[4,768]{1,0:T(4,128)(2,1)S(1)} %get-tuple-element.29), channel_id=1, source_target_pairs={{0,8},{8,0},{16,24},{24,16},{1,9},{9,1},{17,25},{25,17},{2,10},{10... | collective-permute-start | bytes 18440 | tf_op jit(solution)/shard_map/ppermute | solution.py:320

commit v3 on v2

--- a/solution.py
+++ b/solution.py
@@ -1,3 +1,5 @@
+import functools
+
 import jax
 import jax.numpy as jnp
 from jax import lax
@@ -5,12 +7,14 @@
 from jax.experimental.pallas import tpu as pltpu
 from jax.sharding import PartitionSpec as P
 
+
 CAP = 3
 BF16 = jnp.bfloat16
 F32 = jnp.float32
 I32 = jnp.int32
 ROWS = 8
 CHUNKS = 3
+CAPP = 4
 CORES = 2
 LIMIT = 20 * 1024 * 1024
 VMEM = pltpu.VMEM
@@ -99,10 +103,12 @@
     )(p, *(in_hbm(v) for v in (ids, prob, grad, inp)))
 
 
-def scale_kernel(factor_ref, w_ref, out_ref, sem):
+def scale_kernel(exp_hbm, w_ref, out_ref, exp_ref, sem):
+    exp_copy = pltpu.make_async_copy(exp_hbm, exp_ref, sem.at[sem.shape[0] - 1])
+    exp_copy.start()
     n, rows, cols = w_ref.shape
-    tile = rows // factor_ref.shape[1]
-    chunk = rows // CHUNKS if factor_ref.shape[1] % CHUNKS == 0 else rows
+    tile = rows // exp_ref.shape[1]
+    chunk = rows // CHUNKS if exp_ref.shape[1] % CHUNKS == 0 else rows
     copies = []
     for a in range(n):
         for c in range(rows // chunk):
@@ -112,6 +118,7 @@
             )
     for copy in copies:
         copy.start()
+    exp_copy.wait()
     for step, copy in enumerate(copies):
         a, c = divmod(step, rows // chunk)
         copy.wait()
@@ -119,26 +126,31 @@
             for j in range(cols // tile):
                 row = c * (chunk // tile) + i
                 at = (a, slice(row * tile, (row + 1) * tile), slice(j * tile, (j + 1) * tile))
-                out_ref[at] = out_ref[at] * factor_ref[a, row, j].astype(BF16)
-
-
-def scale_weights(factor, w):
-    n, rows, cols = w.shape
+                e = exp_ref[a, row, j]
+                factor = jnp.where(e > 0, 2.0, jnp.where(e < 0, 0.5, 1.0))
+                out_ref[at] = out_ref[at] * factor.astype(BF16)
+
+
+def scale_weights(exps, w):
+    n, _, _ = w.shape
     return pl.pallas_call(
         scale_kernel,
         out_shape=pltpu.VMEM(w.shape, BF16),
-        in_specs=[pl.BlockSpec(memory_space=SMEM), pl.BlockSpec(memory_space=pltpu.HBM)],
+        in_specs=[pl.BlockSpec(memory_space=pltpu.HBM)] * 2,
         out_specs=pl.BlockSpec(memory_space=VMEM),
-        scratch_shapes=[pltpu.SemaphoreType.DMA((n * CHUNKS,))],
+        scratch_shapes=[
+            pltpu.SMEM(exps.shape, I32),
+            pltpu.SemaphoreType.DMA((n * CHUNKS + 1,)),
+        ],
         compiler_params=pltpu.CompilerParams(vmem_limit_bytes=LIMIT),
         name="scale",
-    )(factor, in_hbm(w))
-
-
-def forward_kernel(p_ref, m0_ref, m1_ref, w_ref, x_ref, a_ref, b_ref, *, n_dp, n_z):
+    )(in_hbm(exps), in_hbm(w))
+
+
+def forward_kernel(p_ref, m_ref, w_ref, x_ref, a_ref, b_ref, *, n_dp):
     slot_count = x_ref.shape[1]
     group = slot_count // n_dp
-    span = m0_ref.shape[0]
+    span = m_ref.shape[0]
     p = p_ref[0]
     col = lax.broadcasted_iota(I32, (1, span), 1)
     r = col & (ROWS - 1)
@@ -147,14 +159,10 @@
     line = lax.broadcasted_iota(I32, (slot_count, span), 0)
 
     def pick(low):
-        total = None
-        for ck, m_ref in enumerate((m0_ref, m1_ref)):
-            slot = (p ^ pk) * group + (ck * n_z + zk) * CAP + (r - low)
-            slot = jnp.where((r >= low) & (r < low + CAP), slot, -1)
-            sel = jnp.where(line == slot, 1.0, 0.0).astype(BF16)
-            part = nn(sel, m_ref[...])
-            total = part if total is None else total + part
-        return total.astype(BF16)
+        slot = (p ^ pk) * group + zk * CAP + (r - low)
+        slot = jnp.where((r >= low) & (r < low + CAP), slot, -1)
+        sel = jnp.where(line == slot, 1.0, 0.0).astype(BF16)
+        return nn(sel, m_ref[...]).astype(BF16)
 
     x = pick(0)
     g = pick(CAP)
@@ -166,23 +174,21 @@
         b_ref[i] = nn(left, w_ref[i, :, half:]).astype(BF16)
 
 
-def forward(p, m0, m1, w, n_dp, n_z):
-    import functools
-
-    slot_count = n_dp * CORES * n_z * CAP
+def forward(p, m, w, n_dp, n_z):
+    slot_count = n_dp * n_z * CAP
     n, width, cols = w.shape
-    part = jax.ShapeDtypeStruct((n, slot_count, cols // 2), BF16)
-    return pl.pallas_call(
-        functools.partial(forward_kernel, n_dp=n_dp, n_z=n_z),
-        out_shape=[jax.ShapeDtypeStruct((2, slot_count, width), BF16), part, part],
-        in_specs=[pl.BlockSpec(memory_space=SMEM)] + [pl.BlockSpec(memory_space=VMEM)] * 3,
+    part = pltpu.VMEM((n, slot_count, cols // 2), BF16)
+    return pl.pallas_call(
+        functools.partial(forward_kernel, n_dp=n_dp),
+        out_shape=[pltpu.VMEM((2, slot_count, width), BF16), part, part],
+        in_specs=[pl.BlockSpec(memory_space=SMEM)] + [pl.BlockSpec(memory_space=VMEM)] * 2,
         out_specs=[pl.BlockSpec(memory_space=VMEM)] * 3,
         compiler_params=pltpu.CompilerParams(vmem_limit_bytes=LIMIT),
         name="forward",
-    )(p, m0, m1, w)
-
-
-def backward_kernel(p_ref, a_ref, ra_ref, b_ref, rb_ref, w_ref, g_ref, keep_ref, send_ref, *, n_dp, n_z):
+    )(p, m, w)
+
+
+def backward_kernel(p_ref, a_ref, ra_ref, b_ref, rb_ref, w_ref, g_ref, out_ref, *, n_dp, n_z):
     slot_count = g_ref.shape[1]
     group = slot_count // n_dp
     half = a_ref.shape[2]
@@ -203,56 +209,71 @@
         back = part if back is None else back + part
     back = back.astype(BF16)
     p = p_ref[0]
-    rows = keep_ref.shape[0]
+    rows = out_ref.shape[0]
     capp = rows // (n_z * n_dp)
-    for ck, out_ref in enumerate((keep_ref, send_ref)):
-        o = lax.broadcasted_iota(I32, (rows, slot_count), 0)
-        c = o & (capp - 1)
-        pk = (o >> log2(capp)) & (n_dp - 1)
-        zk = o >> (log2(capp) + log2(n_dp))
-        slot = (p ^ pk) * group + (ck * n_z + zk) * CAP + c
-        hit = (lax.broadcasted_iota(I32, (rows, slot_count), 1) == slot) & (c < CAP)
-        out_ref[...] = nn(jnp.where(hit, 1.0, 0.0).astype(BF16), back).astype(BF16)
+    o = lax.broadcasted_iota(I32, (rows, slot_count), 0)
+    c = o & (capp - 1)
+    pk = (o >> log2(capp)) & (n_dp - 1)
+    zk = o >> (log2(capp) + log2(n_dp))
+    slot = (p ^ pk) * group + zk * CAP + c
+    hit = (lax.broadcasted_iota(I32, (rows, slot_count), 1) == slot) & (c < CAP)
+    out_ref[...] = nn(jnp.where(hit, 1.0, 0.0).astype(BF16), back).astype(BF16)
 
 
 def backward(p, a, ra, b, rb, w, n_dp, n_z):
-    import functools
-
     n, slot_count, half = a.shape
     width = w.shape[1]
-    capp = 4
-    out = jax.ShapeDtypeStruct((n_z * n_dp * capp, width), BF16)
     return pl.pallas_call(
         functools.partial(backward_kernel, n_dp=n_dp, n_z=n_z),
-        out_shape=[jax.ShapeDtypeStruct((n, slot_count, 2 * half), BF16), out, out],
+        out_shape=[
+            pltpu.VMEM((n, slot_count, 2 * half), BF16),
+            pltpu.VMEM((n_z * n_dp * CAPP, width), BF16),
+        ],
         in_specs=[pl.BlockSpec(memory_space=SMEM)] + [pl.BlockSpec(memory_space=VMEM)] * 5,
-        out_specs=[pl.BlockSpec(memory_space=VMEM)] * 3,
+        out_specs=[pl.BlockSpec(memory_space=VMEM)] * 2,
         compiler_params=pltpu.CompilerParams(vmem_limit_bytes=LIMIT),
         name="backward",
     )(p, a, ra, b, rb, w)
 
 
-def weight_grad_kernel(x_ref, g_ref, out_ref):
-    a = pl.program_id(0)
-    tile = out_ref.shape[1]
-    at = pl.multiple_of(pl.program_id(1) * tile, 128)
-    out_ref[0] = tn(x_ref[a // 2, :, pl.ds(at, tile)], g_ref[a])
-
-
-def weight_grad(x, g):
-    n, slot_count, cols = g.shape
-    width = x.shape[2]
-    steps = 3 if width % (3 * 128) == 0 else 1
-    tile = width // steps
-    return pl.pallas_call(
-        weight_grad_kernel,
-        grid=(n, steps),
-        out_shape=jax.ShapeDtypeStruct((n, width, cols), F32),
-        in_specs=[pl.BlockSpec(memory_space=VMEM)] * 2,
-        out_specs=pl.BlockSpec((1, tile, cols), lambda a, r: (a, r, 0)),
+def weight_grad_kernel(*refs, planes, tile):
+    x0_ref, x1_ref, g0_ref, g1_ref = refs[:4]
+    out_ref, scratch, sem = refs[-3:]
+    width = x0_ref.shape[2]
+    copies = []
+    for a in planes:
+        x = jnp.concatenate([x0_ref[a // 2], x1_ref[a // 2]], axis=0)
+        g = jnp.concatenate([g0_ref[a], g1_ref[a]], axis=0)
+        for r in range(0, width, tile):
+            i = len(copies)
+            scratch[i] = tn(x[:, r : r + tile], g)
+            copy = pltpu.make_async_copy(scratch.at[i], out_ref.at[a, pl.ds(r, tile)], sem.at[i])
+            copy.start()
+            copies.append(copy)
+    for copy in copies:
+        copy.wait()
+
+
+def weight_grad(planes, x0, x1, g0, g1, total=None):
+    n, _, cols = g0.shape
+    width = x0.shape[2]
+    tile = width // 3 if width % (3 * 128) == 0 else width
+    steps = len(planes) * (width // tile)
+    operands = [x0, x1, g0, g1] + ([] if total is None else [total])
+    return pl.pallas_call(
+        functools.partial(weight_grad_kernel, planes=planes, tile=tile),
+        out_shape=pltpu.HBM((n, width, cols), F32),
+        in_specs=[pl.BlockSpec(memory_space=VMEM)] * 4
+        + [pl.BlockSpec(memory_space=pltpu.HBM)] * (len(operands) - 4),
+        out_specs=pl.BlockSpec(memory_space=pltpu.HBM),
+        scratch_shapes=[
+            pltpu.VMEM((steps, tile, cols), F32),
+            pltpu.SemaphoreType.DMA((steps,)),
+        ],
+        input_output_aliases={} if total is None else {4: 0},
         compiler_params=pltpu.CompilerParams(vmem_limit_bytes=LIMIT),
         name="weight_grad",
-    )(x, g)
+    )(*operands)
 
 
 def place_kernel(p_ref, hit_ref, *refs):
@@ -267,7 +288,7 @@
 
 
 def place(p, hit, parts, tok):
-    capp, width = parts[0].shape
+    _, width = parts[0].shape
     return pl.pallas_call(
         place_kernel,
         out_shape=jax.ShapeDtypeStruct((tok, width * len(parts)), BF16),
@@ -283,49 +304,58 @@
     return (u.astype(F32) + v.astype(F32)).astype(BF16)
 
 
+def shift(x, axis, k):
+    return lax.ppermute(x, axis, xor_pairs(lax.axis_size(axis), k))
+
+
 def per_device_fast(out_grad, layer_input, expert_ids, gate_prob, w_stack, scale_exps):
+    return fast_body(out_grad, layer_input, expert_ids, gate_prob, w_stack, scale_exps)
+
+
+def fast_body(out_grad, layer_input, expert_ids, gate_prob, w_stack, scale_exps):
     n_dp = lax.axis_size("dp")
-    n_ex = lax.axis_size("expert")
-    n_z = n_ex // CORES
+    n_z = lax.axis_size("expert") // CORES
     tok = out_grad.shape[0]
     p = lax.axis_index("dp").astype(I32).reshape(1)
     hit, *blocks = slots(p, expert_ids.T, gate_prob.T, out_grad, layer_input, n_dp)
-    factor = jnp.exp2(scale_exps.astype(F32))
-    w = scale_weights(factor, w_stack)
-    got = [blocks[0]] + [
-        lax.ppermute(blocks[k], "dp", xor_pairs(n_dp, k)) for k in range(1, n_dp)
-    ]
+    w = scale_weights(scale_exps, w_stack)
+    got = [blocks[0]] + [shift(blocks[k], "dp", k) for k in range(1, n_dp)]
     mine = jnp.concatenate(got, axis=0)
-    column = [mine] + [
-        lax.ppermute(mine, "expert", xor_pairs(n_ex, k * CORES)) for k in range(1, n_z)
-    ]
+    column = [mine] + [shift(mine, "expert", k * CORES) for k in range(1, n_z)]
     m0 = jnp.concatenate(column, axis=0)
-    m1 = lax.ppermute(m0, "expert", xor_pairs(n_ex, 1))
-    x, a, b = forward(p, m0, m1, w, n_dp, n_z)
-    ra = lax.ppermute(a, "dp", xor_pairs(n_dp, 1))
-    rb = lax.ppermute(b, "dp", xor_pairs(n_dp, 2))
-    a = add_bf16(a, ra)
-    b = add_bf16(b, rb)
-    ra = lax.ppermute(a, "dp", xor_pairs(n_dp, 2))
-    rb = lax.ppermute(b, "dp", xor_pairs(n_dp, 1))
-    g, keep, send = backward(p, a, ra, b, rb, w, n_dp, n_z)
-    weight_grads = weight_grad(x, g)
-    summed = add_bf16(keep, lax.ppermute(send, "expert", xor_pairs(n_ex, 1)))
+    m1 = shift(m0, "expert", 1)
+    xs, sums = [], []
+    for m in (m0, m1):
+        x, a, b = forward(p, m, w, n_dp, n_z)
+        ra = shift(a, "dp", 1)
+        rb = shift(b, "dp", 2)
+        a = add_bf16(a, ra)
+        b = add_bf16(b, rb)
+        ra = shift(a, "dp", 2)
+        rb = shift(b, "dp", 1)
+        xs.append(x)
+        sums.append((a, ra, b, rb))
+    gs, outs = [], []
+    for a, ra, b, rb in sums:
+        g, out = backward(p, a, ra, b, rb, w, n_dp, n_z)
+        gs.append(g)
+        outs.append(out)
+    weight_grads = weight_grad((0,), *xs, *gs)
+    weight_grads = weight_grad((1, 2), *xs, *gs, weight_grads)
+    summed = add_bf16(outs[0], shift(outs[1], "expert", 1))
     summed = summed.reshape(n_z, -1, summed.shape[1])
     total = summed[0].astype(F32)
     for k in range(1, n_z):
-        total = total + lax.ppermute(summed[k], "expert", xor_pairs(n_ex, k * CORES)).astype(F32)
+        total = total + shift(summed[k], "expert", k * CORES).astype(F32)
     total = total.astype(BF16).reshape(n_dp, -1, summed.shape[2])
-    parts = [total[0]] + [
-        lax.ppermute(total[k], "dp", xor_pairs(n_dp, k)) for k in range(1, n_dp)
-    ]
+    parts = [total[0]] + [shift(total[k], "dp", k) for k in range(1, n_dp)]
     input_grad = place(p, hit, parts, tok)
     return input_grad, weight_grads
 
 
 def per_device_any(out_grad, layer_input, expert_ids, gate_prob, w_stack, scale_exps):
     n_dp = lax.axis_size("dp")
-    tok, d_model = out_grad.shape
+    _, d_model = out_grad.shape
     routed = expert_ids == 0
     mask = jnp.any(routed, axis=1)
     prob = jnp.sum(jnp.where(routed, gate_prob, 0.0), axis=1)

time: 64.7 us -> 65.1 us (level)
  starting transfers between devices: 18.8 us -> 23.5 us
  waiting for transfers between devices: 29.6 us -> 26.1 us
  other arithmetic: 0.92 us -> 0.2 us
    ppermute x18 -> x22, starting transfers between devices: 18.8 us -> 23.5 us  [shift(): return lax.ppermute(x, axis, xor_pairs(lax.axis_size(axis), k))]
    ppermute x18 -> x22, waiting for transfers between devices: 29.6 us -> 26.1 us  [shift(): return lax.ppermute(x, axis, xor_pairs(lax.axis_size(axis), k))]
    pallas_call x1 -> x2, Pallas kernels: 1.39 us -> 2.42 us  [backward(): pl.pallas_call(functools.partial(backward_kernel, n_dp=n_dp, n_z=n_z), ou...]
    pallas_call x1, Pallas kernels: 3.26 us -> 2.54 us  [scale_weights(): pl.pallas_call(scale_kernel, out_shape=pltpu.VMEM(w.shape, BF16), in_spec...]
    exp2 x1 -> x0, other arithmetic: 0.72 us -> none  [per_device_fast(): factor = jnp.exp2(scale_exps.astype(F32))]
    pallas_call x2 -> x4, Pallas kernels: 7.52 us -> 7.12 us  [the longest x2 5.04 us: weight_grad(): pl.pallas_call(functools.partial(weight_grad_kernel, planes=planes, tile=...]
  transfers between devices with their start and end apart: 18 -> 22, of which waited for: 12 -> 13; matrix products, arithmetic and copies ran while one was open for 1% -> 0% of each run, Pallas kernels for 15% -> 19%
where the time goes in v3:
time: 65.1 us; the launch traced here: 64.9 us
  waiting for transfers between devices  26.1 us (40%)
  starting transfers between devices  23.5 us (36%)
  Pallas kernels  14.2 us (22%)
  between operations  0.83 us (1%)
    ppermute x22, waiting for transfers between devices, shift(): return lax.ppermute(x, axis, xor_pairs(lax.axis_size(axis), k))  26.1 us
    ppermute x22, starting transfers between devices, shift(): return lax.ppermute(x, axis, xor_pairs(lax.axis_size(axis), k))  23.5 us
    pallas_call x2, Pallas kernels, weight_grad(): pl.pallas_call(functools.partial(weight_grad_kernel, planes=planes, tile=...  5.04 us
    pallas_call x1, Pallas kernels, scale_weights(): pl.pallas_call(scale_kernel, out_shape=pltpu.VMEM(w.shape, BF16), in_spec...  2.54 us
    pallas_call x2, Pallas kernels, backward(): pl.pallas_call(functools.partial(backward_kernel, n_dp=n_dp, n_z=n_z), ou...  2.42 us
    pallas_call x2, Pallas kernels, forward(): pl.pallas_call(functools.partial(forward_kernel, n_dp=n_dp), out_shape=[p...  2.08 us
    pallas_call x1, Pallas kernels, slots(): pl.pallas_call(slots_kernel, out_shape=[pltpu.VMEM((ROWS, tok), F32)] + [...  1.32 us
  transfers between devices with their start and end apart: 22, of which 13 were waited for; matrix products, arithmetic and copies ran while one was open for 0% of the time, Pallas kernels for 19%

profile of v3, /device:TPU:0, one launch (start us, length us, event | category | flops | bytes accessed | tf_op | source)
XLA Modules:
  0.0 64.9 jit_solution(4266727636951458937)
XLA Ops:
  0.6 1.3 %slots.1 = (f32[8,12]{1,0:T(8,128)S(1)}, bf16[8,768]{1,0:T(8,128)(2,1)S(1)}, bf16[8,768]{1,0:T(8,128)(2,1)S(1)}, bf16[8,768]{1,0:T(8,128)(2,1)S(1)}, bf16[8,768]{1,0:T(8,128)(2,1)S(1)}) custom-call(s32[1]{0:T(128)} %bitcast.p_ref, s32[2,12]{1,0:T(2,128)} %bitcast.3, f32[2,12]{1,0:T(2,128)} %bitcast.4, bf16[12,3072]{1,0:T(8,128)(2,1)} %grad_hbm.1, ...), custom_call_target="tpu_custom_call" | custom-call | tf_op jit(solution)/shard_map/slots/pallas_call | solution.py:88
  2.0 3.0 %collective-permute-start = (bf16[8,768]{1,0:T(8,128)(2,1)S(1)}, bf16[8,768]{1,0:T(8,128)(2,1)S(1)}, u32[]{:S(2)}, u32[]{:S(2)}) collective-permute-start(bf16[8,768]{1,0:T(8,128)(2,1)S(1)} %get-tuple-element.19), channel_id=1, source_target_pairs={{0,8},{8,0},{16,24},{24,16},{1,9},{9,1},{17,25},{25,17},{2,10},{10... | collective-permute-start | bytes 36872 | tf_op jit(solution)/shard_map/ppermute | solution.py:308
  5.0 1.5 %collective-permute-start.1 = (bf16[8,768]{1,0:T(8,128)(2,1)S(1)}, bf16[8,768]{1,0:T(8,128)(2,1)S(1)}, u32[]{:S(2)}, u32[]{:S(2)}) collective-permute-start(bf16[8,768]{1,0:T(8,128)(2,1)S(1)} %get-tuple-element.20), channel_id=1, source_target_pairs={{0,16},{8,24},{16,0},{24,8},{1,17},{9,25},{17,1},{25,9},{2,18},{10... | collective-permute-start | bytes 36872 | tf_op jit(solution)/shard_map/ppermute | solution.py:308
  6.5 0.0 collective-permute-start.2
  6.5 0.1 collective-permute-done
  6.7 2.0 %collective-permute-done.1 = bf16[8,768]{1,0:T(8,128)(2,1)S(1)} collective-permute-done((bf16[8,768]{1,0:T(8,128)(2,1)S(1)}, bf16[8,768]{1,0:T(8,128)(2,1)S(1)}, u32[]{:S(2)}, u32[]{:S(2)}) %collective-permute-start.1) | collective-permute-done | bytes 12320 | tf_op jit(solution)/shard_map/ppermute | solution.py:308
  8.7 2.4 %collective-permute-done.2 = bf16[8,768]{1,0:T(8,128)(2,1)S(1)} collective-permute-done((bf16[8,768]{1,0:T(8,128)(2,1)S(1)}, bf16[8,768]{1,0:T(8,128)(2,1)S(1)}, u32[]{:S(2)}, u32[]{:S(2)}) %collective-permute-start.2) | collective-permute-done | bytes 12320 | tf_op jit(solution)/shard_map/ppermute | solution.py:308
  11.1 1.6 %collective-permute-start.3 = (bf16[32,768]{1,0:T(8,128)(2,1)S(1)}, bf16[32,768]{1,0:T(8,128)(2,1)S(1)}, u32[]{:S(2)}, u32[]{:S(2)}) collective-permute-start(bf16[32,768]{1,0:T(8,128)(2,1)S(1)} %get-tuple-element.39), channel_id=1, source_target_pairs={{0,2},{1,3},{2,0},{3,1},{4,6},{5,7},{6,4},{7,5},{8,10},{9,11},{10,... | collective-permute-start | bytes 147464 | tf_op jit(solution)/shard_map/ppermute | solution.py:308
  12.7 2.5 %collective-permute-start.5 = (bf16[32,768]{1,0:T(8,128)(2,1)S(1)}, bf16[32,768]{1,0:T(8,128)(2,1)S(1)}, u32[]{:S(2)}, u32[]{:S(2)}) collective-permute-start(bf16[32,768]{1,0:T(8,128)(2,1)S(1)} %get-tuple-element.39), channel_id=1, source_target_pairs={{0,6},{1,7},{2,4},{3,5},{4,2},{5,3},{6,0},{7,1},{8,14},{9,15},{10,... | collective-permute-start | bytes 147464 | tf_op jit(solution)/shard_map/ppermute | solution.py:308
  15.2 0.1 collective-permute-start.4
  15.3 0.5 collective-permute-done.3
  15.7 4.9 %collective-permute-done.4 = bf16[32,768]{1,0:T(8,128)(2,1)S(1)} collective-permute-done((bf16[32,768]{1,0:T(8,128)(2,1)S(1)}, bf16[32,768]{1,0:T(8,128)(2,1)S(1)}, u32[]{:S(2)}, u32[]{:S(2)}) %collective-permute-start.4) | collective-permute-done | bytes 49184 | tf_op jit(solution)/shard_map/ppermute | solution.py:308
  20.7 0.0 collective-permute-done.5
  20.7 0.1 collective-permute-start.10
  20.8 2.5 %scale.1.w_ref = bf16[3,768,1024]{2,1,0:T(8,128)(2,1)S(1)} custom-call(s32[3,6,8]{2,1,0:T(8,128)} %exp_hbm.1, bf16[3,768,1024]{2,1,0:T(8,128)(2,1)} %w_ref.1), custom_call_target="tpu_custom_call" | custom-call | tf_op jit(solution)/shard_map/scale/pallas_call | solution.py:136
  23.3 1.0 %forward.2 = (bf16[2,48,768]{2,1,0:T(8,128)(2,1)S(1)}, bf16[3,48,512]{2,1,0:T(8,128)(2,1)S(1)}, bf16[3,48,512]{2,1,0:T(8,128)(2,1)S(1)}) custom-call(s32[1]{0:T(128)} %bitcast.p_ref, bf16[128,768]{1,0:T(8,128)(2,1)S(1)} %constant_dynamic-update-slice_fusion.4.m_ref, bf16[3,768,1024]{2,1,0:T(8,128)(2,1)S(1)} %scale.1.w_ref), custom_call_target="tpu_custom_call" | custom-call | tf_op jit(solution)/shard_map/forward/pallas_call | solution.py:181
  24.4 0.6 collective-permute-start.6
  25.0 0.5 collective-permute-start.8
  25.5 0.0 collective-permute-done.10.m_ref
  25.5 1.0 %forward.3 = (bf16[2,48,768]{2,1,0:T(8,128)(2,1)S(1)}, bf16[3,48,512]{2,1,0:T(8,128)(2,1)S(1)}, bf16[3,48,512]{2,1,0:T(8,128)(2,1)S(1)}) custom-call(s32[1]{0:T(128)} %bitcast.p_ref, bf16[128,768]{1,0:T(8,128)(2,1)S(1)} %collective-permute-done.10.m_ref, bf16[3,768,1024]{2,1,0:T(8,128)(2,1)S(1)} %scale.1.w_ref), custom_call_target="tpu_custom_call" | custom-call | tf_op jit(solution)/shard_map/forward/pallas_call | solution.py:181
  26.5 1.6 %collective-permute-start.11 = (bf16[3,48,512]{2,1,0:T(8,128)(2,1)S(1)}, bf16[3,48,512]{2,1,0:T(8,128)(2,1)S(1)}, u32[]{:S(2)}, u32[]{:S(2)}) collective-permute-start(bf16[3,48,512]{2,1,0:T(8,128)(2,1)S(1)} %get-tuple-element.25), channel_id=1, source_target_pairs={{0,8},{8,0},{16,24},{24,16},{1,9},{9,1},{17,25},{25,17},{2,10},{10... | collective-permute-start | bytes 442376 | tf_op jit(solution)/shard_map/ppermute | solution.py:308
  28.1 3.1 %collective-permute-done.6 = bf16[3,48,512]{2,1,0:T(8,128)(2,1)S(1)} collective-permute-done((bf16[3,48,512]{2,1,0:T(8,128)(2,1)S(1)}, bf16[3,48,512]{2,1,0:T(8,128)(2,1)S(1)}, u32[]{:S(2)}, u32[]{:S(2)}) %collective-permute-start.6) | collective-permute-done | bytes 147488 | tf_op jit(solution)/shard_map/ppermute | solution.py:308
  31.2 0.6 collective-permute-start.7
  31.8 1.5 %collective-permute-start.13 = (bf16[3,48,512]{2,1,0:T(8,128)(2,1)S(1)}, bf16[3,48,512]{2,1,0:T(8,128)(2,1)S(1)}, u32[]{:S(2)}, u32[]{:S(2)}) collective-permute-start(bf16[3,48,512]{2,1,0:T(8,128)(2,1)S(1)} %get-tuple-element.26), channel_id=1, source_target_pairs={{0,16},{8,24},{16,0},{24,8},{1,17},{9,25},{17,1},{25,9},{2,18},{10... | collective-permute-start | bytes 442376 | tf_op jit(solution)/shard_map/ppermute | solution.py:308
  33.3 0.5 collective-permute-done.11
  33.9 0.6 collective-permute-start.12
  34.5 6.5 %collective-permute-done.13 = bf16[3,48,512]{2,1,0:T(8,128)(2,1)S(1)} collective-permute-done((bf16[3,48,512]{2,1,0:T(8,128)(2,1)S(1)}, bf16[3,48,512]{2,1,0:T(8,128)(2,1)S(1)}, u32[]{:S(2)}, u32[]{:S(2)}) %collective-permute-start.13) | collective-permute-done | bytes 147488 | tf_op jit(solution)/shard_map/ppermute | solution.py:308
  41.0 0.6 collective-permute-start.14
  41.6 1.5 %collective-permute-start.9 = (bf16[3,48,512]{2,1,0:T(8,128)(2,1)S(1)}, bf16[3,48,512]{2,1,0:T(8,128)(2,1)S(1)}, u32[]{:S(2)}, u32[]{:S(2)}) collective-permute-start(bf16[3,48,512]{2,1,0:T(8,128)(2,1)S(1)} %add_convert_fusion.2.b_ref), channel_id=1, source_target_pairs={{0,8},{8,0},{16,24},{24,16},{1,9},{9,1},{17,25},{25,17},{2,10},{10... | collective-permute-start | bytes 442376 | tf_op jit(solution)/shard_map/ppermute | solution.py:308
  43.2 0.0 collective-permute-done.12.ra_ref
  43.2 3.0 %collective-permute-done.14.rb_ref = bf16[3,48,512]{2,1,0:T(8,128)(2,1)S(1)} collective-permute-done((bf16[3,48,512]{2,1,0:T(8,128)(2,1)S(1)}, bf16[3,48,512]{2,1,0:T(8,128)(2,1)S(1)}, u32[]{:S(2)}, u32[]{:S(2)}) %collective-permute-start.14) | collective-permute-done | bytes 147488 | tf_op jit(solution)/shard_map/ppermute | solution.py:308
  46.2 1.2 %backward.3 = (bf16[3,48,1024]{2,1,0:T(8,128)(2,1)S(1)}, bf16[64,768]{1,0:T(8,128)(2,1)S(1)}) custom-call(s32[1]{0:T(128)} %bitcast.p_ref, bf16[3,48,512]{2,1,0:T(8,128)(2,1)S(1)} %add_convert_fusion.1.a_ref, bf16[3,48,512]{2,1,0:T(8,128)(2,1)S(1)} %collective-permute-done.12.ra_ref, bf16[3,48,512]{2,1,0:T(8,128)(2,1)S(1)} %add_convert_fusion.b_ref, ...), custom_call_target="tpu_custom_call" | custom-call | tf_op jit(solution)/shard_map/backward/pallas_call | solution.py:226
  47.4 0.1 collective-permute-start.15
  47.5 0.3 collective-permute-done.9.rb_ref
  47.8 1.2 %backward.2 = (bf16[3,48,1024]{2,1,0:T(8,128)(2,1)S(1)}, bf16[64,768]{1,0:T(8,128)(2,1)S(1)}) custom-call(s32[1]{0:T(128)} %bitcast.p_ref, bf16[3,48,512]{2,1,0:T(8,128)(2,1)S(1)} %add_convert_fusion.3.a_ref, bf16[3,48,512]{2,1,0:T(8,128)(2,1)S(1)} %collective-permute-done.7.ra_ref, bf16[3,48,512]{2,1,0:T(8,128)(2,1)S(1)} %add_convert_fusion.2.b_ref, ...), custom_call_target="tpu_custom_call" | custom-call | tf_op jit(solution)/shard_map/backward/pallas_call | solution.py:226
  49.0 0.0 collective-permute-done.15
  49.0 0.3 collective-permute-start.16
  49.4 1.3 %collective-permute-start.18 = (bf16[16,768]{1,0:T(8,128)(2,1)S(1)}, bf16[16,768]{1,0:T(8,128)(2,1)S(1)}, u32[]{:S(2)}, u32[]{:S(2)}) collective-permute-start(bf16[16,768]{1,0:T(8,128)(2,1)S(1)} %get-tuple-element.33), channel_id=1, source_target_pairs={{0,6},{1,7},{2,4},{3,5},{4,2},{5,3},{6,0},{7,1},{8,14},{9,15},{10,... | collective-permute-start | bytes 73736 | tf_op jit(solution)/shard_map/ppermute | solution.py:308
  50.6 2.0 %collective-permute-start.17 = (bf16[16,768]{1,0:T(8,128)(2,1)S(1)}, bf16[16,768]{1,0:T(8,128)(2,1)S(1)}, u32[]{:S(2)}, u32[]{:S(2)}) collective-permute-start(bf16[16,768]{1,0:T(8,128)(2,1)S(1)} %get-tuple-element.34), channel_id=1, source_target_pairs={{0,4},{1,5},{2,6},{3,7},{4,0},{5,1},{6,2},{7,3},{8,12},{9,13},{10,... | collective-permute-start | bytes 73736 | tf_op jit(solution)/shard_map/ppermute | solution.py:308
  52.6 0.3 collective-permute-done.16
  52.9 2.1 %collective-permute-done.18 = bf16[16,768]{1,0:T(8,128)(2,1)S(1)} collective-permute-done((bf16[16,768]{1,0:T(8,128)(2,1)S(1)}, bf16[16,768]{1,0:T(8,128)(2,1)S(1)}, u32[]{:S(2)}, u32[]{:S(2)}) %collective-permute-start.18) | collective-permute-done | bytes 24608 | tf_op jit(solution)/shard_map/ppermute | solution.py:308
  55.0 0.4 collective-permute-done.17
  55.4 0.5 collective-permute-start.21
  56.0 1.5 %collective-permute-start.20 = (bf16[4,768]{1,0:T(4,128)(2,1)S(1)}, bf16[4,768]{1,0:T(4,128)(2,1)S(1)}, u32[]{:S(2)}, u32[]{:S(2)}) collective-permute-start(bf16[4,768]{1,0:T(4,128)(2,1)S(1)} %get-tuple-element.36), channel_id=1, source_target_pairs={{0,16},{8,24},{16,0},{24,8},{1,17},{9,25},{17,1},{25,9},{2,18},{10... | collective-permute-start | bytes 18440 | tf_op jit(solution)/shard_map/ppermute | solution.py:308
  57.5 1.5 %collective-permute-start.19 = (bf16[4,768]{1,0:T(4,128)(2,1)S(1)}, bf16[4,768]{1,0:T(4,128)(2,1)S(1)}, u32[]{:S(2)}, u32[]{:S(2)}) collective-permute-start(bf16[4,768]{1,0:T(4,128)(2,1)S(1)} %get-tuple-element.37), channel_id=1, source_target_pairs={{0,8},{8,0},{16,24},{24,16},{1,9},{9,1},{17,25},{25,17},{2,10},{10... | collective-permute-start | bytes 18440 | tf_op jit(solution)/shard_map/ppermute | solution.py:308
  59.0 2.0 %weight_grad.2.refs_4_ = f32[3,768,1024]{2,1,0:T(8,128)} custom-call(bf16[2,48,768]{2,1,0:T(8,128)(2,1)S(1)} %get-tuple-element.28.refs_0_, bf16[2,48,768]{2,1,0:T(8,128)(2,1)S(1)} %get-tuple-element.29.refs_1_, bf16[3,48,1024]{2,1,0:T(8,128)(2,1)S(1)} %get-tuple-element.30.refs_2_, bf16[3,48,1024]{2,1,0:T(8,128)(2,1)S(1)} %get-tuple-element.31.refs_3_), custom_call_target="tpu_custom_call" | custom-call | tf_op jit(solution)/shard_map/weight_grad/pallas_call | solution.py:263
  61.0 3.0 %weight_grad.3 = f32[3,768,1024]{2,1,0:T(8,128)} custom-call(bf16[2,48,768]{2,1,0:T(8,128)(2,1)S(1)} %get-tuple-element.28.refs_0_, bf16[2,48,768]{2,1,0:T(8,128)(2,1)S(1)} %get-tuple-element.29.refs_1_, bf16[3,48,1024]{2,1,0:T(8,128)(2,1)S(1)} %get-tuple-element.30.refs_2_, ...), custom_call_target="tpu_custom_call", output_to_operand_aliasing={{}: (4, {})} | custom-call | tf_op jit(solution)/shard_map/weight_grad/pallas_call | solution.py:263
  64.1 0.8 %place.1 = bf16[12,3072]{1,0:T(8,128)(2,1)} custom-call(s32[1]{0:T(128)} %bitcast.p_ref, f32[8,12]{1,0:T(8,128)S(1)} %get-tuple-element.17.hit_ref, bf16[4,768]{1,0:T(4,128)(2,1)S(1)} %get-tuple-element.38.refs_0_, bf16[4,768]{1,0:T(4,128)(2,1)S(1)} %collective-permute-done.19.refs_1_, bf16[4,768]{1,0:T(4,128)(2,1)S(1)} %collective-permute-done.20.refs_2_, ...), custom_call_target="tpu_custom_call" | custom-call | tf_op jit(solution)/shard_map/place/pallas_call | solution.py:292
  (20 shorter events, 0.3 us)
Async XLA Ops:
  2.0 4.7 %collective-permute-start = (bf16[8,768]{1,0:T(8,128)(2,1)S(1)}, bf16[8,768]{1,0:T(8,128)(2,1)S(1)}, u32[]{:S(2)}, u32[]{:S(2)}) collective-permute-start(bf16[8,768]{1,0:T(8,128)(2,1)S(1)} %get-tuple-element.19), channel_id=1, source_target_pairs={{0,8},{8,0},{16,24},{24,16},{1,9},{9,1},{17,25},{25,17},{2,10},{10... | collective-permute-start | bytes 36872 | tf_op jit(solution)/shard_map/ppermute | solution.py:308
  5.0 3.7 %collective-permute-start.1 = (bf16[8,768]{1,0:T(8,128)(2,1)S(1)}, bf16[8,768]{1,0:T(8,128)(2,1)S(1)}, u32[]{:S(2)}, u32[]{:S(2)}) collective-permute-start(bf16[8,768]{1,0:T(8,128)(2,1)S(1)} %get-tuple-element.20), channel_id=1, source_target_pairs={{0,16},{8,24},{16,0},{24,8},{1,17},{9,25},{17,1},{25,9},{2,18},{10... | collective-permute-start | bytes 36872 | tf_op jit(solution)/shard_map/ppermute | solution.py:308
  6.5 4.6 %collective-permute-start.2 = (bf16[8,768]{1,0:T(8,128)(2,1)S(1)}, bf16[8,768]{1,0:T(8,128)(2,1)S(1)}, u32[]{:S(2)}, u32[]{:S(2)}) collective-permute-start(bf16[8,768]{1,0:T(8,128)(2,1)S(1)} %get-tuple-element.21), channel_id=1, source_target_pairs={{0,24},{8,16},{16,8},{24,0},{1,25},{9,17},{17,9},{25,1},{2,26},{10... | collective-permute-start | bytes 36872 | tf_op jit(solution)/shard_map/ppermute | solution.py:308
  11.1 4.6 %collective-permute-start.3 = (bf16[32,768]{1,0:T(8,128)(2,1)S(1)}, bf16[32,768]{1,0:T(8,128)(2,1)S(1)}, u32[]{:S(2)}, u32[]{:S(2)}) collective-permute-start(bf16[32,768]{1,0:T(8,128)(2,1)S(1)} %get-tuple-element.39), channel_id=1, source_target_pairs={{0,2},{1,3},{2,0},{3,1},{4,6},{5,7},{6,4},{7,5},{8,10},{9,11},{10,... | collective-permute-start | bytes 147464 | tf_op jit(solution)/shard_map/ppermute | solution.py:308
  12.7 8.0 %collective-permute-start.5 = (bf16[32,768]{1,0:T(8,128)(2,1)S(1)}, bf16[32,768]{1,0:T(8,128)(2,1)S(1)}, u32[]{:S(2)}, u32[]{:S(2)}) collective-permute-start(bf16[32,768]{1,0:T(8,128)(2,1)S(1)} %get-tuple-element.39), channel_id=1, source_target_pairs={{0,6},{1,7},{2,4},{3,5},{4,2},{5,3},{6,0},{7,1},{8,14},{9,15},{10,... | collective-permute-start | bytes 147464 | tf_op jit(solution)/shard_map/ppermute | solution.py:308
  15.2 5.5 %collective-permute-start.4 = (bf16[32,768]{1,0:T(8,128)(2,1)S(1)}, bf16[32,768]{1,0:T(8,128)(2,1)S(1)}, u32[]{:S(2)}, u32[]{:S(2)}) collective-permute-start(bf16[32,768]{1,0:T(8,128)(2,1)S(1)} %get-tuple-element.39), channel_id=1, source_target_pairs={{0,4},{1,5},{2,6},{3,7},{4,0},{5,1},{6,2},{7,3},{8,12},{9,13},{10,... | collective-permute-start | bytes 147464 | tf_op jit(solution)/shard_map/ppermute | solution.py:308
  20.7 4.8 %collective-permute-start.10 = (bf16[128,768]{1,0:T(8,128)(2,1)S(1)}, bf16[128,768]{1,0:T(8,128)(2,1)S(1)}, u32[]{:S(2)}, u32[]{:S(2)}) collective-permute-start(bf16[128,768]{1,0:T(8,128)(2,1)S(1)} %constant_dynamic-update-slice_fusion.4.m_ref), channel_id=1, source_target_pairs={{0,1},{1,0},{2,3},{3,2},{4,5},{5,4},{6,7},{7,6},{8,9},{9,8},{10,11... | collective-permute-start | bytes 589832 | tf_op jit(solution)/shard_map/ppermute | solution.py:308
  24.4 6.8 %collective-permute-start.6 = (bf16[3,48,512]{2,1,0:T(8,128)(2,1)S(1)}, bf16[3,48,512]{2,1,0:T(8,128)(2,1)S(1)}, u32[]{:S(2)}, u32[]{:S(2)}) collective-permute-start(bf16[3,48,512]{2,1,0:T(8,128)(2,1)S(1)} %get-tuple-element.22), channel_id=1, source_target_pairs={{0,8},{8,0},{16,24},{24,16},{1,9},{9,1},{17,25},{25,17},{2,10},{10... | collective-permute-start | bytes 442376 | tf_op jit(solution)/shard_map/ppermute | solution.py:308
  25.0 16.6 %collective-permute-start.8 = (bf16[3,48,512]{2,1,0:T(8,128)(2,1)S(1)}, bf16[3,48,512]{2,1,0:T(8,128)(2,1)S(1)}, u32[]{:S(2)}, u32[]{:S(2)}) collective-permute-start(bf16[3,48,512]{2,1,0:T(8,128)(2,1)S(1)} %get-tuple-element.23), channel_id=1, source_target_pairs={{0,16},{8,24},{16,0},{24,8},{1,17},{9,25},{17,1},{25,9},{2,18},{10... | collective-permute-start | bytes 442376 | tf_op jit(solution)/shard_map/ppermute | solution.py:308
  26.5 7.3 %collective-permute-start.11 = (bf16[3,48,512]{2,1,0:T(8,128)(2,1)S(1)}, bf16[3,48,512]{2,1,0:T(8,128)(2,1)S(1)}, u32[]{:S(2)}, u32[]{:S(2)}) collective-permute-start(bf16[3,48,512]{2,1,0:T(8,128)(2,1)S(1)} %get-tuple-element.25), channel_id=1, source_target_pairs={{0,8},{8,0},{16,24},{24,16},{1,9},{9,1},{17,25},{25,17},{2,10},{10... | collective-permute-start | bytes 442376 | tf_op jit(solution)/shard_map/ppermute | solution.py:308
  31.2 16.3 %collective-permute-start.7 = (bf16[3,48,512]{2,1,0:T(8,128)(2,1)S(1)}, bf16[3,48,512]{2,1,0:T(8,128)(2,1)S(1)}, u32[]{:S(2)}, u32[]{:S(2)}) collective-permute-start(bf16[3,48,512]{2,1,0:T(8,128)(2,1)S(1)} %add_convert_fusion.3.a_ref), channel_id=1, source_target_pairs={{0,16},{8,24},{16,0},{24,8},{1,17},{9,25},{17,1},{25,9},{2,18},{10... | collective-permute-start | bytes 442376 | tf_op jit(solution)/shard_map/ppermute | solution.py:308
  31.8 9.1 %collective-permute-start.13 = (bf16[3,48,512]{2,1,0:T(8,128)(2,1)S(1)}, bf16[3,48,512]{2,1,0:T(8,128)(2,1)S(1)}, u32[]{:S(2)}, u32[]{:S(2)}) collective-permute-start(bf16[3,48,512]{2,1,0:T(8,128)(2,1)S(1)} %get-tuple-element.26), channel_id=1, source_target_pairs={{0,16},{8,24},{16,0},{24,8},{1,17},{9,25},{17,1},{25,9},{2,18},{10... | collective-permute-start | bytes 442376 | tf_op jit(solution)/shard_map/ppermute | solution.py:308
  33.9 9.3 %collective-permute-start.12 = (bf16[3,48,512]{2,1,0:T(8,128)(2,1)S(1)}, bf16[3,48,512]{2,1,0:T(8,128)(2,1)S(1)}, u32[]{:S(2)}, u32[]{:S(2)}) collective-permute-start(bf16[3,48,512]{2,1,0:T(8,128)(2,1)S(1)} %add_convert_fusion.1.a_ref), channel_id=1, source_target_pairs={{0,16},{8,24},{16,0},{24,8},{1,17},{9,25},{17,1},{25,9},{2,18},{10... | collective-permute-start | bytes 442376 | tf_op jit(solution)/shard_map/ppermute | solution.py:308
  41.0 5.2 %collective-permute-start.14 = (bf16[3,48,512]{2,1,0:T(8,128)(2,1)S(1)}, bf16[3,48,512]{2,1,0:T(8,128)(2,1)S(1)}, u32[]{:S(2)}, u32[]{:S(2)}) collective-permute-start(bf16[3,48,512]{2,1,0:T(8,128)(2,1)S(1)} %add_convert_fusion.b_ref), channel_id=1, source_target_pairs={{0,8},{8,0},{16,24},{24,16},{1,9},{9,1},{17,25},{25,17},{2,10},{10... | collective-permute-start | bytes 442376 | tf_op jit(solution)/shard_map/ppermute | solution.py:308
  41.6 6.1 %collective-permute-start.9 = (bf16[3,48,512]{2,1,0:T(8,128)(2,1)S(1)}, bf16[3,48,512]{2,1,0:T(8,128)(2,1)S(1)}, u32[]{:S(2)}, u32[]{:S(2)}) collective-permute-start(bf16[3,48,512]{2,1,0:T(8,128)(2,1)S(1)} %add_convert_fusion.2.b_ref), channel_id=1, source_target_pairs={{0,8},{8,0},{16,24},{24,16},{1,9},{9,1},{17,25},{25,17},{2,10},{10... | collective-permute-start | bytes 442376 | tf_op jit(solution)/shard_map/ppermute | solution.py:308
  47.4 1.6 %collective-permute-start.15 = (bf16[64,768]{1,0:T(8,128)(2,1)S(1)}, bf16[64,768]{1,0:T(8,128)(2,1)S(1)}, u32[]{:S(2)}, u32[]{:S(2)}) collective-permute-start(bf16[64,768]{1,0:T(8,128)(2,1)S(1)} %get-tuple-element.27), channel_id=1, source_target_pairs={{0,1},{1,0},{2,3},{3,2},{4,5},{5,4},{6,7},{7,6},{8,9},{9,8},{10,11... | collective-permute-start | bytes 294920 | tf_op jit(solution)/shard_map/ppermute | solution.py:308
  49.0 3.9 %collective-permute-start.16 = (bf16[16,768]{1,0:T(8,128)(2,1)S(1)}, bf16[16,768]{1,0:T(8,128)(2,1)S(1)}, u32[]{:S(2)}, u32[]{:S(2)}) collective-permute-start(bf16[16,768]{1,0:T(8,128)(2,1)S(1)} %get-tuple-element.32), channel_id=1, source_target_pairs={{0,2},{1,3},{2,0},{3,1},{4,6},{5,7},{6,4},{7,5},{8,10},{9,11},{10,... | collective-permute-start | bytes 73736 | tf_op jit(solution)/shard_map/ppermute | solution.py:308
  49.4 5.6 %collective-permute-start.18 = (bf16[16,768]{1,0:T(8,128)(2,1)S(1)}, bf16[16,768]{1,0:T(8,128)(2,1)S(1)}, u32[]{:S(2)}, u32[]{:S(2)}) collective-permute-start(bf16[16,768]{1,0:T(8,128)(2,1)S(1)} %get-tuple-element.33), channel_id=1, source_target_pairs={{0,6},{1,7},{2,4},{3,5},{4,2},{5,3},{6,0},{7,1},{8,14},{9,15},{10,... | collective-permute-start | bytes 73736 | tf_op jit(solution)/shard_map/ppermute | solution.py:308
  50.6 4.7 %collective-permute-start.17 = (bf16[16,768]{1,0:T(8,128)(2,1)S(1)}, bf16[16,768]{1,0:T(8,128)(2,1)S(1)}, u32[]{:S(2)}, u32[]{:S(2)}) collective-permute-start(bf16[16,768]{1,0:T(8,128)(2,1)S(1)} %get-tuple-element.34), channel_id=1, source_target_pairs={{0,4},{1,5},{2,6},{3,7},{4,0},{5,1},{6,2},{7,3},{8,12},{9,13},{10,... | collective-permute-start | bytes 73736 | tf_op jit(solution)/shard_map/ppermute | solution.py:308
  55.4 8.6 %collective-permute-start.21 = (bf16[4,768]{1,0:T(4,128)(2,1)S(1)}, bf16[4,768]{1,0:T(4,128)(2,1)S(1)}, u32[]{:S(2)}, u32[]{:S(2)}) collective-permute-start(bf16[4,768]{1,0:T(4,128)(2,1)S(1)} %get-tuple-element.35), channel_id=1, source_target_pairs={{0,24},{8,16},{16,8},{24,0},{1,25},{9,17},{17,9},{25,1},{2,26},{10... | collective-permute-start | bytes 18440 | tf_op jit(solution)/shard_map/ppermute | solution.py:308
  56.0 8.1 %collective-permute-start.20 = (bf16[4,768]{1,0:T(4,128)(2,1)S(1)}, bf16[4,768]{1,0:T(4,128)(2,1)S(1)}, u32[]{:S(2)}, u32[]{:S(2)}) collective-permute-start(bf16[4,768]{1,0:T(4,128)(2,1)S(1)} %get-tuple-element.36), channel_id=1, source_target_pairs={{0,16},{8,24},{16,0},{24,8},{1,17},{9,25},{17,1},{25,9},{2,18},{10... | collective-permute-start | bytes 18440 | tf_op jit(solution)/shard_map/ppermute | solution.py:308
  57.5 6.6 %collective-permute-start.19 = (bf16[4,768]{1,0:T(4,128)(2,1)S(1)}, bf16[4,768]{1,0:T(4,128)(2,1)S(1)}, u32[]{:S(2)}, u32[]{:S(2)}) collective-permute-start(bf16[4,768]{1,0:T(4,128)(2,1)S(1)} %get-tuple-element.37), channel_id=1, source_target_pairs={{0,8},{8,0},{16,24},{24,16},{1,9},{9,1},{17,25},{25,17},{2,10},{10... | collective-permute-start | bytes 18440 | tf_op jit(solution)/shard_map/ppermute | solution.py:308

commit v4 on v3

--- a/solution.py
+++ b/solution.py
@@ -49,7 +49,7 @@
     return lax.dot_general(a, b, (((0,), (0,)), ((), ())), preferred_element_type=F32)
 
 
-def slots_kernel(p_ref, ids_hbm, prob_hbm, grad_hbm, inp_hbm, hit_ref, *refs):
+def slots_kernel(p_ref, e_ref, ids_hbm, prob_hbm, grad_hbm, inp_hbm, hit_ref, *refs):
     outs = refs[:-6]
     scratch, ids_ref, prob_ref, grad_ref, inp_ref, sem = refs[-6:]
     pairs = ((ids_hbm, ids_ref), (prob_hbm, prob_ref), (inp_hbm, inp_ref), (grad_hbm, grad_ref))
@@ -82,13 +82,13 @@
         outs[k][...] = scratch[p ^ k]
 
 
-def slots(p, ids, prob, grad, inp, n_dp):
+def slots(p, e, ids, prob, grad, inp, n_dp):
     tok, d_model = inp.shape
     width = d_model // n_dp
     return pl.pallas_call(
         slots_kernel,
         out_shape=[pltpu.VMEM((ROWS, tok), F32)] + [pltpu.VMEM((ROWS, width), BF16)] * n_dp,
-        in_specs=[pl.BlockSpec(memory_space=SMEM)] + [pl.BlockSpec(memory_space=pltpu.HBM)] * 4,
+        in_specs=[pl.BlockSpec(memory_space=SMEM)] * 2 + [pl.BlockSpec(memory_space=pltpu.HBM)] * 4,
         out_specs=[pl.BlockSpec(memory_space=VMEM)] * (n_dp + 1),
         scratch_shapes=[
             pltpu.VMEM((n_dp, ROWS, width), BF16),
@@ -100,7 +100,7 @@
         ],
         compiler_params=pltpu.CompilerParams(vmem_limit_bytes=LIMIT),
         name="slots",
-    )(p, *(in_hbm(v) for v in (ids, prob, grad, inp)))
+    )(p, e, *(in_hbm(v) for v in (ids, prob, grad, inp)))
 
 
 def scale_kernel(exp_hbm, w_ref, out_ref, exp_ref, sem):
@@ -188,7 +188,9 @@
     )(p, m, w)
 
 
-def backward_kernel(p_ref, a_ref, ra_ref, b_ref, rb_ref, w_ref, g_ref, out_ref, *, n_dp, n_z):
+def backward_kernel(e_ref, a_ref, ra_ref, b_ref, rb_ref, w_ref, *refs, n_dp):
+    g_ref, out_ref = refs[-2:]
+    before_ref = refs[0] if len(refs) == 3 else None
     slot_count = g_ref.shape[1]
     group = slot_count // n_dp
     half = a_ref.shape[2]
@@ -208,32 +210,37 @@
         part = nt(gate_grad, w_ref[0, :, at]) + nt(up_grad, w_ref[1, :, at])
         back = part if back is None else back + part
     back = back.astype(BF16)
-    p = p_ref[0]
-    rows = out_ref.shape[0]
-    capp = rows // (n_z * n_dp)
-    o = lax.broadcasted_iota(I32, (rows, slot_count), 0)
+    if before_ref is None:
+        out_ref[...] = back
+        return
+    count, capp, _ = out_ref.shape
+    n_ex = count // n_dp
+    both = jnp.concatenate([before_ref[...], back], axis=0)
+    o = lax.broadcasted_iota(I32, (count * capp, 1), 0)
     c = o & (capp - 1)
-    pk = (o >> log2(capp)) & (n_dp - 1)
-    zk = o >> (log2(capp) + log2(n_dp))
-    slot = (p ^ pk) * group + zk * CAP + c
-    hit = (lax.broadcasted_iota(I32, (rows, slot_count), 1) == slot) & (c < CAP)
-    out_ref[...] = nn(jnp.where(hit, 1.0, 0.0).astype(BF16), back).astype(BF16)
-
-
-def backward(p, a, ra, b, rb, w, n_dp, n_z):
+    ex = ((o >> log2(capp)) & (n_ex - 1)) ^ e_ref[0]
+    pa = o >> (log2(capp) + log2(n_ex))
+    slot = (ex & 1) * slot_count + pa * group + (ex >> 1) * CAP + c
+    slot = jnp.where(c < CAP, slot, -1)
+    hit = lax.broadcasted_iota(I32, (count * capp, CORES * slot_count), 1) == slot
+    out = nn(jnp.where(hit, 1.0, 0.0).astype(BF16), both).astype(BF16)
+    for d in range(count):
+        out_ref[d] = out[d * capp : (d + 1) * capp]
+
+
+def backward(e, a, ra, b, rb, w, n_dp, n_ex, before=()):
     n, slot_count, half = a.shape
     width = w.shape[1]
-    return pl.pallas_call(
-        functools.partial(backward_kernel, n_dp=n_dp, n_z=n_z),
-        out_shape=[
-            pltpu.VMEM((n, slot_count, 2 * half), BF16),
-            pltpu.VMEM((n_z * n_dp * CAPP, width), BF16),
-        ],
-        in_specs=[pl.BlockSpec(memory_space=SMEM)] + [pl.BlockSpec(memory_space=VMEM)] * 5,
+    shape = (n_dp * n_ex, CAPP, width) if before else (slot_count, width)
+    return pl.pallas_call(
+        functools.partial(backward_kernel, n_dp=n_dp),
+        out_shape=[pltpu.VMEM((n, slot_count, 2 * half), BF16), pltpu.VMEM(shape, BF16)],
+        in_specs=[pl.BlockSpec(memory_space=SMEM)]
+        + [pl.BlockSpec(memory_space=VMEM)] * (5 + len(before)),
         out_specs=[pl.BlockSpec(memory_space=VMEM)] * 2,
         compiler_params=pltpu.CompilerParams(vmem_limit_bytes=LIMIT),
         name="backward",
-    )(p, a, ra, b, rb, w)
+    )(e, a, ra, b, rb, w, *before)
 
 
 def weight_grad_kernel(*refs, planes, tile):
@@ -276,28 +283,27 @@
     )(*operands)
 
 
-def place_kernel(p_ref, hit_ref, *refs):
-    parts, out_ref = refs[:-1], refs[-1]
-    width = parts[0].shape[1]
-    capp = parts[0].shape[0]
-    p = p_ref[0]
+def place_kernel(hit_ref, got_ref, out_ref, *, n_dp):
+    count, capp, width = got_ref.shape
+    n_ex = count // n_dp
     hit = hit_ref[:capp, :].astype(BF16)
-    for k, part in enumerate(parts):
-        at = pl.multiple_of((p ^ k) * width, 128)
-        out_ref[:, pl.ds(at, width)] = tn(hit, part[...]).astype(BF16)
-
-
-def place(p, hit, parts, tok):
-    _, width = parts[0].shape
-    return pl.pallas_call(
-        place_kernel,
-        out_shape=jax.ShapeDtypeStruct((tok, width * len(parts)), BF16),
-        in_specs=[pl.BlockSpec(memory_space=SMEM)]
-        + [pl.BlockSpec(memory_space=VMEM)] * (1 + len(parts)),
+    for p in range(n_dp):
+        total = got_ref[p * n_ex].astype(F32)
+        for e in range(1, n_ex):
+            total = total + got_ref[p * n_ex + e].astype(F32)
+        out_ref[:, p * width : (p + 1) * width] = tn(hit, total.astype(BF16)).astype(BF16)
+
+
+def place(hit, got, tok, n_dp):
+    width = got.shape[2]
+    return pl.pallas_call(
+        functools.partial(place_kernel, n_dp=n_dp),
+        out_shape=jax.ShapeDtypeStruct((tok, width * n_dp), BF16),
+        in_specs=[pl.BlockSpec(memory_space=VMEM)] * 2,
         out_specs=pl.BlockSpec(memory_space=VMEM),
         compiler_params=pltpu.CompilerParams(vmem_limit_bytes=LIMIT),
         name="place",
-    )(p, hit, *parts)
+    )(hit, got)
 
 
 def add_bf16(u, v):
@@ -314,10 +320,12 @@
 
 def fast_body(out_grad, layer_input, expert_ids, gate_prob, w_stack, scale_exps):
     n_dp = lax.axis_size("dp")
-    n_z = lax.axis_size("expert") // CORES
+    n_ex = lax.axis_size("expert")
+    n_z = n_ex // CORES
     tok = out_grad.shape[0]
     p = lax.axis_index("dp").astype(I32).reshape(1)
-    hit, *blocks = slots(p, expert_ids.T, gate_prob.T, out_grad, layer_input, n_dp)
+    e = lax.axis_index("expert").astype(I32).reshape(1)
+    hit, *blocks = slots(p, e, expert_ids.T, gate_prob.T, out_grad, layer_input, n_dp)
     w = scale_weights(scale_exps, w_stack)
     got = [blocks[0]] + [shift(blocks[k], "dp", k) for k in range(1, n_dp)]
     mine = jnp.concatenate(got, axis=0)
@@ -335,21 +343,13 @@
         rb = shift(b, "dp", 1)
         xs.append(x)
         sums.append((a, ra, b, rb))
-    gs, outs = [], []
+    gs, out = [], ()
     for a, ra, b, rb in sums:
-        g, out = backward(p, a, ra, b, rb, w, n_dp, n_z)
+        g, *out = backward(e, a, ra, b, rb, w, n_dp, n_ex, out)
         gs.append(g)
-        outs.append(out)
-    weight_grads = weight_grad((0,), *xs, *gs)
-    weight_grads = weight_grad((1, 2), *xs, *gs, weight_grads)
-    summed = add_bf16(outs[0], shift(outs[1], "expert", 1))
-    summed = summed.reshape(n_z, -1, summed.shape[1])
-    total = summed[0].astype(F32)
-    for k in range(1, n_z):
-        total = total + shift(summed[k], "expert", k * CORES).astype(F32)
-    total = total.astype(BF16).reshape(n_dp, -1, summed.shape[2])
-    parts = [total[0]] + [shift(total[k], "dp", k) for k in range(1, n_dp)]
-    input_grad = place(p, hit, parts, tok)
+    weight_grads = weight_grad((0, 1, 2), *xs, *gs)
+    got = lax.all_to_all(out[0], ("dp", "expert"), split_axis=0, concat_axis=0, tiled=True)
+    input_grad = place(hit, got, tok, n_dp)
     return input_grad, weight_grads
 
 

time: 65.1 us -> 59.5 us (0.914)
  starting transfers between devices: 23.5 us -> 19.2 us
  waiting for transfers between devices: 26.1 us -> 25.1 us
    ppermute x22 -> x15, starting transfers between devices: 23.5 us -> 16.6 us  [shift(): return lax.ppermute(x, axis, xor_pairs(lax.axis_size(axis), k))]
    ppermute x22 -> x15, waiting for transfers between devices: 26.1 us -> 20.3 us  [shift(): return lax.ppermute(x, axis, xor_pairs(lax.axis_size(axis), k))]
    all_to_all x0 -> x1, waiting for transfers between devices: none -> 4.8 us  [fast_body(): lax.all_to_all(out[0], ('dp', 'expert'), split_axis=0, concat_axis=0, til...]
    all_to_all x0 -> x1, starting transfers between devices: none -> 2.58 us  [fast_body(): lax.all_to_all(out[0], ('dp', 'expert'), split_axis=0, concat_axis=0, til...]
    pallas_call x2 -> x1, Pallas kernels: 5.04 us -> 4.01 us  [weight_grad(): pl.pallas_call(functools.partial(weight_grad_kernel, planes=planes, tile=...]
  transfers between devices with their start and end apart: 22 -> 16, of which waited for: 13 -> 10; matrix products, arithmetic and copies ran while one was open for 0% -> 0% of each run, Pallas kernels for 19% -> 15%
where the time goes in v4:
time: 59.5 us; the launch traced here: 59 us
  waiting for transfers between devices  25.1 us (42%)
  starting transfers between devices  19.2 us (32%)
  Pallas kernels  13.8 us (23%)
  between operations  0.74 us (1%)
    ppermute x15, waiting for transfers between devices, shift(): return lax.ppermute(x, axis, xor_pairs(lax.axis_size(axis), k))  20.3 us
    ppermute x15, starting transfers between devices, shift(): return lax.ppermute(x, axis, xor_pairs(lax.axis_size(axis), k))  16.6 us
    all_to_all x1, waiting for transfers between devices, fast_body(): lax.all_to_all(out[0], ('dp', 'expert'), split_axis=0, concat_axis=0, til...  4.8 us
    pallas_call x1, Pallas kernels, weight_grad(): pl.pallas_call(functools.partial(weight_grad_kernel, planes=planes, tile=...  4.01 us
    pallas_call x2, Pallas kernels, backward(): pl.pallas_call(functools.partial(backward_kernel, n_dp=n_dp), out_shape=[...  3.04 us
    all_to_all x1, starting transfers between devices, fast_body(): lax.all_to_all(out[0], ('dp', 'expert'), split_axis=0, concat_axis=0, til...  2.58 us
    pallas_call x1, Pallas kernels, scale_weights(): pl.pallas_call(scale_kernel, out_shape=pltpu.VMEM(w.shape, BF16), in_spec...  2.53 us
    pallas_call x2, Pallas kernels, forward(): pl.pallas_call(functools.partial(forward_kernel, n_dp=n_dp), out_shape=[p...  2.09 us
  transfers between devices with their start and end apart: 16, of which 10 were waited for; matrix products, arithmetic and copies ran while one was open for 0% of the time, Pallas kernels for 15%

profile of v4, /device:TPU:0, one launch (start us, length us, event | category | flops | bytes accessed | tf_op | source)
XLA Modules:
  0.0 59.0 jit_solution(2627814104116656308)
XLA Ops:
  0.6 1.3 %slots.1 = (f32[8,12]{1,0:T(8,128)S(1)}, bf16[8,768]{1,0:T(8,128)(2,1)S(1)}, bf16[8,768]{1,0:T(8,128)(2,1)S(1)}, bf16[8,768]{1,0:T(8,128)(2,1)S(1)}, bf16[8,768]{1,0:T(8,128)(2,1)S(1)}) custom-call(s32[1]{0:T(128)} %bitcast.p_ref, s32[1]{0:T(128)} %bitcast.1.e_ref, s32[2,12]{1,0:T(2,128)} %bitcast.4, f32[2,12]{1,0:T(2,128)} %bitcast.5, ...), custom_call_target="tpu_custom_call" | custom-call | tf_op jit(solution)/shard_map/slots/pallas_call | solution.py:88
  2.0 3.0 %collective-permute-start = (bf16[8,768]{1,0:T(8,128)(2,1)S(1)}, bf16[8,768]{1,0:T(8,128)(2,1)S(1)}, u32[]{:S(2)}, u32[]{:S(2)}) collective-permute-start(bf16[8,768]{1,0:T(8,128)(2,1)S(1)} %get-tuple-element.19), channel_id=1, source_target_pairs={{0,8},{8,0},{16,24},{24,16},{1,9},{9,1},{17,25},{25,17},{2,10},{10... | collective-permute-start | bytes 36872 | tf_op jit(solution)/shard_map/ppermute | solution.py:314
  5.0 1.5 %collective-permute-start.1 = (bf16[8,768]{1,0:T(8,128)(2,1)S(1)}, bf16[8,768]{1,0:T(8,128)(2,1)S(1)}, u32[]{:S(2)}, u32[]{:S(2)}) collective-permute-start(bf16[8,768]{1,0:T(8,128)(2,1)S(1)} %get-tuple-element.20), channel_id=1, source_target_pairs={{0,16},{8,24},{16,0},{24,8},{1,17},{9,25},{17,1},{25,9},{2,18},{10... | collective-permute-start | bytes 36872 | tf_op jit(solution)/shard_map/ppermute | solution.py:314
  6.5 0.0 collective-permute-start.2
  6.5 0.1 collective-permute-done
  6.7 2.0 %collective-permute-done.1 = bf16[8,768]{1,0:T(8,128)(2,1)S(1)} collective-permute-done((bf16[8,768]{1,0:T(8,128)(2,1)S(1)}, bf16[8,768]{1,0:T(8,128)(2,1)S(1)}, u32[]{:S(2)}, u32[]{:S(2)}) %collective-permute-start.1) | collective-permute-done | bytes 12320 | tf_op jit(solution)/shard_map/ppermute | solution.py:314
  8.7 2.4 %collective-permute-done.2 = bf16[8,768]{1,0:T(8,128)(2,1)S(1)} collective-permute-done((bf16[8,768]{1,0:T(8,128)(2,1)S(1)}, bf16[8,768]{1,0:T(8,128)(2,1)S(1)}, u32[]{:S(2)}, u32[]{:S(2)}) %collective-permute-start.2) | collective-permute-done | bytes 12320 | tf_op jit(solution)/shard_map/ppermute | solution.py:314
  11.1 1.6 %collective-permute-start.3 = (bf16[32,768]{1,0:T(8,128)(2,1)S(1)}, bf16[32,768]{1,0:T(8,128)(2,1)S(1)}, u32[]{:S(2)}, u32[]{:S(2)}) collective-permute-start(bf16[32,768]{1,0:T(8,128)(2,1)S(1)} %get-tuple-element.32), channel_id=1, source_target_pairs={{0,2},{1,3},{2,0},{3,1},{4,6},{5,7},{6,4},{7,5},{8,10},{9,11},{10,... | collective-permute-start | bytes 147464 | tf_op jit(solution)/shard_map/ppermute | solution.py:314
  12.7 2.5 %scale.1.w_ref = bf16[3,768,1024]{2,1,0:T(8,128)(2,1)S(1)} custom-call(s32[3,6,8]{2,1,0:T(8,128)} %exp_hbm.1, bf16[3,768,1024]{2,1,0:T(8,128)(2,1)} %w_ref.1), custom_call_target="tpu_custom_call" | custom-call | tf_op jit(solution)/shard_map/scale/pallas_call | solution.py:136
  15.2 2.5 %collective-permute-start.5 = (bf16[32,768]{1,0:T(8,128)(2,1)S(1)}, bf16[32,768]{1,0:T(8,128)(2,1)S(1)}, u32[]{:S(2)}, u32[]{:S(2)}) collective-permute-start(bf16[32,768]{1,0:T(8,128)(2,1)S(1)} %get-tuple-element.32), channel_id=1, source_target_pairs={{0,6},{1,7},{2,4},{3,5},{4,2},{5,3},{6,0},{7,1},{8,14},{9,15},{10,... | collective-permute-start | bytes 147464 | tf_op jit(solution)/shard_map/ppermute | solution.py:314
  17.8 0.2 collective-permute-start.4
  18.0 0.0 collective-permute-done.3
  18.0 5.3 %collective-permute-done.4 = bf16[32,768]{1,0:T(8,128)(2,1)S(1)} collective-permute-done((bf16[32,768]{1,0:T(8,128)(2,1)S(1)}, bf16[32,768]{1,0:T(8,128)(2,1)S(1)}, u32[]{:S(2)}, u32[]{:S(2)}) %collective-permute-start.4) | collective-permute-done | bytes 49184 | tf_op jit(solution)/shard_map/ppermute | solution.py:314
  23.3 0.0 collective-permute-done.5
  23.3 1.0 %forward.3 = (bf16[2,48,768]{2,1,0:T(8,128)(2,1)S(1)}, bf16[3,48,512]{2,1,0:T(8,128)(2,1)S(1)}, bf16[3,48,512]{2,1,0:T(8,128)(2,1)S(1)}) custom-call(s32[1]{0:T(128)} %bitcast.p_ref, bf16[128,768]{1,0:T(8,128)(2,1)S(1)} %constant_dynamic-update-slice_fusion.4.m_ref, bf16[3,768,1024]{2,1,0:T(8,128)(2,1)S(1)} %scale.1.w_ref), custom_call_target="tpu_custom_call" | custom-call | tf_op jit(solution)/shard_map/forward/pallas_call | solution.py:181
  24.4 0.6 %collective-permute-start.11 = (bf16[3,48,512]{2,1,0:T(8,128)(2,1)S(1)}, bf16[3,48,512]{2,1,0:T(8,128)(2,1)S(1)}, u32[]{:S(2)}, u32[]{:S(2)}) collective-permute-start(bf16[3,48,512]{2,1,0:T(8,128)(2,1)S(1)} %get-tuple-element.24), channel_id=1, source_target_pairs={{0,8},{8,0},{16,24},{24,16},{1,9},{9,1},{17,25},{25,17},{2,10},{10... | collective-permute-start | bytes 442376 | tf_op jit(solution)/shard_map/ppermute | solution.py:314
  25.0 0.0 collective-permute-start.6
  25.0 0.5 collective-permute-start.13
  25.5 4.1 %collective-permute-done.11 = bf16[3,48,512]{2,1,0:T(8,128)(2,1)S(1)} collective-permute-done((bf16[3,48,512]{2,1,0:T(8,128)(2,1)S(1)}, bf16[3,48,512]{2,1,0:T(8,128)(2,1)S(1)}, u32[]{:S(2)}, u32[]{:S(2)}) %collective-permute-start.11) | collective-permute-done | bytes 147488 | tf_op jit(solution)/shard_map/ppermute | solution.py:314
  29.6 0.6 collective-permute-start.12
  30.2 0.0 collective-permute-done.6.m_ref
  30.2 1.0 %forward.2 = (bf16[2,48,768]{2,1,0:T(8,128)(2,1)S(1)}, bf16[3,48,512]{2,1,0:T(8,128)(2,1)S(1)}, bf16[3,48,512]{2,1,0:T(8,128)(2,1)S(1)}) custom-call(s32[1]{0:T(128)} %bitcast.p_ref, bf16[128,768]{1,0:T(8,128)(2,1)S(1)} %collective-permute-done.6.m_ref, bf16[3,768,1024]{2,1,0:T(8,128)(2,1)S(1)} %scale.1.w_ref), custom_call_target="tpu_custom_call" | custom-call | tf_op jit(solution)/shard_map/forward/pallas_call | solution.py:181
  31.2 0.6 %collective-permute-start.7 = (bf16[3,48,512]{2,1,0:T(8,128)(2,1)S(1)}, bf16[3,48,512]{2,1,0:T(8,128)(2,1)S(1)}, u32[]{:S(2)}, u32[]{:S(2)}) collective-permute-start(bf16[3,48,512]{2,1,0:T(8,128)(2,1)S(1)} %get-tuple-element.22), channel_id=1, source_target_pairs={{0,8},{8,0},{16,24},{24,16},{1,9},{9,1},{17,25},{25,17},{2,10},{10... | collective-permute-start | bytes 442376 | tf_op jit(solution)/shard_map/ppermute | solution.py:314
  31.8 0.0 collective-permute-done.13
  31.9 1.6 %collective-permute-start.14 = (bf16[3,48,512]{2,1,0:T(8,128)(2,1)S(1)}, bf16[3,48,512]{2,1,0:T(8,128)(2,1)S(1)}, u32[]{:S(2)}, u32[]{:S(2)}) collective-permute-start(bf16[3,48,512]{2,1,0:T(8,128)(2,1)S(1)} %add_convert_fusion.b_ref), channel_id=1, source_target_pairs={{0,8},{8,0},{16,24},{24,16},{1,9},{9,1},{17,25},{25,17},{2,10},{10... | collective-permute-start | bytes 442376 | tf_op jit(solution)/shard_map/ppermute | solution.py:314
  33.4 1.5 %collective-permute-start.9 = (bf16[3,48,512]{2,1,0:T(8,128)(2,1)S(1)}, bf16[3,48,512]{2,1,0:T(8,128)(2,1)S(1)}, u32[]{:S(2)}, u32[]{:S(2)}) collective-permute-start(bf16[3,48,512]{2,1,0:T(8,128)(2,1)S(1)} %get-tuple-element.23), channel_id=1, source_target_pairs={{0,16},{8,24},{16,0},{24,8},{1,17},{9,25},{17,1},{25,9},{2,18},{10... | collective-permute-start | bytes 442376 | tf_op jit(solution)/shard_map/ppermute | solution.py:314
  35.0 1.8 %collective-permute-done.7 = bf16[3,48,512]{2,1,0:T(8,128)(2,1)S(1)} collective-permute-done((bf16[3,48,512]{2,1,0:T(8,128)(2,1)S(1)}, bf16[3,48,512]{2,1,0:T(8,128)(2,1)S(1)}, u32[]{:S(2)}, u32[]{:S(2)}) %collective-permute-start.7) | collective-permute-done | bytes 147488 | tf_op jit(solution)/shard_map/ppermute | solution.py:314
  36.8 1.3 %collective-permute-start.8 = (bf16[3,48,512]{2,1,0:T(8,128)(2,1)S(1)}, bf16[3,48,512]{2,1,0:T(8,128)(2,1)S(1)}, u32[]{:S(2)}, u32[]{:S(2)}) collective-permute-start(bf16[3,48,512]{2,1,0:T(8,128)(2,1)S(1)} %add_convert_fusion.3.a_ref), channel_id=1, source_target_pairs={{0,16},{8,24},{16,0},{24,8},{1,17},{9,25},{17,1},{25,9},{2,18},{10... | collective-permute-start | bytes 442376 | tf_op jit(solution)/shard_map/ppermute | solution.py:314
  38.1 1.5 %collective-permute-done.9 = bf16[3,48,512]{2,1,0:T(8,128)(2,1)S(1)} collective-permute-done((bf16[3,48,512]{2,1,0:T(8,128)(2,1)S(1)}, bf16[3,48,512]{2,1,0:T(8,128)(2,1)S(1)}, u32[]{:S(2)}, u32[]{:S(2)}) %collective-permute-start.9) | collective-permute-done | bytes 147488 | tf_op jit(solution)/shard_map/ppermute | solution.py:314
  39.6 1.1 %collective-permute-start.10 = (bf16[3,48,512]{2,1,0:T(8,128)(2,1)S(1)}, bf16[3,48,512]{2,1,0:T(8,128)(2,1)S(1)}, u32[]{:S(2)}, u32[]{:S(2)}) collective-permute-start(bf16[3,48,512]{2,1,0:T(8,128)(2,1)S(1)} %add_convert_fusion.2.b_ref), channel_id=1, source_target_pairs={{0,8},{8,0},{16,24},{24,16},{1,9},{9,1},{17,25},{25,17},{2,10},{10... | collective-permute-start | bytes 442376 | tf_op jit(solution)/shard_map/ppermute | solution.py:314
  40.7 0.0 collective-permute-done.12.ra_ref
  40.7 0.0 collective-permute-done.14.rb_ref
  40.7 1.1 %backward.2 = (bf16[3,48,1024]{2,1,0:T(8,128)(2,1)S(1)}, bf16[48,768]{1,0:T(8,128)(2,1)S(1)}) custom-call(s32[1]{0:T(128)} %bitcast.1.e_ref, bf16[3,48,512]{2,1,0:T(8,128)(2,1)S(1)} %add_convert_fusion.1.a_ref, bf16[3,48,512]{2,1,0:T(8,128)(2,1)S(1)} %collective-permute-done.12.ra_ref, bf16[3,48,512]{2,1,0:T(8,128)(2,1)S(1)} %add_convert_fusion.b_ref, ...), custom_call_target="tpu_custom_call" | custom-call | tf_op jit(solution)/shard_map/backward/pallas_call | solution.py:235
  41.8 0.2 collective-permute-done.8.ra_ref
  42.0 2.8 %collective-permute-done.10.rb_ref = bf16[3,48,512]{2,1,0:T(8,128)(2,1)S(1)} collective-permute-done((bf16[3,48,512]{2,1,0:T(8,128)(2,1)S(1)}, bf16[3,48,512]{2,1,0:T(8,128)(2,1)S(1)}, u32[]{:S(2)}, u32[]{:S(2)}) %collective-permute-start.10) | collective-permute-done | bytes 147488 | tf_op jit(solution)/shard_map/ppermute | solution.py:314
  44.8 2.0 %backward.3 = (bf16[3,48,1024]{2,1,0:T(8,128)(2,1)S(1)}, bf16[32,4,768]{2,1,0:T(4,128)(2,1)}) custom-call(s32[1]{0:T(128)} %bitcast.1.e_ref, bf16[3,48,512]{2,1,0:T(8,128)(2,1)S(1)} %add_convert_fusion.3.a_ref, bf16[3,48,512]{2,1,0:T(8,128)(2,1)S(1)} %collective-permute-done.8.ra_ref, bf16[3,48,512]{2,1,0:T(8,128)(2,1)S(1)} %add_convert_fusion.2.b_ref, ...), custom_call_target="tpu_custom_call" | custom-call | tf_op jit(solution)/shard_map/backward/pallas_call | solution.py:235
  46.8 2.6 %all-to-all-start = ((bf16[32,4,768]{2,1,0:T(4,128)(2,1)}), bf16[32,4,768]{2,1,0:T(4,128)(2,1)S(1)}, u32[]{:S(2)}, u32[]{:S(2)}) async-start(bf16[32,4,768]{2,1,0:T(4,128)(2,1)} %get-tuple-element.27), calls=%async_computation | async-start | bytes 393216 | tf_op jit(solution)/shard_map/all_to_all | solution.py:351
  49.4 4.0 %weight_grad.1 = f32[3,768,1024]{2,1,0:T(8,128)} custom-call(bf16[2,48,768]{2,1,0:T(8,128)(2,1)S(1)} %get-tuple-element.28.refs_0_, bf16[2,48,768]{2,1,0:T(8,128)(2,1)S(1)} %get-tuple-element.29.refs_1_, bf16[3,48,1024]{2,1,0:T(8,128)(2,1)S(1)} %get-tuple-element.30.refs_2_, bf16[3,48,1024]{2,1,0:T(8,128)(2,1)S(1)} %get-tuple-element.31.refs_3_), custom_call_target="tpu_custom_call" | custom-call | tf_op jit(solution)/shard_map/weight_grad/pallas_call | solution.py:270
  53.4 4.8 %all-to-all-done.got_ref = bf16[32,4,768]{2,1,0:T(4,128)(2,1)S(1)} async-done(((bf16[32,4,768]{2,1,0:T(4,128)(2,1)}), bf16[32,4,768]{2,1,0:T(4,128)(2,1)S(1)}, u32[]{:S(2)}, u32[]{:S(2)}) %all-to-all-start) | async-done | bytes 196640 | tf_op jit(solution)/shard_map/all_to_all | solution.py:351
  58.2 0.8 %place.1 = bf16[12,3072]{1,0:T(8,128)(2,1)} custom-call(f32[8,12]{1,0:T(8,128)S(1)} %get-tuple-element.17.hit_ref, bf16[32,4,768]{2,1,0:T(4,128)(2,1)S(1)} %all-to-all-done.got_ref), custom_call_target="tpu_custom_call" | custom-call | tf_op jit(solution)/shard_map/place/pallas_call | solution.py:299
  (11 shorter events, 0.2 us)
Async XLA Ops:
  2.0 4.7 %collective-permute-start = (bf16[8,768]{1,0:T(8,128)(2,1)S(1)}, bf16[8,768]{1,0:T(8,128)(2,1)S(1)}, u32[]{:S(2)}, u32[]{:S(2)}) collective-permute-start(bf16[8,768]{1,0:T(8,128)(2,1)S(1)} %get-tuple-element.19), channel_id=1, source_target_pairs={{0,8},{8,0},{16,24},{24,16},{1,9},{9,1},{17,25},{25,17},{2,10},{10... | collective-permute-start | bytes 36872 | tf_op jit(solution)/shard_map/ppermute | solution.py:314
  5.0 3.7 %collective-permute-start.1 = (bf16[8,768]{1,0:T(8,128)(2,1)S(1)}, bf16[8,768]{1,0:T(8,128)(2,1)S(1)}, u32[]{:S(2)}, u32[]{:S(2)}) collective-permute-start(bf16[8,768]{1,0:T(8,128)(2,1)S(1)} %get-tuple-element.20), channel_id=1, source_target_pairs={{0,16},{8,24},{16,0},{24,8},{1,17},{9,25},{17,1},{25,9},{2,18},{10... | collective-permute-start | bytes 36872 | tf_op jit(solution)/shard_map/ppermute | solution.py:314
  6.5 4.6 %collective-permute-start.2 = (bf16[8,768]{1,0:T(8,128)(2,1)S(1)}, bf16[8,768]{1,0:T(8,128)(2,1)S(1)}, u32[]{:S(2)}, u32[]{:S(2)}) collective-permute-start(bf16[8,768]{1,0:T(8,128)(2,1)S(1)} %get-tuple-element.21), channel_id=1, source_target_pairs={{0,24},{8,16},{16,8},{24,0},{1,25},{9,17},{17,9},{25,1},{2,26},{10... | collective-permute-start | bytes 36872 | tf_op jit(solution)/shard_map/ppermute | solution.py:314
  11.1 6.9 %collective-permute-start.3 = (bf16[32,768]{1,0:T(8,128)(2,1)S(1)}, bf16[32,768]{1,0:T(8,128)(2,1)S(1)}, u32[]{:S(2)}, u32[]{:S(2)}) collective-permute-start(bf16[32,768]{1,0:T(8,128)(2,1)S(1)} %get-tuple-element.32), channel_id=1, source_target_pairs={{0,2},{1,3},{2,0},{3,1},{4,6},{5,7},{6,4},{7,5},{8,10},{9,11},{10,... | collective-permute-start | bytes 147464 | tf_op jit(solution)/shard_map/ppermute | solution.py:314
  15.2 8.1 %collective-permute-start.5 = (bf16[32,768]{1,0:T(8,128)(2,1)S(1)}, bf16[32,768]{1,0:T(8,128)(2,1)S(1)}, u32[]{:S(2)}, u32[]{:S(2)}) collective-permute-start(bf16[32,768]{1,0:T(8,128)(2,1)S(1)} %get-tuple-element.32), channel_id=1, source_target_pairs={{0,6},{1,7},{2,4},{3,5},{4,2},{5,3},{6,0},{7,1},{8,14},{9,15},{10,... | collective-permute-start | bytes 147464 | tf_op jit(solution)/shard_map/ppermute | solution.py:314
  17.8 5.5 %collective-permute-start.4 = (bf16[32,768]{1,0:T(8,128)(2,1)S(1)}, bf16[32,768]{1,0:T(8,128)(2,1)S(1)}, u32[]{:S(2)}, u32[]{:S(2)}) collective-permute-start(bf16[32,768]{1,0:T(8,128)(2,1)S(1)} %get-tuple-element.32), channel_id=1, source_target_pairs={{0,4},{1,5},{2,6},{3,7},{4,0},{5,1},{6,2},{7,3},{8,12},{9,13},{10,... | collective-permute-start | bytes 147464 | tf_op jit(solution)/shard_map/ppermute | solution.py:314
  24.4 5.2 %collective-permute-start.11 = (bf16[3,48,512]{2,1,0:T(8,128)(2,1)S(1)}, bf16[3,48,512]{2,1,0:T(8,128)(2,1)S(1)}, u32[]{:S(2)}, u32[]{:S(2)}) collective-permute-start(bf16[3,48,512]{2,1,0:T(8,128)(2,1)S(1)} %get-tuple-element.24), channel_id=1, source_target_pairs={{0,8},{8,0},{16,24},{24,16},{1,9},{9,1},{17,25},{25,17},{2,10},{10... | collective-permute-start | bytes 442376 | tf_op jit(solution)/shard_map/ppermute | solution.py:314
  25.0 5.2 %collective-permute-start.6 = (bf16[128,768]{1,0:T(8,128)(2,1)S(1)}, bf16[128,768]{1,0:T(8,128)(2,1)S(1)}, u32[]{:S(2)}, u32[]{:S(2)}) collective-permute-start(bf16[128,768]{1,0:T(8,128)(2,1)S(1)} %constant_dynamic-update-slice_fusion.4.m_ref), channel_id=1, source_target_pairs={{0,1},{1,0},{2,3},{3,2},{4,5},{5,4},{6,7},{7,6},{8,9},{9,8},{10,11... | collective-permute-start | bytes 589832 | tf_op jit(solution)/shard_map/ppermute | solution.py:314
  25.0 6.9 %collective-permute-start.13 = (bf16[3,48,512]{2,1,0:T(8,128)(2,1)S(1)}, bf16[3,48,512]{2,1,0:T(8,128)(2,1)S(1)}, u32[]{:S(2)}, u32[]{:S(2)}) collective-permute-start(bf16[3,48,512]{2,1,0:T(8,128)(2,1)S(1)} %get-tuple-element.25), channel_id=1, source_target_pairs={{0,16},{8,24},{16,0},{24,8},{1,17},{9,25},{17,1},{25,9},{2,18},{10... | collective-permute-start | bytes 442376 | tf_op jit(solution)/shard_map/ppermute | solution.py:314
  29.6 11.1 %collective-permute-start.12 = (bf16[3,48,512]{2,1,0:T(8,128)(2,1)S(1)}, bf16[3,48,512]{2,1,0:T(8,128)(2,1)S(1)}, u32[]{:S(2)}, u32[]{:S(2)}) collective-permute-start(bf16[3,48,512]{2,1,0:T(8,128)(2,1)S(1)} %add_convert_fusion.1.a_ref), channel_id=1, source_target_pairs={{0,16},{8,24},{16,0},{24,8},{1,17},{9,25},{17,1},{25,9},{2,18},{10... | collective-permute-start | bytes 442376 | tf_op jit(solution)/shard_map/ppermute | solution.py:314
  31.2 5.5 %collective-permute-start.7 = (bf16[3,48,512]{2,1,0:T(8,128)(2,1)S(1)}, bf16[3,48,512]{2,1,0:T(8,128)(2,1)S(1)}, u32[]{:S(2)}, u32[]{:S(2)}) collective-permute-start(bf16[3,48,512]{2,1,0:T(8,128)(2,1)S(1)} %get-tuple-element.22), channel_id=1, source_target_pairs={{0,8},{8,0},{16,24},{24,16},{1,9},{9,1},{17,25},{25,17},{2,10},{10... | collective-permute-start | bytes 442376 | tf_op jit(solution)/shard_map/ppermute | solution.py:314
  31.9 8.9 %collective-permute-start.14 = (bf16[3,48,512]{2,1,0:T(8,128)(2,1)S(1)}, bf16[3,48,512]{2,1,0:T(8,128)(2,1)S(1)}, u32[]{:S(2)}, u32[]{:S(2)}) collective-permute-start(bf16[3,48,512]{2,1,0:T(8,128)(2,1)S(1)} %add_convert_fusion.b_ref), channel_id=1, source_target_pairs={{0,8},{8,0},{16,24},{24,16},{1,9},{9,1},{17,25},{25,17},{2,10},{10... | collective-permute-start | bytes 442376 | tf_op jit(solution)/shard_map/ppermute | solution.py:314
  33.4 6.1 %collective-permute-start.9 = (bf16[3,48,512]{2,1,0:T(8,128)(2,1)S(1)}, bf16[3,48,512]{2,1,0:T(8,128)(2,1)S(1)}, u32[]{:S(2)}, u32[]{:S(2)}) collective-permute-start(bf16[3,48,512]{2,1,0:T(8,128)(2,1)S(1)} %get-tuple-element.23), channel_id=1, source_target_pairs={{0,16},{8,24},{16,0},{24,8},{1,17},{9,25},{17,1},{25,9},{2,18},{10... | collective-permute-start | bytes 442376 | tf_op jit(solution)/shard_map/ppermute | solution.py:314
  36.8 5.2 %collective-permute-start.8 = (bf16[3,48,512]{2,1,0:T(8,128)(2,1)S(1)}, bf16[3,48,512]{2,1,0:T(8,128)(2,1)S(1)}, u32[]{:S(2)}, u32[]{:S(2)}) collective-permute-start(bf16[3,48,512]{2,1,0:T(8,128)(2,1)S(1)} %add_convert_fusion.3.a_ref), channel_id=1, source_target_pairs={{0,16},{8,24},{16,0},{24,8},{1,17},{9,25},{17,1},{25,9},{2,18},{10... | collective-permute-start | bytes 442376 | tf_op jit(solution)/shard_map/ppermute | solution.py:314
  39.6 5.2 %collective-permute-start.10 = (bf16[3,48,512]{2,1,0:T(8,128)(2,1)S(1)}, bf16[3,48,512]{2,1,0:T(8,128)(2,1)S(1)}, u32[]{:S(2)}, u32[]{:S(2)}) collective-permute-start(bf16[3,48,512]{2,1,0:T(8,128)(2,1)S(1)} %add_convert_fusion.2.b_ref), channel_id=1, source_target_pairs={{0,8},{8,0},{16,24},{24,16},{1,9},{9,1},{17,25},{25,17},{2,10},{10... | collective-permute-start | bytes 442376 | tf_op jit(solution)/shard_map/ppermute | solution.py:314
  46.8 11.4 %all-to-all-start = ((bf16[32,4,768]{2,1,0:T(4,128)(2,1)}), bf16[32,4,768]{2,1,0:T(4,128)(2,1)S(1)}, u32[]{:S(2)}, u32[]{:S(2)}) async-start(bf16[32,4,768]{2,1,0:T(4,128)(2,1)} %get-tuple-element.27), calls=%async_computation | async-start | bytes 393216 | tf_op jit(solution)/shard_map/all_to_all | solution.py:351

commit v5 on v4

--- a/solution.py
+++ b/solution.py
@@ -14,7 +14,7 @@
 I32 = jnp.int32
 ROWS = 8
 CHUNKS = 3
-CAPP = 4
+CAPP = 2
 CORES = 2
 LIMIT = 20 * 1024 * 1024
 VMEM = pltpu.VMEM
@@ -213,25 +213,36 @@
     if before_ref is None:
         out_ref[...] = back
         return
-    count, capp, _ = out_ref.shape
+    count, capp, lanes = out_ref.shape
     n_ex = count // n_dp
+    part = lanes // CAP
     both = jnp.concatenate([before_ref[...], back], axis=0)
     o = lax.broadcasted_iota(I32, (count * capp, 1), 0)
-    c = o & (capp - 1)
+    q = o & (capp - 1)
     ex = ((o >> log2(capp)) & (n_ex - 1)) ^ e_ref[0]
     pa = o >> (log2(capp) + log2(n_ex))
-    slot = (ex & 1) * slot_count + pa * group + (ex >> 1) * CAP + c
-    slot = jnp.where(c < CAP, slot, -1)
-    hit = lax.broadcasted_iota(I32, (count * capp, CORES * slot_count), 1) == slot
-    out = nn(jnp.where(hit, 1.0, 0.0).astype(BF16), both).astype(BF16)
-    for d in range(count):
-        out_ref[d] = out[d * capp : (d + 1) * capp]
+    slot = (ex & 1) * slot_count + pa * group + (ex >> 1) * CAP
+    line = lax.broadcasted_iota(I32, (count * capp, CORES * slot_count), 1)
+    for j in range(CAP):
+        total = None
+        for half in range(2):
+            wanted = -1
+            for row in range(capp):
+                c, h = divmod(row * CAP + j, 2)
+                if h == half:
+                    wanted = jnp.where(q == row, slot + c, wanted)
+            hit = jnp.where(line == wanted, 1.0, 0.0).astype(BF16)
+            moved = nn(hit, both[:, half * part : (half + 1) * part])
+            total = moved if total is None else total + moved
+        total = total.astype(BF16)
+        for d in range(count):
+            out_ref[d, :, j * part : (j + 1) * part] = total[d * capp : (d + 1) * capp]
 
 
 def backward(e, a, ra, b, rb, w, n_dp, n_ex, before=()):
     n, slot_count, half = a.shape
     width = w.shape[1]
-    shape = (n_dp * n_ex, CAPP, width) if before else (slot_count, width)
+    shape = (n_dp * n_ex, CAPP, width * CAP // CAPP) if before else (slot_count, width)
     return pl.pallas_call(
         functools.partial(backward_kernel, n_dp=n_dp),
         out_shape=[pltpu.VMEM((n, slot_count, 2 * half), BF16), pltpu.VMEM(shape, BF16)],
@@ -284,18 +295,36 @@
 
 
 def place_kernel(hit_ref, got_ref, out_ref, *, n_dp):
-    count, capp, width = got_ref.shape
+    count, capp, lanes = got_ref.shape
     n_ex = count // n_dp
-    hit = hit_ref[:capp, :].astype(BF16)
+    part = lanes // CAP
+    hit = hit_ref[...]
+    row = lax.broadcasted_iota(I32, (capp, hit.shape[1]), 0)
+    picks = []
+    for half in range(2):
+        for j in range(CAP):
+            pick = jnp.zeros(row.shape, F32)
+            for r in range(capp):
+                c, h = divmod(r * CAP + j, 2)
+                if h == half:
+                    pick = jnp.where(row == r, hit[c : c + 1], pick)
+            picks.append(pick.astype(BF16))
     for p in range(n_dp):
         total = got_ref[p * n_ex].astype(F32)
         for e in range(1, n_ex):
             total = total + got_ref[p * n_ex + e].astype(F32)
-        out_ref[:, p * width : (p + 1) * width] = tn(hit, total.astype(BF16)).astype(BF16)
+        total = total.astype(BF16)
+        for half in range(2):
+            out = None
+            for j in range(CAP):
+                moved = tn(picks[half * CAP + j], total[:, j * part : (j + 1) * part])
+                out = moved if out is None else out + moved
+            at = (2 * p + half) * part
+            out_ref[:, at : at + part] = out.astype(BF16)
 
 
 def place(hit, got, tok, n_dp):
-    width = got.shape[2]
+    width = got.shape[2] // CAP * 2
     return pl.pallas_call(
         functools.partial(place_kernel, n_dp=n_dp),
         out_shape=jax.ShapeDtypeStruct((tok, width * n_dp), BF16),

time: 59.5 us -> 59.1 us (level)
  no operation moved by 1% of the time
where the time goes in v5:
time: 59.1 us; the launch traced here: 58.8 us
  waiting for transfers between devices  24.6 us (42%)
  starting transfers between devices  19.2 us (32%)
  Pallas kernels  14.1 us (24%)
  between operations  0.74 us (1%)
    ppermute x15, waiting for transfers between devices, shift(): return lax.ppermute(x, axis, xor_pairs(lax.axis_size(axis), k))  20.3 us
    ppermute x15, starting transfers between devices, shift(): return lax.ppermute(x, axis, xor_pairs(lax.axis_size(axis), k))  16.6 us
    all_to_all x1, waiting for transfers between devices, fast_body(): lax.all_to_all(out[0], ('dp', 'expert'), split_axis=0, concat_axis=0, til...  4.35 us
    pallas_call x1, Pallas kernels, weight_grad(): pl.pallas_call(functools.partial(weight_grad_kernel, planes=planes, tile=...  4.01 us
    pallas_call x2, Pallas kernels, backward(): pl.pallas_call(functools.partial(backward_kernel, n_dp=n_dp), out_shape=[...  3.15 us
    all_to_all x1, starting transfers between devices, fast_body(): lax.all_to_all(out[0], ('dp', 'expert'), split_axis=0, concat_axis=0, til...  2.57 us
    pallas_call x1, Pallas kernels, scale_weights(): pl.pallas_call(scale_kernel, out_shape=pltpu.VMEM(w.shape, BF16), in_spec...  2.53 us
    pallas_call x2, Pallas kernels, forward(): pl.pallas_call(functools.partial(forward_kernel, n_dp=n_dp), out_shape=[p...  2.09 us
  transfers between devices with their start and end apart: 16, of which 10 were waited for; matrix products, arithmetic and copies ran while one was open for 0% of the time, Pallas kernels for 15%

profile of v5, /device:TPU:0, one launch (start us, length us, event | category | flops | bytes accessed | tf_op | source)
XLA Modules:
  0.0 58.8 jit_solution(16426443381164115394)
XLA Ops:
  0.6 1.3 %slots.1 = (f32[8,12]{1,0:T(8,128)S(1)}, bf16[8,768]{1,0:T(8,128)(2,1)S(1)}, bf16[8,768]{1,0:T(8,128)(2,1)S(1)}, bf16[8,768]{1,0:T(8,128)(2,1)S(1)}, bf16[8,768]{1,0:T(8,128)(2,1)S(1)}) custom-call(s32[1]{0:T(128)} %bitcast.p_ref, s32[1]{0:T(128)} %bitcast.1.e_ref, s32[2,12]{1,0:T(2,128)} %bitcast.4, f32[2,12]{1,0:T(2,128)} %bitcast.5, ...), custom_call_target="tpu_custom_call" | custom-call | tf_op jit(solution)/shard_map/slots/pallas_call | solution.py:88
  2.0 3.0 %collective-permute-start = (bf16[8,768]{1,0:T(8,128)(2,1)S(1)}, bf16[8,768]{1,0:T(8,128)(2,1)S(1)}, u32[]{:S(2)}, u32[]{:S(2)}) collective-permute-start(bf16[8,768]{1,0:T(8,128)(2,1)S(1)} %get-tuple-element.19), channel_id=1, source_target_pairs={{0,8},{8,0},{16,24},{24,16},{1,9},{9,1},{17,25},{25,17},{2,10},{10... | collective-permute-start | bytes 36872 | tf_op jit(solution)/shard_map/ppermute | solution.py:343
  5.0 1.5 %collective-permute-start.1 = (bf16[8,768]{1,0:T(8,128)(2,1)S(1)}, bf16[8,768]{1,0:T(8,128)(2,1)S(1)}, u32[]{:S(2)}, u32[]{:S(2)}) collective-permute-start(bf16[8,768]{1,0:T(8,128)(2,1)S(1)} %get-tuple-element.20), channel_id=1, source_target_pairs={{0,16},{8,24},{16,0},{24,8},{1,17},{9,25},{17,1},{25,9},{2,18},{10... | collective-permute-start | bytes 36872 | tf_op jit(solution)/shard_map/ppermute | solution.py:343
  6.5 0.0 collective-permute-start.2
  6.5 0.1 collective-permute-done
  6.7 2.0 %collective-permute-done.1 = bf16[8,768]{1,0:T(8,128)(2,1)S(1)} collective-permute-done((bf16[8,768]{1,0:T(8,128)(2,1)S(1)}, bf16[8,768]{1,0:T(8,128)(2,1)S(1)}, u32[]{:S(2)}, u32[]{:S(2)}) %collective-permute-start.1) | collective-permute-done | bytes 12320 | tf_op jit(solution)/shard_map/ppermute | solution.py:343
  8.7 2.4 %collective-permute-done.2 = bf16[8,768]{1,0:T(8,128)(2,1)S(1)} collective-permute-done((bf16[8,768]{1,0:T(8,128)(2,1)S(1)}, bf16[8,768]{1,0:T(8,128)(2,1)S(1)}, u32[]{:S(2)}, u32[]{:S(2)}) %collective-permute-start.2) | collective-permute-done | bytes 12320 | tf_op jit(solution)/shard_map/ppermute | solution.py:343
  11.1 1.6 %collective-permute-start.3 = (bf16[32,768]{1,0:T(8,128)(2,1)S(1)}, bf16[32,768]{1,0:T(8,128)(2,1)S(1)}, u32[]{:S(2)}, u32[]{:S(2)}) collective-permute-start(bf16[32,768]{1,0:T(8,128)(2,1)S(1)} %get-tuple-element.32), channel_id=1, source_target_pairs={{0,2},{1,3},{2,0},{3,1},{4,6},{5,7},{6,4},{7,5},{8,10},{9,11},{10,... | collective-permute-start | bytes 147464 | tf_op jit(solution)/shard_map/ppermute | solution.py:343
  12.7 2.5 %scale.1.w_ref = bf16[3,768,1024]{2,1,0:T(8,128)(2,1)S(1)} custom-call(s32[3,6,8]{2,1,0:T(8,128)} %exp_hbm.1, bf16[3,768,1024]{2,1,0:T(8,128)(2,1)} %w_ref.1), custom_call_target="tpu_custom_call" | custom-call | tf_op jit(solution)/shard_map/scale/pallas_call | solution.py:136
  15.2 2.5 %collective-permute-start.5 = (bf16[32,768]{1,0:T(8,128)(2,1)S(1)}, bf16[32,768]{1,0:T(8,128)(2,1)S(1)}, u32[]{:S(2)}, u32[]{:S(2)}) collective-permute-start(bf16[32,768]{1,0:T(8,128)(2,1)S(1)} %get-tuple-element.32), channel_id=1, source_target_pairs={{0,6},{1,7},{2,4},{3,5},{4,2},{5,3},{6,0},{7,1},{8,14},{9,15},{10,... | collective-permute-start | bytes 147464 | tf_op jit(solution)/shard_map/ppermute | solution.py:343
  17.8 0.2 collective-permute-start.4
  18.0 0.0 collective-permute-done.3
  18.0 5.3 %collective-permute-done.4 = bf16[32,768]{1,0:T(8,128)(2,1)S(1)} collective-permute-done((bf16[32,768]{1,0:T(8,128)(2,1)S(1)}, bf16[32,768]{1,0:T(8,128)(2,1)S(1)}, u32[]{:S(2)}, u32[]{:S(2)}) %collective-permute-start.4) | collective-permute-done | bytes 49184 | tf_op jit(solution)/shard_map/ppermute | solution.py:343
  23.3 0.0 collective-permute-done.5
  23.3 1.0 %forward.3 = (bf16[2,48,768]{2,1,0:T(8,128)(2,1)S(1)}, bf16[3,48,512]{2,1,0:T(8,128)(2,1)S(1)}, bf16[3,48,512]{2,1,0:T(8,128)(2,1)S(1)}) custom-call(s32[1]{0:T(128)} %bitcast.p_ref, bf16[128,768]{1,0:T(8,128)(2,1)S(1)} %constant_dynamic-update-slice_fusion.4.m_ref, bf16[3,768,1024]{2,1,0:T(8,128)(2,1)S(1)} %scale.1.w_ref), custom_call_target="tpu_custom_call" | custom-call | tf_op jit(solution)/shard_map/forward/pallas_call | solution.py:181
  24.4 0.6 %collective-permute-start.11 = (bf16[3,48,512]{2,1,0:T(8,128)(2,1)S(1)}, bf16[3,48,512]{2,1,0:T(8,128)(2,1)S(1)}, u32[]{:S(2)}, u32[]{:S(2)}) collective-permute-start(bf16[3,48,512]{2,1,0:T(8,128)(2,1)S(1)} %get-tuple-element.24), channel_id=1, source_target_pairs={{0,8},{8,0},{16,24},{24,16},{1,9},{9,1},{17,25},{25,17},{2,10},{10... | collective-permute-start | bytes 442376 | tf_op jit(solution)/shard_map/ppermute | solution.py:343
  25.0 0.0 collective-permute-start.6
  25.0 0.5 collective-permute-start.13
  25.5 4.1 %collective-permute-done.11 = bf16[3,48,512]{2,1,0:T(8,128)(2,1)S(1)} collective-permute-done((bf16[3,48,512]{2,1,0:T(8,128)(2,1)S(1)}, bf16[3,48,512]{2,1,0:T(8,128)(2,1)S(1)}, u32[]{:S(2)}, u32[]{:S(2)}) %collective-permute-start.11) | collective-permute-done | bytes 147488 | tf_op jit(solution)/shard_map/ppermute | solution.py:343
  29.6 0.6 collective-permute-start.12
  30.2 0.0 collective-permute-done.6.m_ref
  30.2 1.0 %forward.2 = (bf16[2,48,768]{2,1,0:T(8,128)(2,1)S(1)}, bf16[3,48,512]{2,1,0:T(8,128)(2,1)S(1)}, bf16[3,48,512]{2,1,0:T(8,128)(2,1)S(1)}) custom-call(s32[1]{0:T(128)} %bitcast.p_ref, bf16[128,768]{1,0:T(8,128)(2,1)S(1)} %collective-permute-done.6.m_ref, bf16[3,768,1024]{2,1,0:T(8,128)(2,1)S(1)} %scale.1.w_ref), custom_call_target="tpu_custom_call" | custom-call | tf_op jit(solution)/shard_map/forward/pallas_call | solution.py:181
  31.2 0.6 %collective-permute-start.7 = (bf16[3,48,512]{2,1,0:T(8,128)(2,1)S(1)}, bf16[3,48,512]{2,1,0:T(8,128)(2,1)S(1)}, u32[]{:S(2)}, u32[]{:S(2)}) collective-permute-start(bf16[3,48,512]{2,1,0:T(8,128)(2,1)S(1)} %get-tuple-element.22), channel_id=1, source_target_pairs={{0,8},{8,0},{16,24},{24,16},{1,9},{9,1},{17,25},{25,17},{2,10},{10... | collective-permute-start | bytes 442376 | tf_op jit(solution)/shard_map/ppermute | solution.py:343
  31.8 0.0 collective-permute-done.13
  31.9 1.6 %collective-permute-start.14 = (bf16[3,48,512]{2,1,0:T(8,128)(2,1)S(1)}, bf16[3,48,512]{2,1,0:T(8,128)(2,1)S(1)}, u32[]{:S(2)}, u32[]{:S(2)}) collective-permute-start(bf16[3,48,512]{2,1,0:T(8,128)(2,1)S(1)} %add_convert_fusion.b_ref), channel_id=1, source_target_pairs={{0,8},{8,0},{16,24},{24,16},{1,9},{9,1},{17,25},{25,17},{2,10},{10... | collective-permute-start | bytes 442376 | tf_op jit(solution)/shard_map/ppermute | solution.py:343
  33.4 1.5 %collective-permute-start.9 = (bf16[3,48,512]{2,1,0:T(8,128)(2,1)S(1)}, bf16[3,48,512]{2,1,0:T(8,128)(2,1)S(1)}, u32[]{:S(2)}, u32[]{:S(2)}) collective-permute-start(bf16[3,48,512]{2,1,0:T(8,128)(2,1)S(1)} %get-tuple-element.23), channel_id=1, source_target_pairs={{0,16},{8,24},{16,0},{24,8},{1,17},{9,25},{17,1},{25,9},{2,18},{10... | collective-permute-start | bytes 442376 | tf_op jit(solution)/shard_map/ppermute | solution.py:343
  35.0 1.8 %collective-permute-done.7 = bf16[3,48,512]{2,1,0:T(8,128)(2,1)S(1)} collective-permute-done((bf16[3,48,512]{2,1,0:T(8,128)(2,1)S(1)}, bf16[3,48,512]{2,1,0:T(8,128)(2,1)S(1)}, u32[]{:S(2)}, u32[]{:S(2)}) %collective-permute-start.7) | collective-permute-done | bytes 147488 | tf_op jit(solution)/shard_map/ppermute | solution.py:343
  36.8 1.3 %collective-permute-start.8 = (bf16[3,48,512]{2,1,0:T(8,128)(2,1)S(1)}, bf16[3,48,512]{2,1,0:T(8,128)(2,1)S(1)}, u32[]{:S(2)}, u32[]{:S(2)}) collective-permute-start(bf16[3,48,512]{2,1,0:T(8,128)(2,1)S(1)} %add_convert_fusion.3.a_ref), channel_id=1, source_target_pairs={{0,16},{8,24},{16,0},{24,8},{1,17},{9,25},{17,1},{25,9},{2,18},{10... | collective-permute-start | bytes 442376 | tf_op jit(solution)/shard_map/ppermute | solution.py:343
  38.1 1.5 %collective-permute-done.9 = bf16[3,48,512]{2,1,0:T(8,128)(2,1)S(1)} collective-permute-done((bf16[3,48,512]{2,1,0:T(8,128)(2,1)S(1)}, bf16[3,48,512]{2,1,0:T(8,128)(2,1)S(1)}, u32[]{:S(2)}, u32[]{:S(2)}) %collective-permute-start.9) | collective-permute-done | bytes 147488 | tf_op jit(solution)/shard_map/ppermute | solution.py:343
  39.6 1.1 %collective-permute-start.10 = (bf16[3,48,512]{2,1,0:T(8,128)(2,1)S(1)}, bf16[3,48,512]{2,1,0:T(8,128)(2,1)S(1)}, u32[]{:S(2)}, u32[]{:S(2)}) collective-permute-start(bf16[3,48,512]{2,1,0:T(8,128)(2,1)S(1)} %add_convert_fusion.2.b_ref), channel_id=1, source_target_pairs={{0,8},{8,0},{16,24},{24,16},{1,9},{9,1},{17,25},{25,17},{2,10},{10... | collective-permute-start | bytes 442376 | tf_op jit(solution)/shard_map/ppermute | solution.py:343
  40.7 0.0 collective-permute-done.12.ra_ref
  40.7 0.0 collective-permute-done.14.rb_ref
  40.7 1.1 %backward.2 = (bf16[3,48,1024]{2,1,0:T(8,128)(2,1)S(1)}, bf16[48,768]{1,0:T(8,128)(2,1)S(1)}) custom-call(s32[1]{0:T(128)} %bitcast.1.e_ref, bf16[3,48,512]{2,1,0:T(8,128)(2,1)S(1)} %add_convert_fusion.1.a_ref, bf16[3,48,512]{2,1,0:T(8,128)(2,1)S(1)} %collective-permute-done.12.ra_ref, bf16[3,48,512]{2,1,0:T(8,128)(2,1)S(1)} %add_convert_fusion.b_ref, ...), custom_call_target="tpu_custom_call" | custom-call | tf_op jit(solution)/shard_map/backward/pallas_call | solution.py:246
  41.8 0.2 collective-permute-done.8.ra_ref
  42.0 2.8 %collective-permute-done.10.rb_ref = bf16[3,48,512]{2,1,0:T(8,128)(2,1)S(1)} collective-permute-done((bf16[3,48,512]{2,1,0:T(8,128)(2,1)S(1)}, bf16[3,48,512]{2,1,0:T(8,128)(2,1)S(1)}, u32[]{:S(2)}, u32[]{:S(2)}) %collective-permute-start.10) | collective-permute-done | bytes 147488 | tf_op jit(solution)/shard_map/ppermute | solution.py:343
  44.8 2.1 %backward.3 = (bf16[3,48,1024]{2,1,0:T(8,128)(2,1)S(1)}, bf16[32,2,1152]{2,1,0:T(2,128)(2,1)}) custom-call(s32[1]{0:T(128)} %bitcast.1.e_ref, bf16[3,48,512]{2,1,0:T(8,128)(2,1)S(1)} %add_convert_fusion.3.a_ref, bf16[3,48,512]{2,1,0:T(8,128)(2,1)S(1)} %collective-permute-done.8.ra_ref, bf16[3,48,512]{2,1,0:T(8,128)(2,1)S(1)} %add_convert_fusion.2.b_ref, ...), custom_call_target="tpu_custom_call" | custom-call | tf_op jit(solution)/shard_map/backward/pallas_call | solution.py:246
  46.9 2.6 %all-to-all-start = ((bf16[32,2,1152]{2,1,0:T(2,128)(2,1)}), bf16[32,2,1152]{2,1,0:T(2,128)(2,1)S(1)}, u32[]{:S(2)}, u32[]{:S(2)}) async-start(bf16[32,2,1152]{2,1,0:T(2,128)(2,1)} %get-tuple-element.27), calls=%async_computation | async-start | bytes 294912 | tf_op jit(solution)/shard_map/all_to_all | solution.py:380
  49.5 4.0 %weight_grad.1 = f32[3,768,1024]{2,1,0:T(8,128)} custom-call(bf16[2,48,768]{2,1,0:T(8,128)(2,1)S(1)} %get-tuple-element.28.refs_0_, bf16[2,48,768]{2,1,0:T(8,128)(2,1)S(1)} %get-tuple-element.29.refs_1_, bf16[3,48,1024]{2,1,0:T(8,128)(2,1)S(1)} %get-tuple-element.30.refs_2_, bf16[3,48,1024]{2,1,0:T(8,128)(2,1)S(1)} %get-tuple-element.31.refs_3_), custom_call_target="tpu_custom_call" | custom-call | tf_op jit(solution)/shard_map/weight_grad/pallas_call | solution.py:281
  53.5 4.3 %all-to-all-done.got_ref = bf16[32,2,1152]{2,1,0:T(2,128)(2,1)S(1)} async-done(((bf16[32,2,1152]{2,1,0:T(2,128)(2,1)}), bf16[32,2,1152]{2,1,0:T(2,128)(2,1)S(1)}, u32[]{:S(2)}, u32[]{:S(2)}) %all-to-all-start) | async-done | bytes 147488 | tf_op jit(solution)/shard_map/all_to_all | solution.py:380
  57.8 1.0 %place.1 = bf16[12,3072]{1,0:T(8,128)(2,1)} custom-call(f32[8,12]{1,0:T(8,128)S(1)} %get-tuple-element.17.hit_ref, bf16[32,2,1152]{2,1,0:T(2,128)(2,1)S(1)} %all-to-all-done.got_ref), custom_call_target="tpu_custom_call" | custom-call | tf_op jit(solution)/shard_map/place/pallas_call | solution.py:328
  (11 shorter events, 0.2 us)
Async XLA Ops:
  2.0 4.7 %collective-permute-start = (bf16[8,768]{1,0:T(8,128)(2,1)S(1)}, bf16[8,768]{1,0:T(8,128)(2,1)S(1)}, u32[]{:S(2)}, u32[]{:S(2)}) collective-permute-start(bf16[8,768]{1,0:T(8,128)(2,1)S(1)} %get-tuple-element.19), channel_id=1, source_target_pairs={{0,8},{8,0},{16,24},{24,16},{1,9},{9,1},{17,25},{25,17},{2,10},{10... | collective-permute-start | bytes 36872 | tf_op jit(solution)/shard_map/ppermute | solution.py:343
  5.0 3.7 %collective-permute-start.1 = (bf16[8,768]{1,0:T(8,128)(2,1)S(1)}, bf16[8,768]{1,0:T(8,128)(2,1)S(1)}, u32[]{:S(2)}, u32[]{:S(2)}) collective-permute-start(bf16[8,768]{1,0:T(8,128)(2,1)S(1)} %get-tuple-element.20), channel_id=1, source_target_pairs={{0,16},{8,24},{16,0},{24,8},{1,17},{9,25},{17,1},{25,9},{2,18},{10... | collective-permute-start | bytes 36872 | tf_op jit(solution)/shard_map/ppermute | solution.py:343
  6.5 4.6 %collective-permute-start.2 = (bf16[8,768]{1,0:T(8,128)(2,1)S(1)}, bf16[8,768]{1,0:T(8,128)(2,1)S(1)}, u32[]{:S(2)}, u32[]{:S(2)}) collective-permute-start(bf16[8,768]{1,0:T(8,128)(2,1)S(1)} %get-tuple-element.21), channel_id=1, source_target_pairs={{0,24},{8,16},{16,8},{24,0},{1,25},{9,17},{17,9},{25,1},{2,26},{10... | collective-permute-start | bytes 36872 | tf_op jit(solution)/shard_map/ppermute | solution.py:343
  11.1 6.9 %collective-permute-start.3 = (bf16[32,768]{1,0:T(8,128)(2,1)S(1)}, bf16[32,768]{1,0:T(8,128)(2,1)S(1)}, u32[]{:S(2)}, u32[]{:S(2)}) collective-permute-start(bf16[32,768]{1,0:T(8,128)(2,1)S(1)} %get-tuple-element.32), channel_id=1, source_target_pairs={{0,2},{1,3},{2,0},{3,1},{4,6},{5,7},{6,4},{7,5},{8,10},{9,11},{10,... | collective-permute-start | bytes 147464 | tf_op jit(solution)/shard_map/ppermute | solution.py:343
  15.2 8.1 %collective-permute-start.5 = (bf16[32,768]{1,0:T(8,128)(2,1)S(1)}, bf16[32,768]{1,0:T(8,128)(2,1)S(1)}, u32[]{:S(2)}, u32[]{:S(2)}) collective-permute-start(bf16[32,768]{1,0:T(8,128)(2,1)S(1)} %get-tuple-element.32), channel_id=1, source_target_pairs={{0,6},{1,7},{2,4},{3,5},{4,2},{5,3},{6,0},{7,1},{8,14},{9,15},{10,... | collective-permute-start | bytes 147464 | tf_op jit(solution)/shard_map/ppermute | solution.py:343
  17.8 5.5 %collective-permute-start.4 = (bf16[32,768]{1,0:T(8,128)(2,1)S(1)}, bf16[32,768]{1,0:T(8,128)(2,1)S(1)}, u32[]{:S(2)}, u32[]{:S(2)}) collective-permute-start(bf16[32,768]{1,0:T(8,128)(2,1)S(1)} %get-tuple-element.32), channel_id=1, source_target_pairs={{0,4},{1,5},{2,6},{3,7},{4,0},{5,1},{6,2},{7,3},{8,12},{9,13},{10,... | collective-permute-start | bytes 147464 | tf_op jit(solution)/shard_map/ppermute | solution.py:343
  24.4 5.2 %collective-permute-start.11 = (bf16[3,48,512]{2,1,0:T(8,128)(2,1)S(1)}, bf16[3,48,512]{2,1,0:T(8,128)(2,1)S(1)}, u32[]{:S(2)}, u32[]{:S(2)}) collective-permute-start(bf16[3,48,512]{2,1,0:T(8,128)(2,1)S(1)} %get-tuple-element.24), channel_id=1, source_target_pairs={{0,8},{8,0},{16,24},{24,16},{1,9},{9,1},{17,25},{25,17},{2,10},{10... | collective-permute-start | bytes 442376 | tf_op jit(solution)/shard_map/ppermute | solution.py:343
  25.0 5.2 %collective-permute-start.6 = (bf16[128,768]{1,0:T(8,128)(2,1)S(1)}, bf16[128,768]{1,0:T(8,128)(2,1)S(1)}, u32[]{:S(2)}, u32[]{:S(2)}) collective-permute-start(bf16[128,768]{1,0:T(8,128)(2,1)S(1)} %constant_dynamic-update-slice_fusion.4.m_ref), channel_id=1, source_target_pairs={{0,1},{1,0},{2,3},{3,2},{4,5},{5,4},{6,7},{7,6},{8,9},{9,8},{10,11... | collective-permute-start | bytes 589832 | tf_op jit(solution)/shard_map/ppermute | solution.py:343
  25.0 6.9 %collective-permute-start.13 = (bf16[3,48,512]{2,1,0:T(8,128)(2,1)S(1)}, bf16[3,48,512]{2,1,0:T(8,128)(2,1)S(1)}, u32[]{:S(2)}, u32[]{:S(2)}) collective-permute-start(bf16[3,48,512]{2,1,0:T(8,128)(2,1)S(1)} %get-tuple-element.25), channel_id=1, source_target_pairs={{0,16},{8,24},{16,0},{24,8},{1,17},{9,25},{17,1},{25,9},{2,18},{10... | collective-permute-start | bytes 442376 | tf_op jit(solution)/shard_map/ppermute | solution.py:343
  29.6 11.1 %collective-permute-start.12 = (bf16[3,48,512]{2,1,0:T(8,128)(2,1)S(1)}, bf16[3,48,512]{2,1,0:T(8,128)(2,1)S(1)}, u32[]{:S(2)}, u32[]{:S(2)}) collective-permute-start(bf16[3,48,512]{2,1,0:T(8,128)(2,1)S(1)} %add_convert_fusion.1.a_ref), channel_id=1, source_target_pairs={{0,16},{8,24},{16,0},{24,8},{1,17},{9,25},{17,1},{25,9},{2,18},{10... | collective-permute-start | bytes 442376 | tf_op jit(solution)/shard_map/ppermute | solution.py:343
  31.2 5.5 %collective-permute-start.7 = (bf16[3,48,512]{2,1,0:T(8,128)(2,1)S(1)}, bf16[3,48,512]{2,1,0:T(8,128)(2,1)S(1)}, u32[]{:S(2)}, u32[]{:S(2)}) collective-permute-start(bf16[3,48,512]{2,1,0:T(8,128)(2,1)S(1)} %get-tuple-element.22), channel_id=1, source_target_pairs={{0,8},{8,0},{16,24},{24,16},{1,9},{9,1},{17,25},{25,17},{2,10},{10... | collective-permute-start | bytes 442376 | tf_op jit(solution)/shard_map/ppermute | solution.py:343
  31.9 8.9 %collective-permute-start.14 = (bf16[3,48,512]{2,1,0:T(8,128)(2,1)S(1)}, bf16[3,48,512]{2,1,0:T(8,128)(2,1)S(1)}, u32[]{:S(2)}, u32[]{:S(2)}) collective-permute-start(bf16[3,48,512]{2,1,0:T(8,128)(2,1)S(1)} %add_convert_fusion.b_ref), channel_id=1, source_target_pairs={{0,8},{8,0},{16,24},{24,16},{1,9},{9,1},{17,25},{25,17},{2,10},{10... | collective-permute-start | bytes 442376 | tf_op jit(solution)/shard_map/ppermute | solution.py:343
  33.4 6.1 %collective-permute-start.9 = (bf16[3,48,512]{2,1,0:T(8,128)(2,1)S(1)}, bf16[3,48,512]{2,1,0:T(8,128)(2,1)S(1)}, u32[]{:S(2)}, u32[]{:S(2)}) collective-permute-start(bf16[3,48,512]{2,1,0:T(8,128)(2,1)S(1)} %get-tuple-element.23), channel_id=1, source_target_pairs={{0,16},{8,24},{16,0},{24,8},{1,17},{9,25},{17,1},{25,9},{2,18},{10... | collective-permute-start | bytes 442376 | tf_op jit(solution)/shard_map/ppermute | solution.py:343
  36.8 5.2 %collective-permute-start.8 = (bf16[3,48,512]{2,1,0:T(8,128)(2,1)S(1)}, bf16[3,48,512]{2,1,0:T(8,128)(2,1)S(1)}, u32[]{:S(2)}, u32[]{:S(2)}) collective-permute-start(bf16[3,48,512]{2,1,0:T(8,128)(2,1)S(1)} %add_convert_fusion.3.a_ref), channel_id=1, source_target_pairs={{0,16},{8,24},{16,0},{24,8},{1,17},{9,25},{17,1},{25,9},{2,18},{10... | collective-permute-start | bytes 442376 | tf_op jit(solution)/shard_map/ppermute | solution.py:343
  39.6 5.2 %collective-permute-start.10 = (bf16[3,48,512]{2,1,0:T(8,128)(2,1)S(1)}, bf16[3,48,512]{2,1,0:T(8,128)(2,1)S(1)}, u32[]{:S(2)}, u32[]{:S(2)}) collective-permute-start(bf16[3,48,512]{2,1,0:T(8,128)(2,1)S(1)} %add_convert_fusion.2.b_ref), channel_id=1, source_target_pairs={{0,8},{8,0},{16,24},{24,16},{1,9},{9,1},{17,25},{25,17},{2,10},{10... | collective-permute-start | bytes 442376 | tf_op jit(solution)/shard_map/ppermute | solution.py:343
  46.9 10.9 %all-to-all-start = ((bf16[32,2,1152]{2,1,0:T(2,128)(2,1)}), bf16[32,2,1152]{2,1,0:T(2,128)(2,1)S(1)}, u32[]{:S(2)}, u32[]{:S(2)}) async-start(bf16[32,2,1152]{2,1,0:T(2,128)(2,1)} %get-tuple-element.27), calls=%async_computation | async-start | bytes 294912 | tf_op jit(solution)/shard_map/all_to_all | solution.py:380

commit v6 on v5

--- a/solution.py
+++ b/solution.py
@@ -56,8 +56,8 @@
     copies = [pltpu.make_async_copy(u, v, sem.at[i]) for i, (u, v) in enumerate(pairs)]
     for copy in copies:
         copy.start()
-    for copy in copies:
-        copy.wait()
+    copies[0].wait()
+    copies[1].wait()
     n_dp = len(outs)
     width = outs[0].shape[1]
     tok = ids_ref.shape[1]
@@ -74,6 +74,8 @@
     hit_gr = jnp.where(hit_gr & (row >= CAP) & (row < 2 * CAP), 1.0, 0.0)
     slot_prob = jnp.sum(hit_gr * prob, axis=1, keepdims=True)
     hit_ref[...] = hit_in
+    copies[2].wait()
+    copies[3].wait()
     rows = nn(hit_in.astype(BF16), inp_ref[...]) + slot_prob * nn(hit_gr.astype(BF16), grad_ref[...])
     for d in range(n_dp):
         scratch[d] = rows[:, d * width : (d + 1) * width].astype(BF16)
@@ -294,7 +296,8 @@
     )(*operands)
 
 
-def place_kernel(hit_ref, got_ref, out_ref, *, n_dp):
+def place_kernel(hit_ref, got_ref, out_hbm, out_ref, sem, *, n_dp):
+    copies = []
     count, capp, lanes = got_ref.shape
     n_ex = count // n_dp
     part = lanes // CAP
@@ -321,15 +324,21 @@
                 out = moved if out is None else out + moved
             at = (2 * p + half) * part
             out_ref[:, at : at + part] = out.astype(BF16)
+        at = pl.ds(2 * p * part, 2 * part)
+        copies.append(pltpu.make_async_copy(out_ref.at[:, at], out_hbm.at[:, at], sem.at[p]))
+        copies[-1].start()
+    for copy in copies:
+        copy.wait()
 
 
 def place(hit, got, tok, n_dp):
     width = got.shape[2] // CAP * 2
     return pl.pallas_call(
         functools.partial(place_kernel, n_dp=n_dp),
-        out_shape=jax.ShapeDtypeStruct((tok, width * n_dp), BF16),
+        out_shape=pltpu.HBM((tok, width * n_dp), BF16),
         in_specs=[pl.BlockSpec(memory_space=VMEM)] * 2,
-        out_specs=pl.BlockSpec(memory_space=VMEM),
+        out_specs=pl.BlockSpec(memory_space=pltpu.HBM),
+        scratch_shapes=[pltpu.VMEM((tok, width * n_dp), BF16), pltpu.SemaphoreType.DMA((n_dp,))],
         compiler_params=pltpu.CompilerParams(vmem_limit_bytes=LIMIT),
         name="place",
     )(hit, got)

time: 59.1 us -> 58.9 us (level)
  no operation moved by 1% of the time
where the time goes in v6:
time: 58.9 us; the launch traced here: 58.7 us
  waiting for transfers between devices  24.6 us (42%)
  starting transfers between devices  19.2 us (33%)
  Pallas kernels  13.9 us (24%)
  between operations  0.74 us (1%)
    ppermute x15, waiting for transfers between devices, shift(): return lax.ppermute(x, axis, xor_pairs(lax.axis_size(axis), k))  20.3 us
    ppermute x15, starting transfers between devices, shift(): return lax.ppermute(x, axis, xor_pairs(lax.axis_size(axis), k))  16.6 us
    all_to_all x1, waiting for transfers between devices, fast_body(): lax.all_to_all(out[0], ('dp', 'expert'), split_axis=0, concat_axis=0, til...  4.35 us
    pallas_call x1, Pallas kernels, weight_grad(): pl.pallas_call(functools.partial(weight_grad_kernel, planes=planes, tile=...  4.01 us
    pallas_call x2, Pallas kernels, backward(): pl.pallas_call(functools.partial(backward_kernel, n_dp=n_dp), out_shape=[...  3.15 us
    all_to_all x1, starting transfers between devices, fast_body(): lax.all_to_all(out[0], ('dp', 'expert'), split_axis=0, concat_axis=0, til...  2.57 us
    pallas_call x1, Pallas kernels, scale_weights(): pl.pallas_call(scale_kernel, out_shape=pltpu.VMEM(w.shape, BF16), in_spec...  2.53 us
    pallas_call x2, Pallas kernels, forward(): pl.pallas_call(functools.partial(forward_kernel, n_dp=n_dp), out_shape=[p...  2.08 us
  transfers between devices with their start and end apart: 16, of which 10 were waited for; matrix products, arithmetic and copies ran while one was open for 0% of the time, Pallas kernels for 15%

profile of v6, /device:TPU:0, one launch (start us, length us, event | category | flops | bytes accessed | tf_op | source)
XLA Modules:
  0.0 58.7 jit_solution(11146500171270054173)
XLA Ops:
  0.6 1.2 %slots.1 = (f32[8,12]{1,0:T(8,128)S(1)}, bf16[8,768]{1,0:T(8,128)(2,1)S(1)}, bf16[8,768]{1,0:T(8,128)(2,1)S(1)}, bf16[8,768]{1,0:T(8,128)(2,1)S(1)}, bf16[8,768]{1,0:T(8,128)(2,1)S(1)}) custom-call(s32[1]{0:T(128)} %bitcast.p_ref, s32[1]{0:T(128)} %bitcast.1.e_ref, s32[2,12]{1,0:T(2,128)} %bitcast.4, f32[2,12]{1,0:T(2,128)} %bitcast.5, ...), custom_call_target="tpu_custom_call" | custom-call | tf_op jit(solution)/shard_map/slots/pallas_call | solution.py:90
  1.8 3.0 %collective-permute-start = (bf16[8,768]{1,0:T(8,128)(2,1)S(1)}, bf16[8,768]{1,0:T(8,128)(2,1)S(1)}, u32[]{:S(2)}, u32[]{:S(2)}) collective-permute-start(bf16[8,768]{1,0:T(8,128)(2,1)S(1)} %get-tuple-element.19), channel_id=1, source_target_pairs={{0,8},{8,0},{16,24},{24,16},{1,9},{9,1},{17,25},{25,17},{2,10},{10... | collective-permute-start | bytes 36872 | tf_op jit(solution)/shard_map/ppermute | solution.py:352
  4.9 1.5 %collective-permute-start.1 = (bf16[8,768]{1,0:T(8,128)(2,1)S(1)}, bf16[8,768]{1,0:T(8,128)(2,1)S(1)}, u32[]{:S(2)}, u32[]{:S(2)}) collective-permute-start(bf16[8,768]{1,0:T(8,128)(2,1)S(1)} %get-tuple-element.20), channel_id=1, source_target_pairs={{0,16},{8,24},{16,0},{24,8},{1,17},{9,25},{17,1},{25,9},{2,18},{10... | collective-permute-start | bytes 36872 | tf_op jit(solution)/shard_map/ppermute | solution.py:352
  6.4 0.0 collective-permute-start.2
  6.4 0.1 collective-permute-done
  6.6 2.0 %collective-permute-done.1 = bf16[8,768]{1,0:T(8,128)(2,1)S(1)} collective-permute-done((bf16[8,768]{1,0:T(8,128)(2,1)S(1)}, bf16[8,768]{1,0:T(8,128)(2,1)S(1)}, u32[]{:S(2)}, u32[]{:S(2)}) %collective-permute-start.1) | collective-permute-done | bytes 12320 | tf_op jit(solution)/shard_map/ppermute | solution.py:352
  8.6 2.4 %collective-permute-done.2 = bf16[8,768]{1,0:T(8,128)(2,1)S(1)} collective-permute-done((bf16[8,768]{1,0:T(8,128)(2,1)S(1)}, bf16[8,768]{1,0:T(8,128)(2,1)S(1)}, u32[]{:S(2)}, u32[]{:S(2)}) %collective-permute-start.2) | collective-permute-done | bytes 12320 | tf_op jit(solution)/shard_map/ppermute | solution.py:352
  11.0 1.6 %collective-permute-start.3 = (bf16[32,768]{1,0:T(8,128)(2,1)S(1)}, bf16[32,768]{1,0:T(8,128)(2,1)S(1)}, u32[]{:S(2)}, u32[]{:S(2)}) collective-permute-start(bf16[32,768]{1,0:T(8,128)(2,1)S(1)} %get-tuple-element.32), channel_id=1, source_target_pairs={{0,2},{1,3},{2,0},{3,1},{4,6},{5,7},{6,4},{7,5},{8,10},{9,11},{10,... | collective-permute-start | bytes 147464 | tf_op jit(solution)/shard_map/ppermute | solution.py:352
  12.6 2.5 %scale.1.w_ref = bf16[3,768,1024]{2,1,0:T(8,128)(2,1)S(1)} custom-call(s32[3,6,8]{2,1,0:T(8,128)} %exp_hbm.1, bf16[3,768,1024]{2,1,0:T(8,128)(2,1)} %w_ref.1), custom_call_target="tpu_custom_call" | custom-call | tf_op jit(solution)/shard_map/scale/pallas_call | solution.py:138
  15.1 2.5 %collective-permute-start.5 = (bf16[32,768]{1,0:T(8,128)(2,1)S(1)}, bf16[32,768]{1,0:T(8,128)(2,1)S(1)}, u32[]{:S(2)}, u32[]{:S(2)}) collective-permute-start(bf16[32,768]{1,0:T(8,128)(2,1)S(1)} %get-tuple-element.32), channel_id=1, source_target_pairs={{0,6},{1,7},{2,4},{3,5},{4,2},{5,3},{6,0},{7,1},{8,14},{9,15},{10,... | collective-permute-start | bytes 147464 | tf_op jit(solution)/shard_map/ppermute | solution.py:352
  17.7 0.2 collective-permute-start.4
  17.8 0.0 collective-permute-done.3
  17.9 5.3 %collective-permute-done.4 = bf16[32,768]{1,0:T(8,128)(2,1)S(1)} collective-permute-done((bf16[32,768]{1,0:T(8,128)(2,1)S(1)}, bf16[32,768]{1,0:T(8,128)(2,1)S(1)}, u32[]{:S(2)}, u32[]{:S(2)}) %collective-permute-start.4) | collective-permute-done | bytes 49184 | tf_op jit(solution)/shard_map/ppermute | solution.py:352
  23.2 0.0 collective-permute-done.5
  23.2 1.0 %forward.3 = (bf16[2,48,768]{2,1,0:T(8,128)(2,1)S(1)}, bf16[3,48,512]{2,1,0:T(8,128)(2,1)S(1)}, bf16[3,48,512]{2,1,0:T(8,128)(2,1)S(1)}) custom-call(s32[1]{0:T(128)} %bitcast.p_ref, bf16[128,768]{1,0:T(8,128)(2,1)S(1)} %constant_dynamic-update-slice_fusion.4.m_ref, bf16[3,768,1024]{2,1,0:T(8,128)(2,1)S(1)} %scale.1.w_ref), custom_call_target="tpu_custom_call" | custom-call | tf_op jit(solution)/shard_map/forward/pallas_call | solution.py:183
  24.2 0.6 %collective-permute-start.11 = (bf16[3,48,512]{2,1,0:T(8,128)(2,1)S(1)}, bf16[3,48,512]{2,1,0:T(8,128)(2,1)S(1)}, u32[]{:S(2)}, u32[]{:S(2)}) collective-permute-start(bf16[3,48,512]{2,1,0:T(8,128)(2,1)S(1)} %get-tuple-element.24), channel_id=1, source_target_pairs={{0,8},{8,0},{16,24},{24,16},{1,9},{9,1},{17,25},{25,17},{2,10},{10... | collective-permute-start | bytes 442376 | tf_op jit(solution)/shard_map/ppermute | solution.py:352
  24.8 0.0 collective-permute-start.6
  24.9 0.5 collective-permute-start.13
  25.4 4.1 %collective-permute-done.11 = bf16[3,48,512]{2,1,0:T(8,128)(2,1)S(1)} collective-permute-done((bf16[3,48,512]{2,1,0:T(8,128)(2,1)S(1)}, bf16[3,48,512]{2,1,0:T(8,128)(2,1)S(1)}, u32[]{:S(2)}, u32[]{:S(2)}) %collective-permute-start.11) | collective-permute-done | bytes 147488 | tf_op jit(solution)/shard_map/ppermute | solution.py:352
  29.5 0.6 collective-permute-start.12
  30.1 0.0 collective-permute-done.6.m_ref
  30.1 1.0 %forward.2 = (bf16[2,48,768]{2,1,0:T(8,128)(2,1)S(1)}, bf16[3,48,512]{2,1,0:T(8,128)(2,1)S(1)}, bf16[3,48,512]{2,1,0:T(8,128)(2,1)S(1)}) custom-call(s32[1]{0:T(128)} %bitcast.p_ref, bf16[128,768]{1,0:T(8,128)(2,1)S(1)} %collective-permute-done.6.m_ref, bf16[3,768,1024]{2,1,0:T(8,128)(2,1)S(1)} %scale.1.w_ref), custom_call_target="tpu_custom_call" | custom-call | tf_op jit(solution)/shard_map/forward/pallas_call | solution.py:183
  31.1 0.6 %collective-permute-start.7 = (bf16[3,48,512]{2,1,0:T(8,128)(2,1)S(1)}, bf16[3,48,512]{2,1,0:T(8,128)(2,1)S(1)}, u32[]{:S(2)}, u32[]{:S(2)}) collective-permute-start(bf16[3,48,512]{2,1,0:T(8,128)(2,1)S(1)} %get-tuple-element.22), channel_id=1, source_target_pairs={{0,8},{8,0},{16,24},{24,16},{1,9},{9,1},{17,25},{25,17},{2,10},{10... | collective-permute-start | bytes 442376 | tf_op jit(solution)/shard_map/ppermute | solution.py:352
  31.7 0.0 collective-permute-done.13
  31.8 1.6 %collective-permute-start.14 = (bf16[3,48,512]{2,1,0:T(8,128)(2,1)S(1)}, bf16[3,48,512]{2,1,0:T(8,128)(2,1)S(1)}, u32[]{:S(2)}, u32[]{:S(2)}) collective-permute-start(bf16[3,48,512]{2,1,0:T(8,128)(2,1)S(1)} %add_convert_fusion.b_ref), channel_id=1, source_target_pairs={{0,8},{8,0},{16,24},{24,16},{1,9},{9,1},{17,25},{25,17},{2,10},{10... | collective-permute-start | bytes 442376 | tf_op jit(solution)/shard_map/ppermute | solution.py:352
  33.3 1.5 %collective-permute-start.9 = (bf16[3,48,512]{2,1,0:T(8,128)(2,1)S(1)}, bf16[3,48,512]{2,1,0:T(8,128)(2,1)S(1)}, u32[]{:S(2)}, u32[]{:S(2)}) collective-permute-start(bf16[3,48,512]{2,1,0:T(8,128)(2,1)S(1)} %get-tuple-element.23), channel_id=1, source_target_pairs={{0,16},{8,24},{16,0},{24,8},{1,17},{9,25},{17,1},{25,9},{2,18},{10... | collective-permute-start | bytes 442376 | tf_op jit(solution)/shard_map/ppermute | solution.py:352
  34.8 1.8 %collective-permute-done.7 = bf16[3,48,512]{2,1,0:T(8,128)(2,1)S(1)} collective-permute-done((bf16[3,48,512]{2,1,0:T(8,128)(2,1)S(1)}, bf16[3,48,512]{2,1,0:T(8,128)(2,1)S(1)}, u32[]{:S(2)}, u32[]{:S(2)}) %collective-permute-start.7) | collective-permute-done | bytes 147488 | tf_op jit(solution)/shard_map/ppermute | solution.py:352
  36.7 1.3 %collective-permute-start.8 = (bf16[3,48,512]{2,1,0:T(8,128)(2,1)S(1)}, bf16[3,48,512]{2,1,0:T(8,128)(2,1)S(1)}, u32[]{:S(2)}, u32[]{:S(2)}) collective-permute-start(bf16[3,48,512]{2,1,0:T(8,128)(2,1)S(1)} %add_convert_fusion.3.a_ref), channel_id=1, source_target_pairs={{0,16},{8,24},{16,0},{24,8},{1,17},{9,25},{17,1},{25,9},{2,18},{10... | collective-permute-start | bytes 442376 | tf_op jit(solution)/shard_map/ppermute | solution.py:352
  37.9 1.5 %collective-permute-done.9 = bf16[3,48,512]{2,1,0:T(8,128)(2,1)S(1)} collective-permute-done((bf16[3,48,512]{2,1,0:T(8,128)(2,1)S(1)}, bf16[3,48,512]{2,1,0:T(8,128)(2,1)S(1)}, u32[]{:S(2)}, u32[]{:S(2)}) %collective-permute-start.9) | collective-permute-done | bytes 147488 | tf_op jit(solution)/shard_map/ppermute | solution.py:352
  39.5 1.1 %collective-permute-start.10 = (bf16[3,48,512]{2,1,0:T(8,128)(2,1)S(1)}, bf16[3,48,512]{2,1,0:T(8,128)(2,1)S(1)}, u32[]{:S(2)}, u32[]{:S(2)}) collective-permute-start(bf16[3,48,512]{2,1,0:T(8,128)(2,1)S(1)} %add_convert_fusion.2.b_ref), channel_id=1, source_target_pairs={{0,8},{8,0},{16,24},{24,16},{1,9},{9,1},{17,25},{25,17},{2,10},{10... | collective-permute-start | bytes 442376 | tf_op jit(solution)/shard_map/ppermute | solution.py:352
  40.6 0.0 collective-permute-done.12.ra_ref
  40.6 0.0 collective-permute-done.14.rb_ref
  40.6 1.1 %backward.2 = (bf16[3,48,1024]{2,1,0:T(8,128)(2,1)S(1)}, bf16[48,768]{1,0:T(8,128)(2,1)S(1)}) custom-call(s32[1]{0:T(128)} %bitcast.1.e_ref, bf16[3,48,512]{2,1,0:T(8,128)(2,1)S(1)} %add_convert_fusion.1.a_ref, bf16[3,48,512]{2,1,0:T(8,128)(2,1)S(1)} %collective-permute-done.12.ra_ref, bf16[3,48,512]{2,1,0:T(8,128)(2,1)S(1)} %add_convert_fusion.b_ref, ...), custom_call_target="tpu_custom_call" | custom-call | tf_op jit(solution)/shard_map/backward/pallas_call | solution.py:248
  41.7 0.2 collective-permute-done.8.ra_ref
  41.9 2.8 %collective-permute-done.10.rb_ref = bf16[3,48,512]{2,1,0:T(8,128)(2,1)S(1)} collective-permute-done((bf16[3,48,512]{2,1,0:T(8,128)(2,1)S(1)}, bf16[3,48,512]{2,1,0:T(8,128)(2,1)S(1)}, u32[]{:S(2)}, u32[]{:S(2)}) %collective-permute-start.10) | collective-permute-done | bytes 147488 | tf_op jit(solution)/shard_map/ppermute | solution.py:352
  44.7 2.1 %backward.3 = (bf16[3,48,1024]{2,1,0:T(8,128)(2,1)S(1)}, bf16[32,2,1152]{2,1,0:T(2,128)(2,1)}) custom-call(s32[1]{0:T(128)} %bitcast.1.e_ref, bf16[3,48,512]{2,1,0:T(8,128)(2,1)S(1)} %add_convert_fusion.3.a_ref, bf16[3,48,512]{2,1,0:T(8,128)(2,1)S(1)} %collective-permute-done.8.ra_ref, bf16[3,48,512]{2,1,0:T(8,128)(2,1)S(1)} %add_convert_fusion.2.b_ref, ...), custom_call_target="tpu_custom_call" | custom-call | tf_op jit(solution)/shard_map/backward/pallas_call | solution.py:248
  46.8 2.6 %all-to-all-start = ((bf16[32,2,1152]{2,1,0:T(2,128)(2,1)}), bf16[32,2,1152]{2,1,0:T(2,128)(2,1)S(1)}, u32[]{:S(2)}, u32[]{:S(2)}) async-start(bf16[32,2,1152]{2,1,0:T(2,128)(2,1)} %get-tuple-element.27), calls=%async_computation | async-start | bytes 294912 | tf_op jit(solution)/shard_map/all_to_all | solution.py:389
  49.4 4.0 %weight_grad.1 = f32[3,768,1024]{2,1,0:T(8,128)} custom-call(bf16[2,48,768]{2,1,0:T(8,128)(2,1)S(1)} %get-tuple-element.28.refs_0_, bf16[2,48,768]{2,1,0:T(8,128)(2,1)S(1)} %get-tuple-element.29.refs_1_, bf16[3,48,1024]{2,1,0:T(8,128)(2,1)S(1)} %get-tuple-element.30.refs_2_, bf16[3,48,1024]{2,1,0:T(8,128)(2,1)S(1)} %get-tuple-element.31.refs_3_), custom_call_target="tpu_custom_call" | custom-call | tf_op jit(solution)/shard_map/weight_grad/pallas_call | solution.py:283
  53.4 4.3 %all-to-all-done.got_ref = bf16[32,2,1152]{2,1,0:T(2,128)(2,1)S(1)} async-done(((bf16[32,2,1152]{2,1,0:T(2,128)(2,1)}), bf16[32,2,1152]{2,1,0:T(2,128)(2,1)S(1)}, u32[]{:S(2)}, u32[]{:S(2)}) %all-to-all-start) | async-done | bytes 147488 | tf_op jit(solution)/shard_map/all_to_all | solution.py:389
  57.7 1.0 %place.1 = bf16[12,3072]{1,0:T(8,128)(2,1)} custom-call(f32[8,12]{1,0:T(8,128)S(1)} %get-tuple-element.17.hit_ref, bf16[32,2,1152]{2,1,0:T(2,128)(2,1)S(1)} %all-to-all-done.got_ref), custom_call_target="tpu_custom_call" | custom-call | tf_op jit(solution)/shard_map/place/pallas_call | solution.py:336
  (11 shorter events, 0.2 us)
Async XLA Ops:
  1.8 4.7 %collective-permute-start = (bf16[8,768]{1,0:T(8,128)(2,1)S(1)}, bf16[8,768]{1,0:T(8,128)(2,1)S(1)}, u32[]{:S(2)}, u32[]{:S(2)}) collective-permute-start(bf16[8,768]{1,0:T(8,128)(2,1)S(1)} %get-tuple-element.19), channel_id=1, source_target_pairs={{0,8},{8,0},{16,24},{24,16},{1,9},{9,1},{17,25},{25,17},{2,10},{10... | collective-permute-start | bytes 36872 | tf_op jit(solution)/shard_map/ppermute | solution.py:352
  4.9 3.7 %collective-permute-start.1 = (bf16[8,768]{1,0:T(8,128)(2,1)S(1)}, bf16[8,768]{1,0:T(8,128)(2,1)S(1)}, u32[]{:S(2)}, u32[]{:S(2)}) collective-permute-start(bf16[8,768]{1,0:T(8,128)(2,1)S(1)} %get-tuple-element.20), channel_id=1, source_target_pairs={{0,16},{8,24},{16,0},{24,8},{1,17},{9,25},{17,1},{25,9},{2,18},{10... | collective-permute-start | bytes 36872 | tf_op jit(solution)/shard_map/ppermute | solution.py:352
  6.4 4.6 %collective-permute-start.2 = (bf16[8,768]{1,0:T(8,128)(2,1)S(1)}, bf16[8,768]{1,0:T(8,128)(2,1)S(1)}, u32[]{:S(2)}, u32[]{:S(2)}) collective-permute-start(bf16[8,768]{1,0:T(8,128)(2,1)S(1)} %get-tuple-element.21), channel_id=1, source_target_pairs={{0,24},{8,16},{16,8},{24,0},{1,25},{9,17},{17,9},{25,1},{2,26},{10... | collective-permute-start | bytes 36872 | tf_op jit(solution)/shard_map/ppermute | solution.py:352
  11.0 6.9 %collective-permute-start.3 = (bf16[32,768]{1,0:T(8,128)(2,1)S(1)}, bf16[32,768]{1,0:T(8,128)(2,1)S(1)}, u32[]{:S(2)}, u32[]{:S(2)}) collective-permute-start(bf16[32,768]{1,0:T(8,128)(2,1)S(1)} %get-tuple-element.32), channel_id=1, source_target_pairs={{0,2},{1,3},{2,0},{3,1},{4,6},{5,7},{6,4},{7,5},{8,10},{9,11},{10,... | collective-permute-start | bytes 147464 | tf_op jit(solution)/shard_map/ppermute | solution.py:352
  15.1 8.1 %collective-permute-start.5 = (bf16[32,768]{1,0:T(8,128)(2,1)S(1)}, bf16[32,768]{1,0:T(8,128)(2,1)S(1)}, u32[]{:S(2)}, u32[]{:S(2)}) collective-permute-start(bf16[32,768]{1,0:T(8,128)(2,1)S(1)} %get-tuple-element.32), channel_id=1, source_target_pairs={{0,6},{1,7},{2,4},{3,5},{4,2},{5,3},{6,0},{7,1},{8,14},{9,15},{10,... | collective-permute-start | bytes 147464 | tf_op jit(solution)/shard_map/ppermute | solution.py:352
  17.7 5.5 %collective-permute-start.4 = (bf16[32,768]{1,0:T(8,128)(2,1)S(1)}, bf16[32,768]{1,0:T(8,128)(2,1)S(1)}, u32[]{:S(2)}, u32[]{:S(2)}) collective-permute-start(bf16[32,768]{1,0:T(8,128)(2,1)S(1)} %get-tuple-element.32), channel_id=1, source_target_pairs={{0,4},{1,5},{2,6},{3,7},{4,0},{5,1},{6,2},{7,3},{8,12},{9,13},{10,... | collective-permute-start | bytes 147464 | tf_op jit(solution)/shard_map/ppermute | solution.py:352
  24.2 5.2 %collective-permute-start.11 = (bf16[3,48,512]{2,1,0:T(8,128)(2,1)S(1)}, bf16[3,48,512]{2,1,0:T(8,128)(2,1)S(1)}, u32[]{:S(2)}, u32[]{:S(2)}) collective-permute-start(bf16[3,48,512]{2,1,0:T(8,128)(2,1)S(1)} %get-tuple-element.24), channel_id=1, source_target_pairs={{0,8},{8,0},{16,24},{24,16},{1,9},{9,1},{17,25},{25,17},{2,10},{10... | collective-permute-start | bytes 442376 | tf_op jit(solution)/shard_map/ppermute | solution.py:352
  24.8 5.2 %collective-permute-start.6 = (bf16[128,768]{1,0:T(8,128)(2,1)S(1)}, bf16[128,768]{1,0:T(8,128)(2,1)S(1)}, u32[]{:S(2)}, u32[]{:S(2)}) collective-permute-start(bf16[128,768]{1,0:T(8,128)(2,1)S(1)} %constant_dynamic-update-slice_fusion.4.m_ref), channel_id=1, source_target_pairs={{0,1},{1,0},{2,3},{3,2},{4,5},{5,4},{6,7},{7,6},{8,9},{9,8},{10,11... | collective-permute-start | bytes 589832 | tf_op jit(solution)/shard_map/ppermute | solution.py:352
  24.9 6.9 %collective-permute-start.13 = (bf16[3,48,512]{2,1,0:T(8,128)(2,1)S(1)}, bf16[3,48,512]{2,1,0:T(8,128)(2,1)S(1)}, u32[]{:S(2)}, u32[]{:S(2)}) collective-permute-start(bf16[3,48,512]{2,1,0:T(8,128)(2,1)S(1)} %get-tuple-element.25), channel_id=1, source_target_pairs={{0,16},{8,24},{16,0},{24,8},{1,17},{9,25},{17,1},{25,9},{2,18},{10... | collective-permute-start | bytes 442376 | tf_op jit(solution)/shard_map/ppermute | solution.py:352
  29.5 11.1 %collective-permute-start.12 = (bf16[3,48,512]{2,1,0:T(8,128)(2,1)S(1)}, bf16[3,48,512]{2,1,0:T(8,128)(2,1)S(1)}, u32[]{:S(2)}, u32[]{:S(2)}) collective-permute-start(bf16[3,48,512]{2,1,0:T(8,128)(2,1)S(1)} %add_convert_fusion.1.a_ref), channel_id=1, source_target_pairs={{0,16},{8,24},{16,0},{24,8},{1,17},{9,25},{17,1},{25,9},{2,18},{10... | collective-permute-start | bytes 442376 | tf_op jit(solution)/shard_map/ppermute | solution.py:352
  31.1 5.5 %collective-permute-start.7 = (bf16[3,48,512]{2,1,0:T(8,128)(2,1)S(1)}, bf16[3,48,512]{2,1,0:T(8,128)(2,1)S(1)}, u32[]{:S(2)}, u32[]{:S(2)}) collective-permute-start(bf16[3,48,512]{2,1,0:T(8,128)(2,1)S(1)} %get-tuple-element.22), channel_id=1, source_target_pairs={{0,8},{8,0},{16,24},{24,16},{1,9},{9,1},{17,25},{25,17},{2,10},{10... | collective-permute-start | bytes 442376 | tf_op jit(solution)/shard_map/ppermute | solution.py:352
  31.8 8.8 %collective-permute-start.14 = (bf16[3,48,512]{2,1,0:T(8,128)(2,1)S(1)}, bf16[3,48,512]{2,1,0:T(8,128)(2,1)S(1)}, u32[]{:S(2)}, u32[]{:S(2)}) collective-permute-start(bf16[3,48,512]{2,1,0:T(8,128)(2,1)S(1)} %add_convert_fusion.b_ref), channel_id=1, source_target_pairs={{0,8},{8,0},{16,24},{24,16},{1,9},{9,1},{17,25},{25,17},{2,10},{10... | collective-permute-start | bytes 442376 | tf_op jit(solution)/shard_map/ppermute | solution.py:352
  33.3 6.1 %collective-permute-start.9 = (bf16[3,48,512]{2,1,0:T(8,128)(2,1)S(1)}, bf16[3,48,512]{2,1,0:T(8,128)(2,1)S(1)}, u32[]{:S(2)}, u32[]{:S(2)}) collective-permute-start(bf16[3,48,512]{2,1,0:T(8,128)(2,1)S(1)} %get-tuple-element.23), channel_id=1, source_target_pairs={{0,16},{8,24},{16,0},{24,8},{1,17},{9,25},{17,1},{25,9},{2,18},{10... | collective-permute-start | bytes 442376 | tf_op jit(solution)/shard_map/ppermute | solution.py:352
  36.7 5.2 %collective-permute-start.8 = (bf16[3,48,512]{2,1,0:T(8,128)(2,1)S(1)}, bf16[3,48,512]{2,1,0:T(8,128)(2,1)S(1)}, u32[]{:S(2)}, u32[]{:S(2)}) collective-permute-start(bf16[3,48,512]{2,1,0:T(8,128)(2,1)S(1)} %add_convert_fusion.3.a_ref), channel_id=1, source_target_pairs={{0,16},{8,24},{16,0},{24,8},{1,17},{9,25},{17,1},{25,9},{2,18},{10... | collective-permute-start | bytes 442376 | tf_op jit(solution)/shard_map/ppermute | solution.py:352
  39.5 5.2 %collective-permute-start.10 = (bf16[3,48,512]{2,1,0:T(8,128)(2,1)S(1)}, bf16[3,48,512]{2,1,0:T(8,128)(2,1)S(1)}, u32[]{:S(2)}, u32[]{:S(2)}) collective-permute-start(bf16[3,48,512]{2,1,0:T(8,128)(2,1)S(1)} %add_convert_fusion.2.b_ref), channel_id=1, source_target_pairs={{0,8},{8,0},{16,24},{24,16},{1,9},{9,1},{17,25},{25,17},{2,10},{10... | collective-permute-start | bytes 442376 | tf_op jit(solution)/shard_map/ppermute | solution.py:352
  46.8 10.9 %all-to-all-start = ((bf16[32,2,1152]{2,1,0:T(2,128)(2,1)}), bf16[32,2,1152]{2,1,0:T(2,128)(2,1)S(1)}, u32[]{:S(2)}, u32[]{:S(2)}) async-start(bf16[32,2,1152]{2,1,0:T(2,128)(2,1)} %get-tuple-element.27), calls=%async_computation | async-start | bytes 294912 | tf_op jit(solution)/shard_map/all_to_all | solution.py:389

commit v7 on v6

--- a/solution.py
+++ b/solution.py
@@ -352,6 +352,16 @@
     return lax.ppermute(x, axis, xor_pairs(lax.axis_size(axis), k))
 
 
+def pair_swap(x, phase):
+    n_dp, n_ex = lax.axis_size("dp"), lax.axis_size("expert")
+    pairs = []
+    for d in range(n_dp):
+        for ex in range(n_ex):
+            k = 1 + ((ex & 1) ^ phase)
+            pairs.append((d * n_ex + ex, (d ^ k) * n_ex + ex))
+    return lax.ppermute(x, ("dp", "expert"), pairs)
+
+
 def per_device_fast(out_grad, layer_input, expert_ids, gate_prob, w_stack, scale_exps):
     return fast_body(out_grad, layer_input, expert_ids, gate_prob, w_stack, scale_exps)
 
@@ -373,12 +383,12 @@
     xs, sums = [], []
     for m in (m0, m1):
         x, a, b = forward(p, m, w, n_dp, n_z)
-        ra = shift(a, "dp", 1)
-        rb = shift(b, "dp", 2)
+        ra = pair_swap(a, 0)
+        rb = pair_swap(b, 1)
         a = add_bf16(a, ra)
         b = add_bf16(b, rb)
-        ra = shift(a, "dp", 2)
-        rb = shift(b, "dp", 1)
+        ra = pair_swap(a, 1)
+        rb = pair_swap(b, 0)
         xs.append(x)
         sums.append((a, ra, b, rb))
     gs, out = [], ()

time: 58.9 us -> 61.2 us (1.039)
  waiting for transfers between devices: 24.6 us -> 27.5 us
    ppermute x0 -> x8, waiting for transfers between devices: none -> 13.2 us  [pair_swap(): return lax.ppermute(x, ('dp', 'expert'), pairs)]
    ppermute x15 -> x7, waiting for transfers between devices: 20.3 us -> 9.88 us  [shift(): return lax.ppermute(x, axis, xor_pairs(lax.axis_size(axis), k))]
    ppermute x15 -> x7, starting transfers between devices: 16.6 us -> 8.89 us  [shift(): return lax.ppermute(x, axis, xor_pairs(lax.axis_size(axis), k))]
    ppermute x0 -> x8, starting transfers between devices: none -> 6.97 us  [pair_swap(): return lax.ppermute(x, ('dp', 'expert'), pairs)]
  transfers between devices with their start and end apart: 16 -> 16, of which waited for: 10 -> 10; matrix products, arithmetic and copies ran while one was open for 0% -> 0% of each run, Pallas kernels for 15% -> 14%
where the time goes in v7:
time: 61.2 us; the launch traced here: 60.9 us
  waiting for transfers between devices  27.5 us (45%)
  starting transfers between devices  18.6 us (30%)
  Pallas kernels  13.9 us (23%)
  between operations  0.78 us (1%)
    ppermute x8, waiting for transfers between devices, pair_swap(): return lax.ppermute(x, ('dp', 'expert'), pairs)  13.2 us
    ppermute x7, waiting for transfers between devices, shift(): return lax.ppermute(x, axis, xor_pairs(lax.axis_size(axis), k))  9.88 us
    ppermute x7, starting transfers between devices, shift(): return lax.ppermute(x, axis, xor_pairs(lax.axis_size(axis), k))  8.89 us
    ppermute x8, starting transfers between devices, pair_swap(): return lax.ppermute(x, ('dp', 'expert'), pairs)  6.97 us
    all_to_all x1, waiting for transfers between devices, fast_body(): lax.all_to_all(out[0], ('dp', 'expert'), split_axis=0, concat_axis=0, til...  4.35 us
    pallas_call x1, Pallas kernels, weight_grad(): pl.pallas_call(functools.partial(weight_grad_kernel, planes=planes, tile=...  4.01 us
    pallas_call x2, Pallas kernels, backward(): pl.pallas_call(functools.partial(backward_kernel, n_dp=n_dp), out_shape=[...  3.16 us
    all_to_all x1, starting transfers between devices, fast_body(): lax.all_to_all(out[0], ('dp', 'expert'), split_axis=0, concat_axis=0, til...  2.72 us
  transfers between devices with their start and end apart: 16, of which 10 were waited for; matrix products, arithmetic and copies ran while one was open for 0% of the time, Pallas kernels for 14%

profile of v7, /device:TPU:0, one launch (start us, length us, event | category | flops | bytes accessed | tf_op | source)
XLA Modules:
  0.0 60.9 jit_solution(357018295809788648)
XLA Ops:
  0.6 1.2 %slots.1 = (f32[8,12]{1,0:T(8,128)S(1)}, bf16[8,768]{1,0:T(8,128)(2,1)S(1)}, bf16[8,768]{1,0:T(8,128)(2,1)S(1)}, bf16[8,768]{1,0:T(8,128)(2,1)S(1)}, bf16[8,768]{1,0:T(8,128)(2,1)S(1)}) custom-call(s32[1]{0:T(128)} %bitcast.p_ref, s32[1]{0:T(128)} %bitcast.1.e_ref, s32[2,12]{1,0:T(2,128)} %bitcast.4, f32[2,12]{1,0:T(2,128)} %bitcast.5, ...), custom_call_target="tpu_custom_call" | custom-call | tf_op jit(solution)/shard_map/slots/pallas_call | solution.py:90
  1.8 3.0 %collective-permute-start = (bf16[8,768]{1,0:T(8,128)(2,1)S(1)}, bf16[8,768]{1,0:T(8,128)(2,1)S(1)}, u32[]{:S(2)}, u32[]{:S(2)}) collective-permute-start(bf16[8,768]{1,0:T(8,128)(2,1)S(1)} %get-tuple-element.19), channel_id=1, source_target_pairs={{0,8},{8,0},{16,24},{24,16},{1,9},{9,1},{17,25},{25,17},{2,10},{10... | collective-permute-start | bytes 36872 | tf_op jit(solution)/shard_map/ppermute | solution.py:352
  4.9 1.5 %collective-permute-start.1 = (bf16[8,768]{1,0:T(8,128)(2,1)S(1)}, bf16[8,768]{1,0:T(8,128)(2,1)S(1)}, u32[]{:S(2)}, u32[]{:S(2)}) collective-permute-start(bf16[8,768]{1,0:T(8,128)(2,1)S(1)} %get-tuple-element.20), channel_id=1, source_target_pairs={{0,16},{8,24},{16,0},{24,8},{1,17},{9,25},{17,1},{25,9},{2,18},{10... | collective-permute-start | bytes 36872 | tf_op jit(solution)/shard_map/ppermute | solution.py:352
  6.4 0.0 collective-permute-start.2
  6.4 0.1 collective-permute-done
  6.6 2.0 %collective-permute-done.1 = bf16[8,768]{1,0:T(8,128)(2,1)S(1)} collective-permute-done((bf16[8,768]{1,0:T(8,128)(2,1)S(1)}, bf16[8,768]{1,0:T(8,128)(2,1)S(1)}, u32[]{:S(2)}, u32[]{:S(2)}) %collective-permute-start.1) | collective-permute-done | bytes 12320 | tf_op jit(solution)/shard_map/ppermute | solution.py:352
  8.6 2.4 %collective-permute-done.2 = bf16[8,768]{1,0:T(8,128)(2,1)S(1)} collective-permute-done((bf16[8,768]{1,0:T(8,128)(2,1)S(1)}, bf16[8,768]{1,0:T(8,128)(2,1)S(1)}, u32[]{:S(2)}, u32[]{:S(2)}) %collective-permute-start.2) | collective-permute-done | bytes 12320 | tf_op jit(solution)/shard_map/ppermute | solution.py:352
  11.0 1.6 %collective-permute-start.3 = (bf16[32,768]{1,0:T(8,128)(2,1)S(1)}, bf16[32,768]{1,0:T(8,128)(2,1)S(1)}, u32[]{:S(2)}, u32[]{:S(2)}) collective-permute-start(bf16[32,768]{1,0:T(8,128)(2,1)S(1)} %get-tuple-element.32), channel_id=1, source_target_pairs={{0,2},{1,3},{2,0},{3,1},{4,6},{5,7},{6,4},{7,5},{8,10},{9,11},{10,... | collective-permute-start | bytes 147464 | tf_op jit(solution)/shard_map/ppermute | solution.py:352
  12.6 2.5 %scale.1.w_ref = bf16[3,768,1024]{2,1,0:T(8,128)(2,1)S(1)} custom-call(s32[3,6,8]{2,1,0:T(8,128)} %exp_hbm.1, bf16[3,768,1024]{2,1,0:T(8,128)(2,1)} %w_ref.1), custom_call_target="tpu_custom_call" | custom-call | tf_op jit(solution)/shard_map/scale/pallas_call | solution.py:138
  15.1 2.5 %collective-permute-start.5 = (bf16[32,768]{1,0:T(8,128)(2,1)S(1)}, bf16[32,768]{1,0:T(8,128)(2,1)S(1)}, u32[]{:S(2)}, u32[]{:S(2)}) collective-permute-start(bf16[32,768]{1,0:T(8,128)(2,1)S(1)} %get-tuple-element.32), channel_id=1, source_target_pairs={{0,6},{1,7},{2,4},{3,5},{4,2},{5,3},{6,0},{7,1},{8,14},{9,15},{10,... | collective-permute-start | bytes 147464 | tf_op jit(solution)/shard_map/ppermute | solution.py:352
  17.7 0.2 collective-permute-start.4
  17.8 0.0 collective-permute-done.3
  17.9 5.3 %collective-permute-done.4 = bf16[32,768]{1,0:T(8,128)(2,1)S(1)} collective-permute-done((bf16[32,768]{1,0:T(8,128)(2,1)S(1)}, bf16[32,768]{1,0:T(8,128)(2,1)S(1)}, u32[]{:S(2)}, u32[]{:S(2)}) %collective-permute-start.4) | collective-permute-done | bytes 49184 | tf_op jit(solution)/shard_map/ppermute | solution.py:352
  23.2 0.0 collective-permute-done.5
  23.2 1.0 %forward.3 = (bf16[2,48,768]{2,1,0:T(8,128)(2,1)S(1)}, bf16[3,48,512]{2,1,0:T(8,128)(2,1)S(1)}, bf16[3,48,512]{2,1,0:T(8,128)(2,1)S(1)}) custom-call(s32[1]{0:T(128)} %bitcast.p_ref, bf16[128,768]{1,0:T(8,128)(2,1)S(1)} %constant_dynamic-update-slice_fusion.4.m_ref, bf16[3,768,1024]{2,1,0:T(8,128)(2,1)S(1)} %scale.1.w_ref), custom_call_target="tpu_custom_call" | custom-call | tf_op jit(solution)/shard_map/forward/pallas_call | solution.py:183
  24.2 0.6 collective-permute-start.11
  24.8 0.0 collective-permute-start.6
  24.9 0.5 collective-permute-start.13
  25.4 5.6 %collective-permute-done.11 = bf16[3,48,512]{2,1,0:T(8,128)(2,1)S(1)} collective-permute-done((bf16[3,48,512]{2,1,0:T(8,128)(2,1)S(1)}, bf16[3,48,512]{2,1,0:T(8,128)(2,1)S(1)}, u32[]{:S(2)}, u32[]{:S(2)}) %collective-permute-start.11) | collective-permute-done | bytes 147488 | tf_op jit(solution)/shard_map/ppermute | solution.py:362
  31.0 0.6 collective-permute-start.12
  31.6 0.0 collective-permute-done.6.m_ref
  31.6 1.0 %forward.2 = (bf16[2,48,768]{2,1,0:T(8,128)(2,1)S(1)}, bf16[3,48,512]{2,1,0:T(8,128)(2,1)S(1)}, bf16[3,48,512]{2,1,0:T(8,128)(2,1)S(1)}) custom-call(s32[1]{0:T(128)} %bitcast.p_ref, bf16[128,768]{1,0:T(8,128)(2,1)S(1)} %collective-permute-done.6.m_ref, bf16[3,768,1024]{2,1,0:T(8,128)(2,1)S(1)} %scale.1.w_ref), custom_call_target="tpu_custom_call" | custom-call | tf_op jit(solution)/shard_map/forward/pallas_call | solution.py:183
  32.6 0.1 collective-permute-start.7
  32.7 0.0 collective-permute-done.13
  32.8 2.1 %collective-permute-start.14 = (bf16[3,48,512]{2,1,0:T(8,128)(2,1)S(1)}, bf16[3,48,512]{2,1,0:T(8,128)(2,1)S(1)}, u32[]{:S(2)}, u32[]{:S(2)}) collective-permute-start(bf16[3,48,512]{2,1,0:T(8,128)(2,1)S(1)} %add_convert_fusion.b_ref), channel_id=1, source_target_pairs={{0,8},{1,17},{2,10},{3,19},{4,12},{5,21},{6,14},{7,23},{8,0},{9,25... | collective-permute-start | bytes 442376 | tf_op jit(solution)/shard_map/ppermute | solution.py:362
  34.8 1.5 %collective-permute-start.9 = (bf16[3,48,512]{2,1,0:T(8,128)(2,1)S(1)}, bf16[3,48,512]{2,1,0:T(8,128)(2,1)S(1)}, u32[]{:S(2)}, u32[]{:S(2)}) collective-permute-start(bf16[3,48,512]{2,1,0:T(8,128)(2,1)S(1)} %get-tuple-element.23), channel_id=1, source_target_pairs={{0,16},{1,9},{2,18},{3,11},{4,20},{5,13},{6,22},{7,15},{8,24},{9,1... | collective-permute-start | bytes 442376 | tf_op jit(solution)/shard_map/ppermute | solution.py:362
  36.3 2.4 %collective-permute-done.7 = bf16[3,48,512]{2,1,0:T(8,128)(2,1)S(1)} collective-permute-done((bf16[3,48,512]{2,1,0:T(8,128)(2,1)S(1)}, bf16[3,48,512]{2,1,0:T(8,128)(2,1)S(1)}, u32[]{:S(2)}, u32[]{:S(2)}) %collective-permute-start.7) | collective-permute-done | bytes 147488 | tf_op jit(solution)/shard_map/ppermute | solution.py:362
  38.8 1.6 %collective-permute-start.8 = (bf16[3,48,512]{2,1,0:T(8,128)(2,1)S(1)}, bf16[3,48,512]{2,1,0:T(8,128)(2,1)S(1)}, u32[]{:S(2)}, u32[]{:S(2)}) collective-permute-start(bf16[3,48,512]{2,1,0:T(8,128)(2,1)S(1)} %add_convert_fusion.3.a_ref), channel_id=1, source_target_pairs={{0,16},{1,9},{2,18},{3,11},{4,20},{5,13},{6,22},{7,15},{8,24},{9,1... | collective-permute-start | bytes 442376 | tf_op jit(solution)/shard_map/ppermute | solution.py:362
  40.4 1.2 %collective-permute-done.9 = bf16[3,48,512]{2,1,0:T(8,128)(2,1)S(1)} collective-permute-done((bf16[3,48,512]{2,1,0:T(8,128)(2,1)S(1)}, bf16[3,48,512]{2,1,0:T(8,128)(2,1)S(1)}, u32[]{:S(2)}, u32[]{:S(2)}) %collective-permute-start.9) | collective-permute-done | bytes 147488 | tf_op jit(solution)/shard_map/ppermute | solution.py:362
  41.6 0.1 collective-permute-start.10
  41.7 0.0 collective-permute-done.12.ra_ref
  41.7 0.0 collective-permute-done.14.rb_ref
  41.7 1.1 %backward.2 = (bf16[3,48,1024]{2,1,0:T(8,128)(2,1)S(1)}, bf16[48,768]{1,0:T(8,128)(2,1)S(1)}) custom-call(s32[1]{0:T(128)} %bitcast.1.e_ref, bf16[3,48,512]{2,1,0:T(8,128)(2,1)S(1)} %add_convert_fusion.1.a_ref, bf16[3,48,512]{2,1,0:T(8,128)(2,1)S(1)} %collective-permute-done.12.ra_ref, bf16[3,48,512]{2,1,0:T(8,128)(2,1)S(1)} %add_convert_fusion.b_ref, ...), custom_call_target="tpu_custom_call" | custom-call | tf_op jit(solution)/shard_map/backward/pallas_call | solution.py:248
  42.8 1.2 %collective-permute-done.8.ra_ref = bf16[3,48,512]{2,1,0:T(8,128)(2,1)S(1)} collective-permute-done((bf16[3,48,512]{2,1,0:T(8,128)(2,1)S(1)}, bf16[3,48,512]{2,1,0:T(8,128)(2,1)S(1)}, u32[]{:S(2)}, u32[]{:S(2)}) %collective-permute-start.8) | collective-permute-done | bytes 147488 | tf_op jit(solution)/shard_map/ppermute | solution.py:362
  44.0 2.8 %collective-permute-done.10.rb_ref = bf16[3,48,512]{2,1,0:T(8,128)(2,1)S(1)} collective-permute-done((bf16[3,48,512]{2,1,0:T(8,128)(2,1)S(1)}, bf16[3,48,512]{2,1,0:T(8,128)(2,1)S(1)}, u32[]{:S(2)}, u32[]{:S(2)}) %collective-permute-start.10) | collective-permute-done | bytes 147488 | tf_op jit(solution)/shard_map/ppermute | solution.py:362
  46.8 2.1 %backward.3 = (bf16[3,48,1024]{2,1,0:T(8,128)(2,1)S(1)}, bf16[32,2,1152]{2,1,0:T(2,128)(2,1)}) custom-call(s32[1]{0:T(128)} %bitcast.1.e_ref, bf16[3,48,512]{2,1,0:T(8,128)(2,1)S(1)} %add_convert_fusion.3.a_ref, bf16[3,48,512]{2,1,0:T(8,128)(2,1)S(1)} %collective-permute-done.8.ra_ref, bf16[3,48,512]{2,1,0:T(8,128)(2,1)S(1)} %add_convert_fusion.2.b_ref, ...), custom_call_target="tpu_custom_call" | custom-call | tf_op jit(solution)/shard_map/backward/pallas_call | solution.py:248
  48.9 2.7 %all-to-all-start = ((bf16[32,2,1152]{2,1,0:T(2,128)(2,1)}), bf16[32,2,1152]{2,1,0:T(2,128)(2,1)S(1)}, u32[]{:S(2)}, u32[]{:S(2)}) async-start(bf16[32,2,1152]{2,1,0:T(2,128)(2,1)} %get-tuple-element.27), calls=%async_computation | async-start | bytes 294912 | tf_op jit(solution)/shard_map/all_to_all | solution.py:399
  51.6 4.0 %weight_grad.1 = f32[3,768,1024]{2,1,0:T(8,128)} custom-call(bf16[2,48,768]{2,1,0:T(8,128)(2,1)S(1)} %get-tuple-element.28.refs_0_, bf16[2,48,768]{2,1,0:T(8,128)(2,1)S(1)} %get-tuple-element.29.refs_1_, bf16[3,48,1024]{2,1,0:T(8,128)(2,1)S(1)} %get-tuple-element.30.refs_2_, bf16[3,48,1024]{2,1,0:T(8,128)(2,1)S(1)} %get-tuple-element.31.refs_3_), custom_call_target="tpu_custom_call" | custom-call | tf_op jit(solution)/shard_map/weight_grad/pallas_call | solution.py:283
  55.6 4.3 %all-to-all-done.got_ref = bf16[32,2,1152]{2,1,0:T(2,128)(2,1)S(1)} async-done(((bf16[32,2,1152]{2,1,0:T(2,128)(2,1)}), bf16[32,2,1152]{2,1,0:T(2,128)(2,1)S(1)}, u32[]{:S(2)}, u32[]{:S(2)}) %all-to-all-start) | async-done | bytes 147488 | tf_op jit(solution)/shard_map/all_to_all | solution.py:399
  60.0 1.0 %place.1 = bf16[12,3072]{1,0:T(8,128)(2,1)} custom-call(f32[8,12]{1,0:T(8,128)S(1)} %get-tuple-element.17.hit_ref, bf16[32,2,1152]{2,1,0:T(2,128)(2,1)S(1)} %all-to-all-done.got_ref), custom_call_target="tpu_custom_call" | custom-call | tf_op jit(solution)/shard_map/place/pallas_call | solution.py:336
  (11 shorter events, 0.2 us)
Async XLA Ops:
  1.8 4.7 %collective-permute-start = (bf16[8,768]{1,0:T(8,128)(2,1)S(1)}, bf16[8,768]{1,0:T(8,128)(2,1)S(1)}, u32[]{:S(2)}, u32[]{:S(2)}) collective-permute-start(bf16[8,768]{1,0:T(8,128)(2,1)S(1)} %get-tuple-element.19), channel_id=1, source_target_pairs={{0,8},{8,0},{16,24},{24,16},{1,9},{9,1},{17,25},{25,17},{2,10},{10... | collective-permute-start | bytes 36872 | tf_op jit(solution)/shard_map/ppermute | solution.py:352
  4.9 3.7 %collective-permute-start.1 = (bf16[8,768]{1,0:T(8,128)(2,1)S(1)}, bf16[8,768]{1,0:T(8,128)(2,1)S(1)}, u32[]{:S(2)}, u32[]{:S(2)}) collective-permute-start(bf16[8,768]{1,0:T(8,128)(2,1)S(1)} %get-tuple-element.20), channel_id=1, source_target_pairs={{0,16},{8,24},{16,0},{24,8},{1,17},{9,25},{17,1},{25,9},{2,18},{10... | collective-permute-start | bytes 36872 | tf_op jit(solution)/shard_map/ppermute | solution.py:352
  6.4 4.6 %collective-permute-start.2 = (bf16[8,768]{1,0:T(8,128)(2,1)S(1)}, bf16[8,768]{1,0:T(8,128)(2,1)S(1)}, u32[]{:S(2)}, u32[]{:S(2)}) collective-permute-start(bf16[8,768]{1,0:T(8,128)(2,1)S(1)} %get-tuple-element.21), channel_id=1, source_target_pairs={{0,24},{8,16},{16,8},{24,0},{1,25},{9,17},{17,9},{25,1},{2,26},{10... | collective-permute-start | bytes 36872 | tf_op jit(solution)/shard_map/ppermute | solution.py:352
  11.0 6.9 %collective-permute-start.3 = (bf16[32,768]{1,0:T(8,128)(2,1)S(1)}, bf16[32,768]{1,0:T(8,128)(2,1)S(1)}, u32[]{:S(2)}, u32[]{:S(2)}) collective-permute-start(bf16[32,768]{1,0:T(8,128)(2,1)S(1)} %get-tuple-element.32), channel_id=1, source_target_pairs={{0,2},{1,3},{2,0},{3,1},{4,6},{5,7},{6,4},{7,5},{8,10},{9,11},{10,... | collective-permute-start | bytes 147464 | tf_op jit(solution)/shard_map/ppermute | solution.py:352
  15.1 8.1 %collective-permute-start.5 = (bf16[32,768]{1,0:T(8,128)(2,1)S(1)}, bf16[32,768]{1,0:T(8,128)(2,1)S(1)}, u32[]{:S(2)}, u32[]{:S(2)}) collective-permute-start(bf16[32,768]{1,0:T(8,128)(2,1)S(1)} %get-tuple-element.32), channel_id=1, source_target_pairs={{0,6},{1,7},{2,4},{3,5},{4,2},{5,3},{6,0},{7,1},{8,14},{9,15},{10,... | collective-permute-start | bytes 147464 | tf_op jit(solution)/shard_map/ppermute | solution.py:352
  17.7 5.5 %collective-permute-start.4 = (bf16[32,768]{1,0:T(8,128)(2,1)S(1)}, bf16[32,768]{1,0:T(8,128)(2,1)S(1)}, u32[]{:S(2)}, u32[]{:S(2)}) collective-permute-start(bf16[32,768]{1,0:T(8,128)(2,1)S(1)} %get-tuple-element.32), channel_id=1, source_target_pairs={{0,4},{1,5},{2,6},{3,7},{4,0},{5,1},{6,2},{7,3},{8,12},{9,13},{10,... | collective-permute-start | bytes 147464 | tf_op jit(solution)/shard_map/ppermute | solution.py:352
  24.2 6.7 %collective-permute-start.11 = (bf16[3,48,512]{2,1,0:T(8,128)(2,1)S(1)}, bf16[3,48,512]{2,1,0:T(8,128)(2,1)S(1)}, u32[]{:S(2)}, u32[]{:S(2)}) collective-permute-start(bf16[3,48,512]{2,1,0:T(8,128)(2,1)S(1)} %get-tuple-element.24), channel_id=1, source_target_pairs={{0,8},{1,17},{2,10},{3,19},{4,12},{5,21},{6,14},{7,23},{8,0},{9,25... | collective-permute-start | bytes 442376 | tf_op jit(solution)/shard_map/ppermute | solution.py:362
  24.8 6.7 %collective-permute-start.6 = (bf16[128,768]{1,0:T(8,128)(2,1)S(1)}, bf16[128,768]{1,0:T(8,128)(2,1)S(1)}, u32[]{:S(2)}, u32[]{:S(2)}) collective-permute-start(bf16[128,768]{1,0:T(8,128)(2,1)S(1)} %constant_dynamic-update-slice_fusion.4.m_ref), channel_id=1, source_target_pairs={{0,1},{1,0},{2,3},{3,2},{4,5},{5,4},{6,7},{7,6},{8,9},{9,8},{10,11... | collective-permute-start | bytes 589832 | tf_op jit(solution)/shard_map/ppermute | solution.py:352
  24.9 7.9 %collective-permute-start.13 = (bf16[3,48,512]{2,1,0:T(8,128)(2,1)S(1)}, bf16[3,48,512]{2,1,0:T(8,128)(2,1)S(1)}, u32[]{:S(2)}, u32[]{:S(2)}) collective-permute-start(bf16[3,48,512]{2,1,0:T(8,128)(2,1)S(1)} %get-tuple-element.25), channel_id=1, source_target_pairs={{0,16},{1,9},{2,18},{3,11},{4,20},{5,13},{6,22},{7,15},{8,24},{9,1... | collective-permute-start | bytes 442376 | tf_op jit(solution)/shard_map/ppermute | solution.py:362
  31.0 10.7 %collective-permute-start.12 = (bf16[3,48,512]{2,1,0:T(8,128)(2,1)S(1)}, bf16[3,48,512]{2,1,0:T(8,128)(2,1)S(1)}, u32[]{:S(2)}, u32[]{:S(2)}) collective-permute-start(bf16[3,48,512]{2,1,0:T(8,128)(2,1)S(1)} %add_convert_fusion.1.a_ref), channel_id=1, source_target_pairs={{0,16},{1,9},{2,18},{3,11},{4,20},{5,13},{6,22},{7,15},{8,24},{9,1... | collective-permute-start | bytes 442376 | tf_op jit(solution)/shard_map/ppermute | solution.py:362
  32.6 6.1 %collective-permute-start.7 = (bf16[3,48,512]{2,1,0:T(8,128)(2,1)S(1)}, bf16[3,48,512]{2,1,0:T(8,128)(2,1)S(1)}, u32[]{:S(2)}, u32[]{:S(2)}) collective-permute-start(bf16[3,48,512]{2,1,0:T(8,128)(2,1)S(1)} %get-tuple-element.22), channel_id=1, source_target_pairs={{0,8},{1,17},{2,10},{3,19},{4,12},{5,21},{6,14},{7,23},{8,0},{9,25... | collective-permute-start | bytes 442376 | tf_op jit(solution)/shard_map/ppermute | solution.py:362
  32.8 8.9 %collective-permute-start.14 = (bf16[3,48,512]{2,1,0:T(8,128)(2,1)S(1)}, bf16[3,48,512]{2,1,0:T(8,128)(2,1)S(1)}, u32[]{:S(2)}, u32[]{:S(2)}) collective-permute-start(bf16[3,48,512]{2,1,0:T(8,128)(2,1)S(1)} %add_convert_fusion.b_ref), channel_id=1, source_target_pairs={{0,8},{1,17},{2,10},{3,19},{4,12},{5,21},{6,14},{7,23},{8,0},{9,25... | collective-permute-start | bytes 442376 | tf_op jit(solution)/shard_map/ppermute | solution.py:362
  34.8 6.7 %collective-permute-start.9 = (bf16[3,48,512]{2,1,0:T(8,128)(2,1)S(1)}, bf16[3,48,512]{2,1,0:T(8,128)(2,1)S(1)}, u32[]{:S(2)}, u32[]{:S(2)}) collective-permute-start(bf16[3,48,512]{2,1,0:T(8,128)(2,1)S(1)} %get-tuple-element.23), channel_id=1, source_target_pairs={{0,16},{1,9},{2,18},{3,11},{4,20},{5,13},{6,22},{7,15},{8,24},{9,1... | collective-permute-start | bytes 442376 | tf_op jit(solution)/shard_map/ppermute | solution.py:362
  38.8 5.2 %collective-permute-start.8 = (bf16[3,48,512]{2,1,0:T(8,128)(2,1)S(1)}, bf16[3,48,512]{2,1,0:T(8,128)(2,1)S(1)}, u32[]{:S(2)}, u32[]{:S(2)}) collective-permute-start(bf16[3,48,512]{2,1,0:T(8,128)(2,1)S(1)} %add_convert_fusion.3.a_ref), channel_id=1, source_target_pairs={{0,16},{1,9},{2,18},{3,11},{4,20},{5,13},{6,22},{7,15},{8,24},{9,1... | collective-permute-start | bytes 442376 | tf_op jit(solution)/shard_map/ppermute | solution.py:362
  41.6 5.2 %collective-permute-start.10 = (bf16[3,48,512]{2,1,0:T(8,128)(2,1)S(1)}, bf16[3,48,512]{2,1,0:T(8,128)(2,1)S(1)}, u32[]{:S(2)}, u32[]{:S(2)}) collective-permute-start(bf16[3,48,512]{2,1,0:T(8,128)(2,1)S(1)} %add_convert_fusion.2.b_ref), channel_id=1, source_target_pairs={{0,8},{1,17},{2,10},{3,19},{4,12},{5,21},{6,14},{7,23},{8,0},{9,25... | collective-permute-start | bytes 442376 | tf_op jit(solution)/shard_map/ppermute | solution.py:362
  48.9 11.1 %all-to-all-start = ((bf16[32,2,1152]{2,1,0:T(2,128)(2,1)}), bf16[32,2,1152]{2,1,0:T(2,128)(2,1)S(1)}, u32[]{:S(2)}, u32[]{:S(2)}) async-start(bf16[32,2,1152]{2,1,0:T(2,128)(2,1)} %get-tuple-element.27), calls=%async_computation | async-start | bytes 294912 | tf_op jit(solution)/shard_map/all_to_all | solution.py:399
